TPU v7x, 32 devices: a whole 2x2x4 slice. The times are simulated.
32 devices in a mesh: ctx: 8 (over z, y), tp: 4 (over x, core).
Axes of the slice: x: 2, y: 2, z: 4, core: 2. Of those that a mesh axis runs over, the one named last changes fastest.
Arguments:
- stream_in: float32 [3072, 2048], P('ctx'), may hold values from -6 to 6
- cotangent: float32 [3072, 2048], P('ctx'), may hold values from -6 to 6
- ln_gain: float32 [2, 2048], replicated, may hold values from 0.5 to 1.5
- ln_bias: float32 [2, 2048], replicated, may hold values from -3 to 3
- w_qkv: bfloat16 [2048, 6144], P(None, 'tp'), may hold values from -0.46403883 to 0.46403883
- b_qkv: float32 [6144], P('tp'), may hold values from -1 to 1
- w_out: bfloat16 [2048, 2048], P('tp'), may hold values from -0.5 to 0.5
- out_bias: float32 [2048], replicated, may hold values from -3 to 3
- w_up: bfloat16 [2048, 8192], P(None, 'tp'), may hold values from -0.125 to 0.125
- b_up: float32 [8192], P('tp'), may hold values from -3 to 3
- w_down: bfloat16 [8192, 2048], P('tp'), may hold values from -0.0625 to 0.0625
- block_order: int32 [16], replicated, may hold values from 0 to 15, as said below
Outputs:
- stream_out: float32 [3072, 2048], P('ctx')
- grad_in: float32 [3072, 2048], P('ctx')
- grad_w_qkv: float32 [2048, 6144], P('ctx', 'tp')
- grad_b_qkv: float32 [6144], P('tp')
- grad_w_out: float32 [2048, 2048], P('tp', 'ctx')
- grad_out_bias: float32 [2048], replicated
- grad_w_up: float32 [2048, 8192], P('ctx', 'tp')
- grad_b_up: float32 [8192], P('tp')
- grad_w_down: float32 [8192, 2048], P('tp', 'ctx')
- grad_ln_gain: float32 [2, 2048], replicated
- grad_ln_bias: float32 [2, 2048], replicated
Inputs may be any that keep to these rules, and one draw needn't show every extreme that they name: `block_order`: entries 2 d and 2 d + 1 are b and 15 - b for some b; each value appears once.
All inputs are finite; a program needn't handle non-finite values.
Results may differ from a plain program's by a relative error of at most 0.04.
Values may be sent and summed in bfloat16 or wider, within the bound.
A program may use at most 384 MiB of HBM per device.

v0:
```python
import math

import jax
import jax.numpy as jnp
from jax import lax
from jax.sharding import PartitionSpec as P

HD = 256
ROT = 64


masked_value = -1e30
norm_epsilon = 1e-05
root_half = 0.7071067811865476
inverse_root_two_pi = 0.3989422804014327


def stored_positions(block_order, first_row, row_count, block_rows):
    row_index = first_row + jnp.arange(row_count, dtype=jnp.int32)
    owner_block = row_index // block_rows
    block_ids = jnp.arange(block_order.shape[0], dtype=jnp.int32)
    picked = jnp.sum(
        jnp.where(owner_block[:, None] == block_ids[None, :], block_order[None, :], 0), axis=1
    )
    return picked * block_rows + row_index % block_rows


def rope_tables(positions, rotary_dims):
    half_rot = rotary_dims // 2
    frequency = jnp.exp(
        jnp.arange(half_rot, dtype=jnp.float32) * (-2.0 * math.log(10000.0) / rotary_dims)
    )
    angles = positions.astype(jnp.float32)[:, None] * frequency[None, :]
    angles = jnp.concatenate([angles, angles], axis=1)
    return (jnp.cos(angles), jnp.sin(angles))


def rotate(tensor, cosine, sine_table, rotary_dims):
    half_rot = rotary_dims // 2
    rotary_part = tensor[..., :rotary_dims]
    turned = jnp.concatenate([-rotary_part[..., half_rot:], rotary_part[..., :half_rot]], axis=-1)
    moved = rotary_part * cosine[:, None, :] + turned * sine_table[:, None, :]
    return jnp.concatenate([moved, tensor[..., rotary_dims:]], axis=-1)


def unrotate(incoming, cosine, sine_table, rotary_dims):
    half_rot = rotary_dims // 2
    rotary_part = incoming[..., :rotary_dims]
    scaled = rotary_part * sine_table[:, None, :]
    swapped = jnp.concatenate([scaled[..., half_rot:], -scaled[..., :half_rot]], axis=-1)
    moved = rotary_part * cosine[:, None, :] + swapped
    return jnp.concatenate([moved, incoming[..., rotary_dims:]], axis=-1)


def normalize(tensor, gain_row, shift_row):
    row_mean = jnp.mean(tensor, axis=-1, keepdims=True)
    centred = tensor - row_mean
    variance = jnp.mean(centred * centred, axis=-1, keepdims=True)
    inv_scale = lax.rsqrt(variance + norm_epsilon)
    unit_field = centred * inv_scale
    return (unit_field * gain_row + shift_row, unit_field, inv_scale)


def normalize_back(incoming, unit_field, inv_scale, gain_row):
    unit_grad = incoming * gain_row
    return inv_scale * (
        unit_grad
        - jnp.mean(unit_grad, axis=-1, keepdims=True)
        - unit_field * jnp.mean(unit_grad * unit_field, axis=-1, keepdims=True)
    )


def gelu_exact(argument):
    return 0.5 * argument * (1.0 + jax.scipy.special.erf(argument * root_half))


def gelu_slope(argument):
    return (
        0.5 * (1.0 + jax.scipy.special.erf(argument * root_half))
        + argument * jnp.exp(-0.5 * argument * argument) * inverse_root_two_pi
    )


def shards(
    stream_in,
    cotangent,
    ln_gain,
    ln_bias,
    w_qkv,
    b_qkv,
    w_out,
    out_bias,
    w_up,
    b_up,
    w_down,
    block_order,
):
    row_count = stream_in.shape[0]
    block_rows = row_count // 2
    head_count = w_out.shape[0] // HD
    inner_width = head_count * HD
    score_scale = HD ** (-0.5)
    own_start = lax.axis_index("ctx") * row_count
    positions = stored_positions(block_order, own_start, row_count, block_rows)
    cosine, sine_table = rope_tables(positions, ROT)
    normed_a, unit_a, scale_a = normalize(stream_in, ln_gain[0], ln_bias[0])
    normed_m, unit_m, scale_m = normalize(stream_in, ln_gain[1], ln_bias[1])
    attn_in = normed_a.astype(jnp.bfloat16)
    mlp_in = normed_m.astype(jnp.bfloat16)
    joined = (jnp.dot(attn_in, w_qkv, preferred_element_type=jnp.float32) + b_qkv).reshape(
        row_count, head_count, 3, HD
    )
    query_b = rotate(joined[:, :, 0], cosine, sine_table, ROT).astype(jnp.bfloat16)
    key_b = (
        rotate(joined[:, :, 1], cosine, sine_table, ROT)
        .astype(jnp.bfloat16)
        .reshape(row_count, inner_width)
    )
    value_b = joined[:, :, 2].astype(jnp.bfloat16).reshape(row_count, inner_width)
    running_max = jnp.full((head_count, row_count), masked_value, jnp.float32)
    accum = jnp.zeros((row_count, head_count, HD), jnp.float32)
    key_piece = lax.all_gather(key_b, "ctx", axis=0, tiled=True)
    value_piece = lax.all_gather(value_b, "ctx", axis=0, tiled=True)
    count_here = key_piece.shape[0]
    key_pos = stored_positions(block_order, jnp.int32(0), count_here, block_rows)
    key_heads = key_piece.reshape(count_here, head_count, HD)
    value_heads = value_piece.reshape(count_here, head_count, HD)
    scores = (
        jnp.einsum("qhd,khd->hqk", query_b, key_heads, preferred_element_type=jnp.float32)
        * score_scale
    )
    allowed = (key_pos[None, :] <= positions[:, None])[None]
    new_max = jnp.maximum(running_max, jnp.max(jnp.where(allowed, scores, masked_value), axis=2))
    weights = jnp.exp(jnp.where(allowed, scores - new_max[:, :, None], masked_value))
    rescale = jnp.exp(running_max - new_max)
    running_sum = jnp.sum(weights, axis=2)
    accum = accum * rescale.T[:, :, None] + jnp.einsum(
        "hqk,khd->qhd",
        weights.astype(jnp.bfloat16),
        value_heads,
        preferred_element_type=jnp.float32,
    )
    running_max, running_sum, accum = (new_max, running_sum, accum)
    log_total = running_max + jnp.log(running_sum)
    attn_out = (
        (accum / running_sum.T[:, :, None]).astype(jnp.bfloat16).reshape(row_count, inner_width)
    )
    hidden = jnp.dot(mlp_in, w_up, preferred_element_type=jnp.float32) + b_up
    gelu_out = gelu_exact(hidden).astype(jnp.bfloat16)
    branch_part = jnp.dot(attn_out, w_out, preferred_element_type=jnp.float32) + jnp.dot(
        gelu_out, w_down, preferred_element_type=jnp.float32
    )
    stream_out = (
        stream_in + out_bias + lax.psum(branch_part.astype(jnp.bfloat16), "tp").astype(jnp.float32)
    )
    cot_b = cotangent.astype(jnp.bfloat16)
    grad_down = jnp.einsum("rf,rd->fd", gelu_out, cot_b, preferred_element_type=jnp.float32)
    grad_out = jnp.einsum("re,rd->ed", attn_out, cot_b, preferred_element_type=jnp.float32)
    hidden_grad = jnp.einsum(
        "rd,fd->rf", cot_b, w_down, preferred_element_type=jnp.float32
    ) * gelu_slope(hidden)
    grad_bup = jnp.sum(hidden_grad, axis=0)
    hidden_b = hidden_grad.astype(jnp.bfloat16)
    grad_up = jnp.einsum("rd,rf->df", mlp_in, hidden_b, preferred_element_type=jnp.float32)
    mlp_back = jnp.einsum("rf,df->rd", hidden_b, w_up, preferred_element_type=jnp.float32)
    out_grad = jnp.einsum("rd,ed->re", cot_b, w_out, preferred_element_type=jnp.float32).astype(
        jnp.bfloat16
    )
    out_grad_heads = out_grad.reshape(row_count, head_count, HD)
    row_dot = jnp.sum(
        out_grad_heads.astype(jnp.float32)
        * attn_out.reshape(row_count, head_count, HD).astype(jnp.float32),
        axis=2,
    ).T

    def pair_terms(
        queries, query_pos, query_total, query_dot, query_grad, key_heads, key_pos, value_heads
    ):
        scores = (
            jnp.einsum("qhd,khd->hqk", queries, key_heads, preferred_element_type=jnp.float32)
            * score_scale
        )
        allowed = (key_pos[None, :] <= query_pos[:, None])[None]
        probability = jnp.exp(jnp.where(allowed, scores - query_total[:, :, None], masked_value))
        prob_grad = jnp.einsum(
            "qhd,khd->hqk", query_grad, value_heads, preferred_element_type=jnp.float32
        )
        score_grad = (probability * (prob_grad - query_dot[:, :, None]) * score_scale).astype(
            jnp.bfloat16
        )
        return (probability.astype(jnp.bfloat16), score_grad)

    key_piece = lax.all_gather(key_b, "ctx", axis=0, tiled=True)
    value_piece = lax.all_gather(value_b, "ctx", axis=0, tiled=True)
    count_here = key_piece.shape[0]
    key_pos = stored_positions(block_order, jnp.int32(0), count_here, block_rows)
    key_heads = key_piece.reshape(count_here, head_count, HD)
    value_heads = value_piece.reshape(count_here, head_count, HD)
    prob_b, score_b = pair_terms(
        query_b, positions, log_total, row_dot, out_grad_heads, key_heads, key_pos, value_heads
    )
    query_acc = jnp.einsum("hqk,khd->qhd", score_b, key_heads, preferred_element_type=jnp.float32)
    query_grad = query_acc
    total_all, dot_all = (
        lax.all_gather(log_total.T, "ctx", axis=0, tiled=True),
        lax.all_gather(row_dot.T, "ctx", axis=0, tiled=True),
    )
    own_keys = key_b.reshape(row_count, head_count, HD)
    own_values = value_b.reshape(row_count, head_count, HD)
    query_piece = lax.all_gather(query_b.reshape(row_count, inner_width), "ctx", axis=0, tiled=True)
    grad_piece = lax.all_gather(out_grad, "ctx", axis=0, tiled=True)
    count_here = query_piece.shape[0]
    query_pos = stored_positions(block_order, jnp.int32(0), count_here, block_rows)
    query_heads = query_piece.reshape(count_here, head_count, HD)
    grad_heads = grad_piece.reshape(count_here, head_count, HD)
    piece_total = total_all.T
    piece_dot = dot_all.T
    prob_b, score_b = pair_terms(
        query_heads, query_pos, piece_total, piece_dot, grad_heads, own_keys, positions, own_values
    )
    key_acc = jnp.einsum("hqk,qhd->khd", score_b, query_heads, preferred_element_type=jnp.float32)
    value_acc = jnp.einsum("hqk,qhd->khd", prob_b, grad_heads, preferred_element_type=jnp.float32)
    joined_grad = jnp.stack(
        [
            unrotate(query_grad, cosine, sine_table, ROT),
            unrotate(key_acc, cosine, sine_table, ROT),
            value_acc,
        ],
        axis=2,
    ).reshape(row_count, 3 * inner_width)
    grad_bqkv = jnp.sum(joined_grad, axis=0)
    joined_b = joined_grad.astype(jnp.bfloat16)
    grad_qkv = jnp.einsum("rd,re->de", attn_in, joined_b, preferred_element_type=jnp.float32)
    attn_back = jnp.einsum("re,de->rd", joined_b, w_qkv, preferred_element_type=jnp.float32)
    attn_total, mlp_total = (
        lax.psum(attn_back.astype(jnp.bfloat16), "tp").astype(jnp.float32),
        lax.psum(mlp_back.astype(jnp.bfloat16), "tp").astype(jnp.float32),
    )
    grad_in = (
        cotangent
        + normalize_back(attn_total, unit_a, scale_a, ln_gain[0])
        + normalize_back(mlp_total, unit_m, scale_m, ln_gain[1])
    )
    gain_grad = jnp.stack(
        [jnp.sum(attn_total * unit_a, axis=0), jnp.sum(mlp_total * unit_m, axis=0)]
    )
    shift_grad = jnp.stack([jnp.sum(attn_total, axis=0), jnp.sum(mlp_total, axis=0)])
    summed_qkv, summed_up = (
        lax.psum_scatter(
            grad_qkv.astype(jnp.bfloat16), "ctx", scatter_dimension=0, tiled=True
        ).astype(jnp.float32),
        lax.psum_scatter(
            grad_up.astype(jnp.bfloat16), "ctx", scatter_dimension=0, tiled=True
        ).astype(jnp.float32),
    )
    summed_out, summed_down = (
        lax.psum_scatter(
            grad_out.astype(jnp.bfloat16), "ctx", scatter_dimension=1, tiled=True
        ).astype(jnp.float32),
        lax.psum_scatter(
            grad_down.astype(jnp.bfloat16), "ctx", scatter_dimension=1, tiled=True
        ).astype(jnp.float32),
    )
    summed_small = (
        lax.psum(grad_bqkv.astype(jnp.bfloat16), "ctx").astype(jnp.float32),
        lax.psum(grad_bup.astype(jnp.bfloat16), "ctx").astype(jnp.float32),
        lax.psum(jnp.sum(cotangent, axis=0).astype(jnp.bfloat16), "ctx").astype(jnp.float32),
        lax.psum(gain_grad.astype(jnp.bfloat16), "ctx").astype(jnp.float32),
        lax.psum(shift_grad.astype(jnp.bfloat16), "ctx").astype(jnp.float32),
    )
    return (
        stream_out,
        grad_in,
        summed_qkv,
        summed_small[0],
        summed_out,
        summed_small[2],
        summed_up,
        summed_small[1],
        summed_down,
        summed_small[3],
        summed_small[4],
    )


def solution(mesh):
    placed = (
        P("ctx", None),
        P("ctx", None),
        P(),
        P(),
        P(None, "tp"),
        P("tp"),
        P("tp", None),
        P(),
        P(None, "tp"),
        P("tp"),
        P("tp", None),
        P(),
    )
    return jax.shard_map(
        shards,
        mesh=mesh,
        in_specs=placed,
        out_specs=(
            P("ctx", None),
            P("ctx", None),
            P("ctx", "tp"),
            P("tp"),
            P("tp", "ctx"),
            P(),
            P("ctx", "tp"),
            P("tp"),
            P("tp", "ctx"),
            P(),
            P(),
        ),
        check_vma=False,
    )
```

profile of v0, /device:TPU:0, one launch (start us, length us, event | category | flops | bytes accessed | tf_op | source)
XLA Modules:
  0.0 932.4 jit_solution(13913219721741613737)
XLA Ops:
  12.4 6.9 convolution_add_fusion
  51.9 7.4 multiply_convert_fusion.2
  59.3 9.1 fusion.100
  82.6 21.8 %all-gather.5.cloned.1.call-done = bf16[3072,512]{0,1:T(8,128)(2,1)} async-done(((bf16[384,512]{0,1:T(8,128)(2,1)}), bf16[3072,512]{0,1:T(8,128)(2,1)}) %all-gather.5.cloned.1.call-update) | async-done | bytes 3145744 | tf_op jit(solution)/shard_map/all_gather | solution.py:122
  112.4 54.9 %all-gather.7.cloned.1.call-done = bf16[3072,512]{0,1:T(8,128)(2,1)} async-done(((bf16[384,512]{0,1:T(8,128)(2,1)}), bf16[3072,512]{0,1:T(8,128)(2,1)}) %all-gather.7.cloned.1.call-update) | async-done | bytes 3145744 | tf_op jit(solution)/shard_map/all_gather | solution.py:123
  167.4 8.4 multiply_reduce_fusion.1
  175.8 11.4 %fusion.40 = f32[384,2,256]{2,0,1:T(8,128)} fusion(bf16[3072,2,256]{0,2,1:T(8,128)(2,1)} %bitcast.127, f32[2,384,3072]{2,1,0:T(8,128)} %copy-done.2, bf16[384,2,256]{0,2,1:T(8,128)(2,1)} %bitcast.106, bf16[3072,2,256]{0,2,1:T(8,128)(2,1)} %bitcast.129, f32[2,384]{1,0:T(2,128)S(1)} %bitcast.123, f32[2,384]{1,0:T(2,128)S(1)} %log_add_fusion, ...), kind=kOutput, calls=%fused_computation.67 | convolution fusion | flops 2432434176 | bytes 18094080 | tf_op jit(solution)/shard_map/hqk,khd->qhd/dot_general | solution.py:202
  189.5 31.1 %all_gather.25 = f32[3072,2]{0,1:T(2,128)S(1)} all-gather(f32[384,2]{0,1:T(2,128)S(1)} %get-tuple-element.61), channel_id=1, replica_groups=mesh['ctx'=8,'tp'=4] {'ctx'}, dimensions={0}, use_global_device_ids=true | all-gather | bytes 27648 | tf_op jit(solution)/shard_map/all_gather | solution.py:206
  220.7 31.0 %all_gather.23 = f32[3072,2]{0,1:T(2,128)S(1)} all-gather(f32[384,2]{0,1:T(2,128)S(1)} %get-tuple-element.55), channel_id=1, replica_groups=mesh['ctx'=8,'tp'=4] {'ctx'}, dimensions={0}, use_global_device_ids=true | all-gather | bytes 27648 | tf_op jit(solution)/shard_map/all_gather | solution.py:205
  251.7 8.1 fusion.101
  259.8 31.8 %all-gather.11.cloned.1.call-done = bf16[3072,512]{1,0:T(8,128)(2,1)} async-done(((bf16[384,512]{1,0:T(8,128)(2,1)}), bf16[3072,512]{1,0:T(8,128)(2,1)}) %all-gather.11.cloned.1.call-update) | async-done | bytes 3145744 | tf_op jit(solution)/shard_map/all_gather | solution.py:211
  296.2 13.1 %fusion.41 = f32[384,2,256]{2,0,1:T(8,128)} fusion(bf16[3072,2,256]{0,2,1:T(8,128)(2,1)} %bitcast.98, f32[2,3072,384]{2,1,0:T(8,128)} %fusion.101, bf16[3072,2,256]{0,2,1:T(8,128)(2,1)} %bitcast.95, f32[2,3072]{1,0:T(2,128)S(1)} %bitcast.118, f32[2,3072]{1,0:T(2,128)S(1)} %bitcast.116, pred[3072,384]{1,0:T(8,128)(4,1)} %broadcast_compare_fusion, ...), kind=kOutput, calls=%fused_computation.68 | convolution fusion | flops 2432434176 | bytes 18137088 | tf_op jit(solution)/shard_map/hqk,qhd->khd/dot_general | solution.py:221
  312.0 7.1 fusion.45
  326.2 7.1 convolution_convert_fusion.5
  339.6 10.7 %convolution_convert_fusion.1 = bf16[2048,2048]{1,0:T(8,128)(2,1)} fusion(bf16[384,2048]{1,0:T(8,128)(2,1)} %copy-done.24, f32[2048]{0:T(1024)S(1)} %bitcast.122, f32[2048]{0:T(1024)S(1)} %bitcast.112, f32[384,2048]{1,0:T(8,128)} %param.12, f32[384]{0:T(512)S(1)} %add_rsqrt_fusion, f32[384]{0:T(512)S(1)} %broadcast_multiply_fusion.5), kind=kOutput, calls=%fused_computation.6 | convolution fusion | flops 3229351936 | bytes 13126656 | tf_op jit(solution)/shard_map/rd,rf->df/dot_general | solution.py:164
  350.6 9.7 %convolution_convert_fusion = bf16[2048,2048]{1,0:T(8,128)(2,1)} fusion(bf16[384,2048]{1,0:T(8,128)(2,1)} %copy-done.23, bf16[384,2048]{1,0:T(8,128)(2,1)} %copy-done.14), kind=kOutput, calls=%fused_computation.5 | convolution fusion | flops 3225419776 | bytes 11534336 | tf_op jit(solution)/shard_map/rf,rd->fd/dot_general | solution.py:157
  360.4 8.5 convolution_convert_fusion.2
  370.5 57.9 %all-reduce.4.cloned.1.call-done = (bf16[384,2048]{1,0:T(8,128)(2,1)}, bf16[384,2048]{1,0:T(8,128)(2,1)}, bf16[384,2048]{1,0:T(8,128)(2,1)}) async-done(((bf16[384,2048]{1,0:T(8,128)(2,1)}, bf16[384,2048]{1,0:T(8,128)(2,1)}, bf16[384,2048]{1,0:T(8,128)(2,1)}), (bf16[384,2048]{1,0:T(8,128)(2,1)}, bf16[384,2048]{1,0:T(8,128)(2,1)}, bf16[384,2048]{1,0:T(8,128)(2,1)})) %all-reduce.4.cloned.1.call-update) | async-done | bytes 4718608 | tf_op jit(solution)/shard_map/psum | solution.py:154
  437.5 37.5 %all-reduce = (bf16[1536]{0:T(1024)(128)(2,1)S(1)}, bf16[2048]{0:T(1024)(128)(2,1)S(1)}, bf16[2048]{0:T(1024)(128)(2,1)S(1)}, bf16[2,2048]{1,0:T(2,128)(2,1)S(1)}, bf16[2,2048]{1,0:T(2,128)(2,1)S(1)}) all-reduce(bf16[1536]{0:T(1024)(128)(2,1)S(1)} %convert_element_type.179, ...), channel_id=1, replica_groups=mesh['ctx'=8,'tp'=4] {'ctx'}, use_global_device_ids=true, to_apply=%region_16.17 | all-reduce | flops 13824 | bytes 55296 | tf_op jit(solution)/shard_map/psum | solution.py:265
  478.0 7.0 fusion.24
  485.0 16.7 %reduce-scatter.7.cloned.1.call-done = bf16[512,256]{1,0:T(8,128)(2,1)} async-done(((bf16[512,2048]{1,0:T(8,128)(2,1)}), bf16[512,256]{1,0:T(8,128)(2,1)}) %reduce-scatter.7.cloned.1.call-update) | async-done | bytes 262160 | tf_op jit(solution)/shard_map/reduce_scatter | solution.py:257
  503.4 148.2 %reduce-scatter.9.cloned.1.call-done = bf16[256,2048]{1,0:T(8,128)(2,1)} async-done(((bf16[2048,2048]{1,0:T(8,128)(2,1)}), bf16[256,2048]{1,0:T(8,128)(2,1)}) %reduce-scatter.9.cloned.1.call-update) | async-done | bytes 1048592 | tf_op jit(solution)/shard_map/reduce_scatter | solution.py:252
  654.4 147.8 %reduce-scatter.11.cloned.1.call-done = bf16[2048,256]{1,0:T(8,128)(2,1)} async-done(((bf16[2048,2048]{1,0:T(8,128)(2,1)}), bf16[2048,256]{1,0:T(8,128)(2,1)}) %reduce-scatter.11.cloned.1.call-update) | async-done | bytes 1048592 | tf_op jit(solution)/shard_map/reduce_scatter | solution.py:260
  805.0 118.1 %reduce-scatter.5.cloned.1.call-done = bf16[256,1536]{1,0:T(8,128)(2,1)} async-done(((bf16[2048,1536]{1,0:T(8,128)(2,1)}), bf16[256,1536]{1,0:T(8,128)(2,1)}) %reduce-scatter.5.cloned.1.call-update) | async-done | bytes 786448 | tf_op jit(solution)/shard_map/reduce_scatter | solution.py:249
  (152 shorter events, 106.3 us)
Async XLA Ops:
  7.2 40.5 %copy-start = (bf16[512,2048]{1,0:T(8,128)(2,1)S(1)}, bf16[512,2048]{1,0:T(8,128)(2,1)}, u32[]{:S(2)}) copy-start(bf16[512,2048]{1,0:T(8,128)(2,1)} %param.18) | copy-start | bytes 6291460
  7.2 97.2 %all-gather.5.cloned.1.call-start = ((), (), s32[]{:S(2)}) async-start(), calls=%async_computation.4 | async-start | bytes 3538944 | tf_op jit(solution)/shard_map/all_gather | solution.py:122
  7.3 4.8 copy-start.18
  7.3 4.8 copy-start.21
  26.4 6.8 copy-start.20
  37.9 8.6 copy-start.5
  38.9 128.5 %all-gather.7.cloned.1.call-start = ((), (), s32[]{:S(2)}) async-start(), calls=%async_computation.5 | async-start | bytes 3538944 | tf_op jit(solution)/shard_map/all_gather | solution.py:123
  40.9 210.8 %all-gather.9.cloned.1.call-start = ((), (), s32[]{:S(2)}) async-start(), calls=%async_computation.6 | async-start | bytes 3538944 | tf_op jit(solution)/shard_map/all_gather | solution.py:210
  42.3 7.2 copy-start.13
  43.2 248.4 %all-gather.11.cloned.1.call-start = ((), (), s32[]{:S(2)}) async-start(), calls=%async_computation.7 | async-start | bytes 3538944 | tf_op jit(solution)/shard_map/all_gather | solution.py:211
  49.5 378.9 %all-reduce.4.cloned.1.call-start = ((), (), s32[]{:S(2)}) async-start(), calls=%async_computation.12 | async-start | bytes 9437184 | tf_op jit(solution)/shard_map/psum | solution.py:154
  51.8 23.2 %slice-start = ((s8[8388608]{0:T(1024)(128)(4,1)}), s8[4194304]{0:T(1024)(128)(4,1)S(1)}, s32[]{:S(2)}) async-start(s8[8388608]{0:T(1024)(128)(4,1)} %bitcast.124), calls=%async_computation.13 | async-start | bytes 8388608
  59.2 9.1 copy-start.23
  59.2 9.1 copy-start.15
  59.3 15.8 %slice-start.1 = ((s8[8388608]{0:T(1024)(128)(4,1)}), s8[4194304]{0:T(1024)(128)(4,1)S(1)}, s32[]{:S(2)}) async-start(s8[8388608]{0:T(1024)(128)(4,1)} %bitcast.124), calls=%async_computation.14 | async-start | bytes 8388608
  296.2 13.1 %copy-start.7 = (f32[384,2,256]{2,0,1:T(8,128)S(1)}, f32[384,2,256]{2,0,1:T(8,128)}, u32[]{:S(2)}) copy-start(f32[384,2,256]{2,0,1:T(8,128)} %fusion.40) | copy-start | bytes 2359300
  296.2 13.1 %copy-start.12 = (f32[384,64]{1,0:T(8,128)S(1)}, f32[384,64]{1,0:T(8,128)}, u32[]{:S(2)}) copy-start(f32[384,64]{1,0:T(8,128)} %copy-done.11) | copy-start | bytes 294916
  326.2 7.1 copy-start.4
  326.2 7.1 copy-start.16
  335.5 166.1 %reduce-scatter.7.cloned.1.call-start = ((), (), s32[]{:S(2)}) async-start(), calls=%async_computation.9 | async-start | bytes 2359296 | tf_op jit(solution)/shard_map/reduce_scatter | solution.py:257
  339.6 312.1 %reduce-scatter.9.cloned.1.call-start = ((), (), s32[]{:S(2)}) async-start(), calls=%async_computation.10 | async-start | bytes 9437184 | tf_op jit(solution)/shard_map/reduce_scatter | solution.py:252
  350.3 451.9 %reduce-scatter.11.cloned.1.call-start = ((), (), s32[]{:S(2)}) async-start(), calls=%async_computation.11 | async-start | bytes 9437184 | tf_op jit(solution)/shard_map/reduce_scatter | solution.py:260
  360.4 562.7 %reduce-scatter.5.cloned.1.call-start = ((), (), s32[]{:S(2)}) async-start(), calls=%async_computation.8 | async-start | bytes 7077888 | tf_op jit(solution)/shard_map/reduce_scatter | solution.py:249
  431.7 46.3 %copy-start.19 = (f32[2048]{0:T(1024)S(1)}, f32[2048]{0:T(1024)}, u32[]{:S(2)}) copy-start(f32[2048]{0:T(1024)} %param.19) | copy-start | bytes 24580
  (12 other events, 32.7 us)
Sparse Core Ops, SparseCore 0:
  39.0 65.3 all-gather.4
  106.5 60.8 all-gather.6
  169.4 61.2 all-gather.8
  233.3 58.2 all-gather.10
  335.6 92.6 all-reduce.3
  432.3 69.2 reduce-scatter.6
  505.3 146.3 reduce-scatter.8
  655.3 146.9 reduce-scatter.10
  805.8 117.1 reduce-scatter.4
where the time goes:
time: 939 us; the launch traced here: 932 us
  waiting for transfers between devices  597 us (64%)
  matrix products  131 us (14%)
  blocking collectives  99.6 us (11%)
  other arithmetic  56.1 us (6%)
  local copies, waits for them, and re-layouts  32.6 us (3%)
  between operations  14.8 us (2%)
    reduce_scatter x1, waiting for transfers between devices, shards(): lax.psum_scatter(grad_up.astype(jnp.bfloat16), 'ctx', scatter_dimension=0...  148 us
    reduce_scatter x1, waiting for transfers between devices, shards(): lax.psum_scatter(grad_down.astype(jnp.bfloat16), 'ctx', scatter_dimension...  148 us
    reduce_scatter x1, waiting for transfers between devices, shards(): lax.psum_scatter(grad_qkv.astype(jnp.bfloat16), 'ctx', scatter_dimension=...  118 us
    psum x1, waiting for transfers between devices, shards(): lax.psum(branch_part.astype(jnp.bfloat16), 'tp').astype(jnp.float32)  57.9 us
    all_gather x1, waiting for transfers between devices, shards(): value_piece = lax.all_gather(value_b, 'ctx', axis=0, tiled=True)  54.9 us
    psum x1, blocking collectives, shards(): lax.psum(grad_bqkv.astype(jnp.bfloat16), 'ctx').astype(jnp.float32)  37.5 us
    all_gather x1, waiting for transfers between devices, shards(): grad_piece = lax.all_gather(out_grad, 'ctx', axis=0, tiled=True)  31.8 us
    all_gather x1, blocking collectives, shards(): lax.all_gather(row_dot.T, 'ctx', axis=0, tiled=True)  31.1 us
  transfers between devices with their start and end apart: 9, of which 8 were waited for; matrix products, arithmetic and copies ran while one was open for 15% of the time, Pallas kernels for 0%

commit v1 on v0

v1 whole, which is shorter than its diff:
```python
import functools
import math

import jax
import jax.numpy as jnp
from jax import lax
from jax.experimental import pallas as pl
from jax.experimental.pallas import tpu as pltpu
from jax.sharding import PartitionSpec as P

HD = 256
ROT = 64
LANES = 128
TILE = 256

masked_value = -1e30
norm_epsilon = 1e-05
root_half = 0.7071067811865476
inverse_root_two_pi = 0.3989422804014327

F32 = jnp.float32
BF16 = jnp.bfloat16
MESH = pl.DeviceIdType.MESH
ANY = pl.BlockSpec(memory_space=pl.ANY)
VMEM = pl.BlockSpec(memory_space=pltpu.VMEM)
SMEM = pl.BlockSpec(memory_space=pltpu.SMEM)


def nt(a, b):
    return lax.dot_general(a, b, (((1,), (1,)), ((), ())), preferred_element_type=F32)


def nn(a, b):
    return lax.dot_general(a, b, (((1,), (0,)), ((), ())), preferred_element_type=F32)


def tn(a, b):
    return lax.dot_general(a, b, (((0,), (0,)), ((), ())), preferred_element_type=F32)


def rope_tables(positions):
    half_rot = ROT // 2
    frequency = jnp.exp(jnp.arange(half_rot, dtype=F32) * (-2.0 * math.log(10000.0) / ROT))
    angles = positions.astype(F32)[..., None] * frequency
    cosine, sine = jnp.cos(angles), jnp.sin(angles)
    rest = angles.shape[:-1] + (LANES - ROT,)
    return (
        jnp.concatenate([cosine, cosine, jnp.ones(rest, F32)], axis=-1),
        jnp.concatenate([sine, sine, jnp.zeros(rest, F32)], axis=-1),
    )


def turn(first, cosine, sine, sign):
    half_rot = ROT // 2
    scaled = first * sine if sign < 0 else first
    lane = lax.broadcasted_iota(jnp.int32, first.shape, 1)
    down = jnp.where(lane < half_rot, pltpu.roll(scaled, LANES - half_rot, 1), 0.0)
    up = jnp.where(
        jnp.logical_and(lane >= half_rot, lane < ROT), pltpu.roll(scaled, half_rot, 1), 0.0
    )
    if sign < 0:
        return first * cosine + (down - up)
    return first * cosine + (up - down) * sine


def front_kernel(
    order,
    side_ref,
    x_ref,
    cot_ref,
    gain_ref,
    bias_ref,
    w_ref,
    b_ref,
    wo_ref,
    cos_ref,
    sin_ref,
    attn_o,
    mlp_o,
    cot_o,
    kv_o,
    qg_o,
):
    step = pl.program_id(0)
    blk = x_ref.shape[1]
    half = x_ref.shape[2] // 2
    own_heads = kv_o.shape[-1] // (2 * HD)
    width = own_heads * HD
    chunk = 64

    @pl.when(step == 0)
    def _():
        for lh in range(2):

            def norm(i, _):
                at = pl.ds(pl.multiple_of(i * chunk, chunk), chunk)
                to = pl.ds(pl.multiple_of(lh * blk + i * chunk, chunk), chunk)
                x = x_ref[order[lh], at, :]
                centred = x - jnp.mean(x, axis=-1, keepdims=True)
                variance = jnp.mean(centred * centred, axis=-1, keepdims=True)
                unit = centred * lax.rsqrt(variance + norm_epsilon)
                a = (unit * gain_ref[0:1, :] + bias_ref[0:1, :]).astype(BF16)
                m = (unit * gain_ref[1:2, :] + bias_ref[1:2, :]).astype(BF16)
                c = cot_ref[order[lh], at, :].astype(BF16)
                for out, value in ((attn_o, a), (mlp_o, m), (cot_o, c)):
                    out[0, to, :] = value[:, :half]
                    out[1, to, :] = value[:, half:]
                return 0

            lax.fori_loop(0, blk // chunk, norm, 0)

        def out_grad(h, _):
            at = pl.ds(pl.multiple_of(h * HD, HD), HD)
            g = nt(cot_o[0], wo_ref[at, :half]) + nt(cot_o[1], wo_ref[at, half:])
            g = g.astype(BF16).reshape(2, blk, HD)
            which = jnp.where(h // own_heads == side_ref[0], 0, 1)
            for k in range(own_heads):

                @pl.when(lax.rem(h, own_heads) == k)
                def _():
                    qg_o[which, :, :, width + k * HD : width + (k + 1) * HD] = g

            return 0

        lax.fori_loop(0, 2 * own_heads, out_grad, 0)

    head, kind = step // 3, lax.rem(step, 3)
    z = nn(attn_o[0], w_ref[:half, :]) + nn(attn_o[1], w_ref[half:, :]) + b_ref[0]
    which = jnp.where(head // own_heads == side_ref[0], 0, 1)
    first = z[:, :LANES]
    turned = turn(first, cos_ref[...], sin_ref[...], 1)
    first = jnp.where(kind < 2, turned, first).astype(BF16).reshape(2, blk, LANES)
    rest = z[:, LANES:].astype(BF16).reshape(2, blk, HD - LANES)
    for k in range(own_heads):
        for what, out, base in ((0, qg_o, 0), (1, kv_o, 0), (2, kv_o, width)):

            @pl.when(jnp.logical_and(kind == what, lax.rem(head, own_heads) == k))
            def _():
                at = base + k * HD
                out[which, :, :, at : at + LANES] = first
                out[which, :, :, at + LANES : at + HD] = rest


def front(order, side, stream_in, cotangent, ln_gain, ln_bias, w_qkv, b_qkv, w_out, cosine, sine):
    rows, model = stream_in.shape
    blk, half = rows // 2, model // 2
    tiles = w_qkv.shape[1] // HD
    width = w_out.shape[0] // 2
    whole = lambda a: pl.BlockSpec(a.shape, lambda i, *_: (0,) * a.ndim)
    tokens = jax.ShapeDtypeStruct((2, rows, half), BF16)
    heads = jax.ShapeDtypeStruct((2, 2, blk, 2 * width), BF16)
    outs = (tokens, tokens, tokens, heads, heads)
    x, c = stream_in.reshape(2, blk, model), cotangent.reshape(2, blk, model)
    b = b_qkv.reshape(tiles, 1, HD)
    return pl.pallas_call(
        front_kernel,
        name="front",
        out_shape=outs,
        grid_spec=pltpu.PrefetchScalarGridSpec(
            num_scalar_prefetch=2,
            grid=(tiles,),
            in_specs=[
                whole(x),
                whole(c),
                whole(ln_gain),
                whole(ln_bias),
                pl.BlockSpec((model, HD), lambda i, *_: (0, i)),
                pl.BlockSpec((1, 1, HD), lambda i, *_: (i, 0, 0)),
                whole(w_out),
                whole(cosine),
                whole(sine),
            ],
            out_specs=[whole(o) for o in outs],
        ),
        cost_estimate=pl.CostEstimate(
            flops=2 * rows * model * (w_qkv.shape[1] + w_out.shape[0]),
            transcendentals=rows,
            bytes_accessed=2 * w_qkv.size + 2 * w_out.size + 8 * x.size + 10 * x.size,
        ),
        compiler_params=pltpu.CompilerParams(vmem_limit_bytes=50 * 1024 * 1024),
    )(order, side, x, c, ln_gain, ln_bias, w_qkv, b, w_out, cosine, sine)


DOWN, UP, OUT, QKV = range(4)
(Y_KV, Y_QG, Y_COT, Y_MLP, Y_ATTN, Y_ACT, Y_HID, Y_ATT, Y_GQKV, Y_FIN) = range(10)
BRANCH, MLPB, ATTNB = range(3)


def middle_kernel(
    line,
    n_tp,
    kv_in,
    qg_in,
    attn_in,
    mlp_in,
    cot_in,
    w_up,
    w_down,
    w_out,
    w_qkv,
    b_up,
    row_pos,
    col_pos,
    cosine,
    sine,
    down_o,
    up_o,
    out_o,
    qkv_o,
    branch_o,
    mlpb_o,
    attnb_o,
    bup_o,
    bqkv_o,
    kv_all,
    qg_all,
    rs_down,
    rs_up,
    rs_out,
    rs_qkv,
    attn_far,
    cot,
    cot_far,
    norm,
    norm_far,
    act,
    hid,
    act_far,
    hid_far,
    wcol,
    wrow,
    c_down,
    c_up,
    c_out,
    c_qkv,
    stage_down,
    stage_up,
    stage_out,
    stage_qkv,
    tp_part,
    tp_recv,
    kv_own,
    qg_own,
    chunk,
    att,
    att_far,
    stats,
    stats_all,
    gqkv,
    gqkv_far,
    acc_a,
    acc_b,
    run_m,
    run_l,
    ag_s,
    ag_r,
    y_s,
    y_r,
    core_s,
    core_r,
    rs_s,
    rs_r,
    tp_s,
    tp_r,
    st_s,
    st_r,
    local,
    wsem,
    csem,
    tsem,
):
    me, tp = lax.axis_index("ctx"), lax.axis_index("tp")
    z, y = me // 2, lax.rem(me, 2)
    core = lax.rem(tp, 2)
    partner = (me + 1 - 2 * y, tp)
    sibling = (me, tp + 1 - 2 * core)
    right, left = (me + 2, tp), (me - 2, tp)
    far_steps = []
    step = 2
    while step < n_tp:
        far_steps.append((me, tp + step - 2 * step * lax.rem(tp // step, 2)))
        step *= 2

    rows = norm.shape[1]
    blk = rows // 2
    half = norm.shape[2]
    hidden_half = act.shape[2]
    own_heads = kv_own.shape[-1] // (2 * HD)
    width = own_heads * HD
    block_cols = 2 * half // line
    scale = HD ** (-0.5)

    def place_of(j):
        return lax.rem(z + j, line) * 2 + y

    barrier = pltpu.get_barrier_semaphore()
    greet = [partner, sibling] + far_steps + [(place_of(j), tp) for j in range(1, line)]
    for device in greet:
        pl.semaphore_signal(barrier, inc=1, device_id=device, device_id_type=MESH)
    pl.semaphore_wait(barrier, len(greet))

    def rcopy(src, dst, s, r, device):
        return pltpu.make_async_remote_copy(
            src_ref=src, dst_ref=dst, send_sem=s, recv_sem=r, device_id=device, device_id_type=MESH
        )

    def lcopy(src, dst, sem):
        return pltpu.make_async_copy(src, dst, sem)

    def fin_parts(t):
        c = (c_down, c_up, c_out, c_qkv)[t]
        if t == DOWN:
            dst = down_o.at[pl.ds(pl.multiple_of(y * hidden_half, hidden_half), hidden_half), :]
        elif t == UP:
            dst = up_o.at[:, pl.ds(pl.multiple_of(y * hidden_half, hidden_half), hidden_half)]
        elif t == OUT:
            dst = out_o.at[pl.ds(pl.multiple_of(y * width, width), width), :]
        else:
            dst = qkv_o.at[:, pl.ds(pl.multiple_of(y * 3 * width, 3 * width), 3 * width)]
        return c, dst

    def y_copy(item, t=0):
        if item == Y_KV:
            src, dst = kv_in.at[1], kv_all.at[:, 1]
        elif item == Y_QG:
            src, dst = qg_in.at[1], qg_all.at[:, 1]
        elif item == Y_COT:
            src, dst = cot_in.at[core], cot_far.at[core]
        elif item == Y_MLP:
            src, dst = mlp_in.at[core], norm_far.at[core]
        elif item == Y_ATTN:
            src, dst = attn_in.at[core], attn_far.at[core]
        elif item == Y_ACT:
            src, dst = act.at[1 - y], act_far
        elif item == Y_HID:
            src, dst = hid.at[1 - y], hid_far
        elif item == Y_ATT:
            src, dst = att.at[:, 1], att_far
        elif item == Y_GQKV:
            src, dst = gqkv.at[:, 1], gqkv_far
        else:
            c, dst = fin_parts(t)
            src = c.at[0, 1 - y]
            item = Y_FIN + t
        return rcopy(src, dst, y_s.at[item], y_r.at[item], partner)

    def core_copy(k):
        ref = (cot_far, norm_far, attn_far)[k]
        return rcopy(ref.at[core], ref.at[core], core_s.at[k], core_r.at[k], sibling)

    def pass_on(item, k):
        y_copy(item).wait_recv()
        core_copy(k).start()

    def ag_copy(t, h, to, hop, j_src, j_dst):
        ref = (kv_all, qg_all)[t]
        return rcopy(
            ref.at[:, 2 * j_src + h],
            ref.at[:, 2 * j_dst + h],
            ag_s.at[t, h, to, hop],
            ag_r.at[t, h, j_dst],
            (right, left)[to],
        )

    def ag_wait(t, h, hop):
        @pl.when(z >= hop)
        def _():
            ag_copy(t, h, 0, hop, line - hop, line - hop).wait_recv()

        @pl.when(z + hop <= line - 1)
        def _():
            ag_copy(t, h, 1, hop, hop, hop).wait_recv()

    def ag_send_when(hop):
        return (
            jnp.logical_and(z >= hop - 1, z <= line - 2),
            jnp.logical_and(z + hop - 1 <= line - 1, z >= 1),
        )

    def ag_hop(t, h, hop):
        if not (isinstance(hop, int) and hop == 1):
            ag_wait(t, h, hop - 1)
        to_right, to_left = ag_send_when(hop)

        @pl.when(to_right)
        def _():
            ag_copy(t, h, 0, hop, lax.rem(line - hop + 1, line), line - hop).start()

        @pl.when(to_left)
        def _():
            ag_copy(t, h, 1, hop, hop - 1, hop).start()

    def ag_rest(t, h, hop):
        def one(i, _):
            ag_hop(t, h, i)
            return 0

        if hop < line:
            lax.fori_loop(hop, line, one, 0)
        ag_wait(t, h, line - 1)

    def ag_drain(t, h):
        def one(hop, _):
            to_right, to_left = ag_send_when(hop)

            @pl.when(to_right)
            def _():
                ag_copy(t, h, 0, hop, lax.rem(line - hop + 1, line), line - hop).wait_send()

            @pl.when(to_left)
            def _():
                ag_copy(t, h, 1, hop, hop - 1, hop).wait_send()

            return 0

        lax.fori_loop(1, line, one, 0)

    rs = (
        (c_down, rs_down, stage_down),
        (c_up, rs_up, stage_up),
        (c_out, rs_out, stage_out),
        (c_qkv, rs_qkv, stage_qkv),
    )

    def rs_copy(t, j, slot, device):
        c, recv, _ = rs[t]
        return rcopy(c.at[j], recv.at[slot], rs_s.at[t, j], rs_r.at[t, slot], device)

    def rs_take(t, j, slot):
        c, recv, held = rs[t]
        rs_copy(t, j, slot, partner).wait_recv()
        copy = lcopy(recv.at[slot], held, tsem.at[t])
        copy.start()
        copy.wait()
        n = c.shape[2]
        part = min(64, n)

        def add(i, _):
            at = pl.ds(pl.multiple_of(i * part, part), part)
            for s in range(2):
                c[j, s, at, :] = (c[j, s, at, :].astype(F32) + held[s, at, :].astype(F32)).astype(
                    BF16
                )
            return 0

        lax.fori_loop(0, n // part, add, 0)

    def rs_step(t, hop):
        jr, jl = line - hop, hop

        @pl.when(hop >= z + 1)
        def _():
            @pl.when(z >= 1)
            def _():
                rs_take(t, jr, jr)

            rs_copy(t, jr, jr - 1, right).start()

        @pl.when(hop >= line - z)
        def _():
            @pl.when(z <= line - 2)
            def _():
                rs_take(t, jl, jl)

            rs_copy(t, jl, jl + 1, left).start()

    def rs_rest(t, hop):
        def one(i, _):
            rs_step(t, i)
            return 0

        if hop < line:
            lax.fori_loop(hop, line, one, 0)

    def rs_finish(t):
        @pl.when(z >= 1)
        def _():
            rs_take(t, 0, 0)

        @pl.when(z <= line - 2)
        def _():
            rs_take(t, 0, line)

        c, dst = fin_parts(t)
        y_copy(Y_FIN, t).start()
        lcopy(c.at[0, y], dst, local.at[4 + t]).start()

    def rs_drain(t):
        def one(j, _):
            @pl.when(j <= line - 1 - z)
            def _():
                rs_copy(t, j, j - 1, right).wait_send()

            @pl.when(j > line - 1 - z)
            def _():
                rs_copy(t, j, j + 1, left).wait_send()

            return 0

        lax.fori_loop(1, line, one, 0)
        c, dst = fin_parts(t)
        y_copy(Y_FIN, t).wait()
        lcopy(c.at[0, y], dst, local.at[4 + t]).wait()

    tp_out = (branch_o, mlpb_o, attnb_o)
    last = len(far_steps) + 1

    def tp_copy(i, k):
        part = tp_part.at[i]
        if k == 0:
            src, dst, device = part.at[1 - core], tp_recv.at[i, 0], sibling
        elif k < last:
            src, dst, device = part.at[core], tp_recv.at[i, k], far_steps[k - 1]
        else:
            src, dst, device = part.at[core], tp_out[i].at[core], sibling
        return rcopy(src, dst, tp_s.at[i, k], tp_r.at[i, k], device)

    def tp_add(i, k):
        part = 64

        def add(n, _):
            at = pl.ds(pl.multiple_of(n * part, part), part)
            tp_part[i, core, at, :] = (
                tp_part[i, core, at, :].astype(F32) + tp_recv[i, k, at, :].astype(F32)
            ).astype(BF16)
            return 0

        lax.fori_loop(0, blk // part, add, 0)

    def tp_next(i, k):
        if k > 1:
            tp_copy(i, k - 1).wait_send()
        tp_copy(i, k - 1).wait_recv()
        tp_add(i, k - 1)
        tp_copy(i, k).start()
        if k == last:
            lcopy(tp_part.at[i, core], tp_out[i].at[core], local.at[8 + i]).start()

    def tp_rest(i):
        for k in range(1, last + 1):
            tp_next(i, k)

    def tp_drain(i):
        tp_copy(i, 0).wait_send()
        tp_copy(i, last).wait()
        lcopy(tp_part.at[i, core], tp_out[i].at[core], local.at[8 + i]).wait()

    def stream(lo, hi, fetches, body):
        for f in fetches:
            f(lo, lax.rem(lo, 2)).start()

        def one(i, _):
            slot = lax.rem(i, 2)

            @pl.when(i + 1 < hi)
            def _():
                for f in fetches:
                    f(i + 1, 1 - slot).start()

            for f in fetches:
                f(i, slot).wait()
            body(i, slot)
            return 0

        lax.fori_loop(lo, hi, one, 0)

    def col_tile(w):
        def fetch(i, slot):
            at = pl.ds(pl.multiple_of(i * TILE, TILE), TILE)
            return lcopy(w.at[:, at], wcol.at[slot, pl.ds(0, w.shape[0]), :], wsem.at[0, slot])

        return fetch

    def row_tile(w):
        def fetch(i, slot):
            at = pl.ds(pl.multiple_of(i * TILE, TILE), TILE)
            return lcopy(w.at[at, :], wrow.at[slot, pl.ds(0, TILE), pl.ds(0, w.shape[1])], wsem.at[1, slot])

        return fetch

    kv_own_load = lcopy(kv_in.at[0], kv_own.at[:, 0], local.at[11])
    qg_own_load = lcopy(qg_in.at[0], qg_own.at[:, 0], local.at[12])
    norm_load = lcopy(mlp_in, norm, local.at[2])
    cot_load = lcopy(cot_in, cot, local.at[3])
    y_copy(Y_KV).start()
    y_copy(Y_COT).start()
    kv_own_load.start()
    qg_own_load.start()
    norm_load.start()
    cot_load.start()
    kv_own_load.wait()
    lcopy(kv_own.at[:, 0], kv_all.at[:, 0], local.at[0]).start()
    qg_own_load.wait()
    lcopy(qg_own.at[:, 0], qg_all.at[:, 0], local.at[1]).start()
    norm_load.wait()
    cot_load.wait()
    lcopy(kv_own.at[:, 0], kv_all.at[:, 0], local.at[0]).wait()
    ag_hop(0, 0, 1)

    def feed_forward(i, slot):
        h = nn(norm[0], wcol[slot, :half, :]) + nn(norm[1], wcol[slot, half : 2 * half, :]) + b_up[i]
        gate = 0.5 * (1.0 + lax.erf(h * root_half))
        slope = gate + h * jnp.exp(-0.5 * h * h) * inverse_root_two_pi
        g = nt(cot[0], wrow[slot, :TILE, :half]) + nt(cot[1], wrow[slot, :TILE, half : 2 * half])
        g = g * slope
        bup_o[i] = jnp.sum(g, axis=0, keepdims=True)
        at = pl.ds(pl.multiple_of(lax.rem(i * TILE, hidden_half), TILE), TILE)
        which = i * TILE // hidden_half
        act[which, :, at] = (h * gate).astype(BF16)
        hid[which, :, at] = g.astype(BF16)

    hidden_tiles = 2 * hidden_half // TILE
    cut = hidden_tiles // 2
    stream(0, cut, (col_tile(w_up), row_tile(w_down)), feed_forward)

    y_copy(Y_KV).wait_recv()
    ag_hop(0, 1, 1)
    pass_on(Y_COT, 0)
    ag_hop(0, 0, 2)

    stream(cut, hidden_tiles, (col_tile(w_up), row_tile(w_down)), feed_forward)
    y_copy(Y_ACT).start()
    y_copy(Y_MLP).start()
    y_copy(Y_HID).start()
    y_copy(Y_QG).start()
    ag_hop(0, 1, 2)

    def part_tile(i, slot, value):
        at = pl.ds(pl.multiple_of(i * TILE, TILE), TILE)
        return at, value.astype(BF16).reshape(2, blk, TILE)

    def mlp_back(i, slot):
        value = nt(hid[0], wrow[slot, :TILE, :hidden_half]) + nt(hid[1], wrow[slot, :TILE, hidden_half : 2 * hidden_half])
        at, value = part_tile(i, slot, value)
        tp_part[MLPB, :, :, at] = value

    model_tiles = 2 * half // TILE
    stream(0, model_tiles, (row_tile(w_up),), mlp_back)
    tp_copy(MLPB, 0).start()
    ag_rest(0, 0, 3)

    def cols_at(ref, j):
        start = lax.rem(z + j, line) * block_cols
        at = pl.ds(pl.multiple_of(lax.rem(start, half), LANES), block_cols)
        return ref[start // half, :, at]

    def split_cols(ref, j, at, value):
        n = value.shape[1] // 2
        ref[j, 0, at, :] = value[:, :n].astype(BF16)
        ref[j, 1, at, :] = value[:, n:].astype(BF16)

    def split_rows(ref, j, at, value):
        n = value.shape[0] // 2
        ref[j, 0, :, at] = value[:n].astype(BF16)
        ref[j, 1, :, at] = value[n:].astype(BF16)

    y_copy(Y_ACT).wait_recv()
    core_copy(0).wait_recv()

    def share_down(j, _):
        g0, g1 = cols_at(cot, j), cols_at(cot_far, j)

        def one(i, _):
            at = pl.ds(pl.multiple_of(i * TILE, TILE), TILE)
            split_cols(c_down, j, at, tn(act[y, :, at], g0) + tn(act_far[:, at], g1))
            return 0

        lax.fori_loop(0, hidden_half // TILE, one, 0)
        return 0

    lax.fori_loop(0, line, share_down, 0)
    rs_step(DOWN, 1)
    tp_next(MLPB, 1)
    ag_hop(0, 1, 3) if line > 3 else None
    pass_on(Y_MLP, 1)

    y_copy(Y_HID).wait_recv()
    core_copy(1).wait_recv()

    def share_up(j, _):
        m0, m1 = cols_at(norm, j), cols_at(norm_far, j)

        def one(i, _):
            at = pl.ds(pl.multiple_of(i * TILE, TILE), TILE)
            split_rows(c_up, j, at, tn(m0, hid[y, :, at]) + tn(m1, hid_far[:, at]))
            return 0

        lax.fori_loop(0, hidden_half // TILE, one, 0)
        return 0

    lax.fori_loop(0, line, share_up, 0)
    rs_step(UP, 1)
    y_copy(Y_QG).wait_recv()
    lcopy(qg_own.at[:, 0], qg_all.at[:, 0], local.at[1]).wait()
    ag_hop(1, 0, 1)
    ag_hop(1, 1, 1)
    y_copy(Y_ATTN).start()
    ag_rest(0, 1, 4 if line > 3 else 3)
    lcopy(kv_all.at[:, 1], kv_own.at[:, 1], local.at[11]).start()
    lcopy(qg_all.at[:, 1], qg_own.at[:, 1], local.at[12]).start()
    lcopy(kv_all.at[:, 1], kv_own.at[:, 1], local.at[11]).wait()
    lcopy(qg_all.at[:, 1], qg_own.at[:, 1], local.at[12]).wait()

    pair = 2 * blk
    same = lax.broadcasted_iota(jnp.int32, (pair, pair), 0) == lax.broadcasted_iota(
        jnp.int32, (pair, pair), 1
    )

    def piece(t):
        def fetch(i, slot):
            ref = (kv_all, qg_all)[t]
            return lcopy(
                ref.at[i // line, pl.ds(2 * lax.rem(i, line), 2)], chunk.at[slot], csem.at[slot]
            )

        return fetch

    def heads_of(value, at):
        return value[:, :, at : at + HD].reshape(pair, HD)

    for lh in range(2):
        for head in range(own_heads):
            at_k, at_v = head * HD, width + head * HD
            run_m[...] = jnp.full(run_m.shape, masked_value, F32)
            run_l[...] = jnp.zeros(run_l.shape, F32)
            acc_a[...] = jnp.zeros(acc_a.shape, F32)

            def attend(i, slot):
                k = chunk[slot, :, :, at_k : at_k + HD].reshape(pair, HD)
                v = chunk[slot, :, :, at_v : at_v + HD].reshape(pair, HD)
                q = qg_own[lh, :, :, at_k : at_k + HD].reshape(pair, HD)
                s = nt(q, k) * scale
                s = jnp.where(row_pos[i] <= col_pos[lh], s, masked_value)
                old = run_m[...]
                top = jnp.maximum(old, jnp.max(s, axis=1, keepdims=True))
                p = jnp.exp(s - top)
                fade = jnp.exp(old - top)
                run_m[...] = top
                run_l[...] = run_l[...] * fade + jnp.sum(p, axis=1, keepdims=True)
                acc_a[...] = acc_a[...] * fade + nn(p.astype(BF16), v)

            stream(0, line * (lh + 1), (piece(0),), attend)
            out = (acc_a[...] / run_l[...]).astype(BF16)
            att[lh, :, :, at_k : at_k + HD] = out.reshape(2, blk, HD)
            log_total = run_m[...] + jnp.log(run_l[...])
            g = qg_own[lh, :, :, at_v : at_v + HD].reshape(pair, HD)
            dots = jnp.sum(g.astype(F32) * out.astype(F32), axis=1, keepdims=True)
            stats[lh, head, 0:1, :] = jnp.sum(jnp.where(same, log_total, 0.0), 0, keepdims=True)
            stats[lh, head, 1:2, :] = jnp.sum(jnp.where(same, dots, 0.0), 0, keepdims=True)
        if lh == 0:
            rs_step(DOWN, 2)

    def stat_copy(j, k):
        return rcopy(
            stats, stats_all.at[line - j], st_s.at[j], st_r.at[line - j], (place_of(j), tp)
        )

    for j in range(1, line):
        stat_copy(j, 0).start()
    y_copy(Y_ATT).start()
    ag_hop(1, 0, 2)
    ag_hop(1, 1, 2)
    tp_next(MLPB, 2)
    rs_step(UP, 2)

    def undo(value, lh, head, kind):
        at = (3 * head + kind) * HD
        value = value[...]
        first = value[:, :LANES]
        if kind < 2:
            first = turn(first, cosine[lh], sine[lh], -1)
        for lo, hi, part in ((0, LANES, first), (LANES, HD, value[:, LANES:])):
            bqkv_o[0:1, at + lo : at + hi] += jnp.sum(part, axis=0, keepdims=True)
            gqkv[lh, :, :, at + lo : at + hi] = part.astype(BF16).reshape(2, blk, hi - lo)

    bqkv_o[...] = jnp.zeros(bqkv_o.shape, F32)
    for lh in range(2):
        for head in range(own_heads):
            at_k, at_v = head * HD, width + head * HD
            run_m[...] = jnp.sum(
                jnp.where(same, stats[lh, head, 0:1, :], 0.0), axis=1, keepdims=True
            )
            run_l[...] = jnp.sum(
                jnp.where(same, stats[lh, head, 1:2, :], 0.0), axis=1, keepdims=True
            )
            acc_a[...] = jnp.zeros(acc_a.shape, F32)

            def back_q(i, slot):
                k = chunk[slot, :, :, at_k : at_k + HD].reshape(pair, HD)
                v = chunk[slot, :, :, at_v : at_v + HD].reshape(pair, HD)
                q = qg_own[lh, :, :, at_k : at_k + HD].reshape(pair, HD)
                g = qg_own[lh, :, :, at_v : at_v + HD].reshape(pair, HD)
                s = nt(q, k) * scale
                s = jnp.where(row_pos[i] <= col_pos[lh], s, masked_value)
                p = jnp.exp(s - run_m[...])
                ds = (p * (nt(g, v) - run_l[...]) * scale).astype(BF16)
                acc_a[...] += nn(ds, k)

            stream(0, line * (lh + 1), (piece(0),), back_q)
            undo(acc_a, lh, head, 0)

    def share_out(j, _):
        g0, g1 = cols_at(cot, j), cols_at(cot_far, j)

        def one(i, _):
            at = pl.ds(pl.multiple_of(i * TILE, TILE), TILE)
            a0 = att[:, 0, :, at].reshape(rows, TILE)
            a1 = att[:, 1, :, at].reshape(rows, TILE)
            split_cols(c_out, j, at, tn(a0, g0) + tn(a1, g1))
            return 0

        lax.fori_loop(0, width // TILE, one, 0)
        return 0

    lax.fori_loop(0, line, share_out, 0)
    rs_step(OUT, 1)
    rs_step(DOWN, 3) if line > 3 else None
    ag_rest(1, 0, 3)
    ag_rest(1, 1, 3)

    y_copy(Y_ATT).wait_recv()

    def branch(i, slot):
        value = nn(act[0], wcol[slot, :hidden_half, :]) + nn(act[1], wcol[slot, hidden_half : 2 * hidden_half, :])
        at, _ = part_tile(i, slot, value)
        own = att[:, 0].reshape(rows, width)
        far = att_far[...].reshape(rows, width)
        mine = wrow[0, pl.ds(pl.multiple_of(y * width, width), width), at]
        theirs = wrow[0, pl.ds(pl.multiple_of((1 - y) * width, width), width), at]
        value += nn(own, mine) + nn(far, theirs)
        tp_part[BRANCH, :, :, at] = value.astype(BF16).reshape(2, blk, TILE)

    w_out_load = lcopy(w_out, wrow.at[0, pl.ds(0, w_out.shape[0]), :], wsem.at[1, 0])
    w_out_load.start()
    w_out_load.wait()
    stream(0, model_tiles, (col_tile(w_down),), branch)
    tp_copy(BRANCH, 0).start()
    rs_step(UP, 3) if line > 3 else None

    for j in range(1, line):
        stat_copy(line - j, 0).wait_recv()
    lcopy(stats, stats_all.at[0], local.at[0]).start()
    lcopy(stats, stats_all.at[0], local.at[0]).wait()

    for lh in range(2):
        for head in range(own_heads):
            at_k, at_v = head * HD, width + head * HD
            acc_a[...] = jnp.zeros(acc_a.shape, F32)
            acc_b[...] = jnp.zeros(acc_b.shape, F32)

            def back_k(i, slot):
                q = chunk[slot, :, :, at_k : at_k + HD].reshape(pair, HD)
                g = chunk[slot, :, :, at_v : at_v + HD].reshape(pair, HD)
                k = kv_own[lh, :, :, at_k : at_k + HD].reshape(pair, HD)
                v = kv_own[lh, :, :, at_v : at_v + HD].reshape(pair, HD)
                stat = stats_all[lax.rem(i, line), i // line, head]
                s = nt(k, q) * scale
                s = jnp.where(col_pos[lh] <= row_pos[i], s, masked_value)
                p = jnp.exp(s - stat[0:1, :])
                ds = (p * (nt(v, g) - stat[1:2, :]) * scale).astype(BF16)
                acc_a[...] += nn(ds, q)
                acc_b[...] += nn(p.astype(BF16), g)

            stream(lh * line, 2 * line, (piece(1),), back_k)
            undo(acc_a, lh, head, 1)
            undo(acc_b, lh, head, 2)
    y_copy(Y_GQKV).start()
    tp_next(BRANCH, 1)
    pass_on(Y_ATTN, 2)
    norm_again = lcopy(attn_in, norm, local.at[2])
    norm_again.start()
    core_copy(2).wait_recv()
    far_again = lcopy(attn_far, norm_far, local.at[3])
    core_copy(1).wait_send()
    far_again.start()
    norm_again.wait()
    far_again.wait()

    def share_qkv(j, _):
        m0, m1 = cols_at(norm, j), cols_at(norm_far, j)

        def one(i, _):
            at = pl.ds(pl.multiple_of(i * TILE, TILE), TILE)
            g0 = gqkv[:, 0, :, at].reshape(rows, TILE)
            g1 = gqkv[:, 1, :, at].reshape(rows, TILE)
            split_rows(c_qkv, j, at, tn(m0, g0) + tn(m1, g1))
            return 0

        lax.fori_loop(0, 3 * width // TILE, one, 0)
        return 0

    lax.fori_loop(0, line, share_qkv, 0)
    rs_step(QKV, 1)
    rs_step(OUT, 2)
    y_copy(Y_GQKV).wait_recv()

    def attn_back(i, slot):
        own = gqkv[:, 0].reshape(rows, 3 * width)
        far = gqkv_far[...].reshape(rows, 3 * width)
        mine = wrow[slot, :TILE, pl.ds(pl.multiple_of(y * 3 * width, 3 * width), 3 * width)]
        theirs = wrow[slot, :TILE, pl.ds(pl.multiple_of((1 - y) * 3 * width, 3 * width), 3 * width)]
        at, value = part_tile(i, slot, nt(own, mine) + nt(far, theirs))
        tp_part[ATTNB, :, :, at] = value

    stream(0, model_tiles, (row_tile(w_qkv),), attn_back)
    tp_copy(ATTNB, 0).start()
    tp_next(BRANCH, 2)
    tp_next(ATTNB, 1)
    rs_rest(DOWN, 4 if line > 3 else 3)
    rs_rest(UP, 4 if line > 3 else 3)
    rs_finish(DOWN)
    rs_finish(UP)
    rs_step(QKV, 2)
    tp_next(ATTNB, 2)
    rs_rest(OUT, 3)
    rs_rest(QKV, 3)
    rs_finish(OUT)
    rs_finish(QKV)

    for t in range(2):
        for h in range(2):
            ag_drain(t, h)
    for item in (Y_KV, Y_QG, Y_COT, Y_MLP, Y_ATTN, Y_ACT, Y_HID, Y_ATT, Y_GQKV):
        y_copy(item).wait_send()
    core_copy(0).wait_send()
    core_copy(2).wait_send()
    for j in range(1, line):
        stat_copy(j, 0).wait_send()
    for i in range(3):
        tp_drain(i)
    for t in range(4):
        rs_drain(t)


def middle(line, n_tp, kv, qg, attn_in, mlp_in, cot_b, w_up, w_down, w_out, w_qkv, b_up, row_pos, col_pos, cosine, sine):
    _, rows, half = mlp_in.shape
    model = 2 * half
    blk = rows // 2
    hidden = w_up.shape[1]
    hidden_half = hidden // 2
    width = kv.shape[-1] // 2
    own_heads = width // HD
    part_cols = model // line // 2
    pair = 2 * blk
    tp_steps = 0
    while (2 << tp_steps) < n_tp:
        tp_steps += 1
    shares = (
        (2, hidden_half, part_cols),
        (2, part_cols, hidden_half),
        (2, width, part_cols),
        (2, part_cols, 3 * width),
    )
    b = lambda *s: jax.ShapeDtypeStruct(s, BF16)
    f = lambda *s: jax.ShapeDtypeStruct(s, F32)
    vb = lambda *s: pltpu.VMEM(s, BF16)
    vf = lambda *s: pltpu.VMEM(s, F32)
    dma = pltpu.SemaphoreType.DMA
    outs = (
        b(hidden, part_cols),
        b(part_cols, hidden),
        b(2 * width, part_cols),
        b(part_cols, 6 * width),
        b(2, blk, model),
        b(2, blk, model),
        b(2, blk, model),
        f(hidden // TILE, 1, TILE),
        f(1, 3 * width),
        b(2, 2 * line, blk, 2 * width),
        b(2, 2 * line, blk, 2 * width),
        b(line + 1, *shares[0]),
        b(line + 1, *shares[1]),
        b(line + 1, *shares[2]),
        b(line + 1, *shares[3]),
        b(2, rows, half),
    )
    out_specs = [ANY] * 7 + [VMEM] * 2 + [ANY] * 7
    wide = max(model, hidden)
    scratch = [
        vb(2, rows, half),
        vb(2, rows, half),
        vb(2, rows, half),
        vb(2, rows, half),
        vb(2, rows, hidden_half),
        vb(2, rows, hidden_half),
        vb(rows, hidden_half),
        vb(rows, hidden_half),
        vb(2, wide, TILE),
        vb(2, max(TILE, 2 * width), wide),
        vb(line, *shares[0]),
        vb(line, *shares[1]),
        vb(line, *shares[2]),
        vb(line, *shares[3]),
        vb(*shares[0]),
        vb(*shares[1]),
        vb(*shares[2]),
        vb(*shares[3]),
        vb(3, 2, blk, model),
        vb(3, tp_steps + 1, blk, model),
        vb(2, 2, blk, 2 * width),
        vb(2, 2, blk, 2 * width),
        vb(2, 2, blk, 2 * width),
        vb(2, 2, blk, width),
        vb(2, blk, width),
        vf(2, own_heads, 2, pair),
        vf(line, 2, own_heads, 2, pair),
        vb(2, 2, blk, 3 * width),
        vb(2, blk, 3 * width),
        vf(pair, HD),
        vf(pair, HD),
        vf(pair, 1),
        vf(pair, 1),
        dma((2, 2, 2, line)),
        dma((2, 2, line)),
        dma((Y_FIN + 4,)),
        dma((Y_FIN + 4,)),
        dma((3,)),
        dma((3,)),
        dma((4, line)),
        dma((4, line + 1)),
        dma((3, tp_steps + 2)),
        dma((3, tp_steps + 2)),
        dma((line,)),
        dma((line,)),
        dma((13,)),
        dma((2, 2)),
        dma((2,)),
        dma((4,)),
    ]
    return pl.pallas_call(
        functools.partial(middle_kernel, line, n_tp),
        name="middle",
        out_shape=outs,
        in_specs=[ANY] * 9 + [VMEM] * 5,
        out_specs=out_specs,
        scratch_shapes=scratch,
        cost_estimate=pl.CostEstimate(
            flops=30 * rows * model * hidden, transcendentals=rows * hidden, bytes_accessed=8 * w_up.size
        ),
        compiler_params=pltpu.CompilerParams(
            collective_id=0, has_side_effects=True, vmem_limit_bytes=63 * 1024 * 1024
        ),
    )(kv, qg, attn_in, mlp_in, cot_b, w_up, w_down, w_out, w_qkv, b_up, row_pos, col_pos, cosine, sine)


def normalize_back(incoming, unit_field, inv_scale, gain_row):
    unit_grad = incoming * gain_row
    return inv_scale * (
        unit_grad
        - jnp.mean(unit_grad, axis=-1, keepdims=True)
        - unit_field * jnp.mean(unit_grad * unit_field, axis=-1, keepdims=True)
    )


def shards(
    n_ctx,
    n_tp,
    stream_in,
    cotangent,
    ln_gain,
    ln_bias,
    w_qkv,
    b_qkv,
    w_out,
    out_bias,
    w_up,
    b_up,
    w_down,
    block_order,
):
    rows, model = stream_in.shape
    blk = rows // 2
    line = n_ctx // 2
    me = lax.axis_index("ctx")
    place, side = me // 2, me % 2

    numbers = jnp.sort(block_order.reshape(line, 2, 2), axis=2)
    seen = (place + jnp.arange(line)) % line
    sides = jnp.stack([side, 1 - side])
    numbers = jnp.transpose(numbers[seen][:, sides], (2, 0, 1))
    positions = numbers[..., None] * blk + jnp.arange(blk, dtype=jnp.int32)
    row_pos = positions.reshape(2 * line, 1, 2 * blk)
    own_pos = positions[:, 0].reshape(2, 2 * blk)
    col_pos = own_pos[:, :, None]
    own_blocks = lax.dynamic_slice_in_dim(block_order, 2 * me, 2)
    late_first = own_blocks[0] > own_blocks[1]
    order = jnp.stack([late_first, jnp.logical_not(late_first)]).astype(jnp.int32)
    cosine, sine = rope_tables(own_pos)
    cos_here = cosine[:, :blk].reshape(rows, LANES)
    sin_here = sine[:, :blk].reshape(rows, LANES)

    attn_in, mlp_in, cot_b, kv, qg = front(
        order,
        side.reshape(1),
        stream_in,
        cotangent,
        ln_gain,
        ln_bias,
        w_qkv,
        b_qkv,
        w_out,
        cos_here,
        sin_here,
    )
    (down, up, out, qkv, branch, mlp_total, attn_total, grad_bup, grad_bqkv, *_) = middle(
        line,
        n_tp,
        kv,
        qg,
        attn_in,
        mlp_in,
        cot_b,
        w_up,
        w_down,
        w_out,
        w_qkv,
        b_up.reshape(-1, 1, TILE),
        row_pos,
        col_pos,
        cosine,
        sine,
    )

    def stored(value):
        flipped = jnp.concatenate([value[1], value[0]], axis=0)
        straight = value.reshape(rows, model)
        return jnp.where(late_first, flipped, straight).astype(F32)

    row_mean = jnp.mean(stream_in, axis=-1, keepdims=True)
    centred = stream_in - row_mean
    variance = jnp.mean(centred * centred, axis=-1, keepdims=True)
    inv_scale = lax.rsqrt(variance + norm_epsilon)
    unit = centred * inv_scale
    attn_total, mlp_total = stored(attn_total), stored(mlp_total)
    stream_out = stream_in + out_bias + stored(branch)
    grad_in = (
        cotangent
        + normalize_back(attn_total, unit, inv_scale, ln_gain[0])
        + normalize_back(mlp_total, unit, inv_scale, ln_gain[1])
    )
    bias_half = grad_bqkv.reshape(-1)
    nothing = jnp.zeros_like(bias_half)
    parts = [
        jnp.where(
            side == 0,
            jnp.concatenate([bias_half, nothing]),
            jnp.concatenate([nothing, bias_half]),
        ),
        grad_bup.reshape(-1),
        jnp.sum(cotangent, axis=0),
        jnp.sum(attn_total * unit, axis=0),
        jnp.sum(mlp_total * unit, axis=0),
        jnp.sum(attn_total, axis=0),
        jnp.sum(mlp_total, axis=0),
    ]
    small = jnp.concatenate(parts)
    step = 1
    while step < n_ctx:
        small = small + lax.ppermute(small, "ctx", [(i, i ^ step) for i in range(n_ctx)])
        step *= 2
    cuts, at = [], 0
    for part in parts:
        cuts.append(small[at : at + part.shape[0]])
        at += part.shape[0]
    return (
        stream_out,
        grad_in,
        qkv.astype(F32),
        cuts[0],
        out.astype(F32),
        cuts[2],
        up.astype(F32),
        cuts[1],
        down.astype(F32),
        jnp.stack([cuts[3], cuts[4]]),
        jnp.stack([cuts[5], cuts[6]]),
    )


def solution(mesh):
    placed = (
        P("ctx", None),
        P("ctx", None),
        P(),
        P(),
        P(None, "tp"),
        P("tp"),
        P("tp", None),
        P(),
        P(None, "tp"),
        P("tp"),
        P("tp", None),
        P(),
    )
    return jax.shard_map(
        functools.partial(shards, mesh.shape["ctx"], mesh.shape["tp"]),
        mesh=mesh,
        in_specs=placed,
        out_specs=(
            P("ctx", None),
            P("ctx", None),
            P("ctx", "tp"),
            P("tp"),
            P("tp", "ctx"),
            P(),
            P("ctx", "tp"),
            P("tp"),
            P("tp", "ctx"),
            P(),
            P(),
        ),
        check_vma=False,
    )
```

time: 939 us -> 387 us (0.41)
  waiting for transfers between devices: 597 us -> 6.11 us
  Pallas kernels: 0 us -> 328 us
  matrix products: 131 us -> 0 us
  blocking collectives: 99.6 us -> 0 us
  other arithmetic: 56.1 us -> 26.6 us
  local copies, waits for them, and re-layouts: 32.6 us -> 15.7 us
  between operations: 14.8 us -> 2.36 us
    reduce_scatter x4 -> x0, waiting for transfers between devices: 431 us -> none  [the longest x1 148 us: shards(): lax.psum_scatter(grad_up.astype(jnp.bfloat16), 'ctx', scatter_dimension=0...]
    pallas_call x0 -> x2, Pallas kernels: none -> 328 us  [the longest x1 313 us: middle(): pl.pallas_call(functools.partial(middle_kernel, line, n_tp), name='middle...]
    dot_general x18 -> x0, matrix products: 131 us -> none  [the longest x1 13.1 us: shards(): jnp.einsum('hqk,qhd->khd', score_b, query_heads, preferred_element_type=j...]
    all_gather x4 -> x0, waiting for transfers between devices: 109 us -> none  [the longest x1 54.9 us: shards(): value_piece = lax.all_gather(value_b, 'ctx', axis=0, tiled=True)]
    all_gather x2 -> x0, blocking collectives: 62.2 us -> none  [the longest x1 31.1 us: shards(): lax.all_gather(row_dot.T, 'ctx', axis=0, tiled=True)]
    psum x1 -> x0, waiting for transfers between devices: 57.9 us -> none  [shards(): lax.psum(branch_part.astype(jnp.bfloat16), 'tp').astype(jnp.float32)]
    psum x1 -> x0, blocking collectives: 37.5 us -> none  [shards(): lax.psum(grad_bqkv.astype(jnp.bfloat16), 'ctx').astype(jnp.float32)]
    convert_element_type x13 -> x5, other arithmetic: 16.3 us -> 5.27 us  [the longest x1 1.56 us: shards(): up.astype(F32)]
  transfers between devices with their start and end apart: 9 -> 3, of which waited for: 8 -> 2; matrix products, arithmetic and copies ran while one was open for 15% -> 1% of each run, Pallas kernels for 0% -> 0%
where the time goes in v1:
time: 387 us; the launch traced here: 385 us
  Pallas kernels  328 us (85%)
  other arithmetic  26.6 us (7%)
  local copies, waits for them, and re-layouts  15.7 us (4%)
  starting transfers between devices  6.37 us (2%)
  waiting for transfers between devices  6.11 us (2%)
    pallas_call x1, Pallas kernels, middle(): pl.pallas_call(functools.partial(middle_kernel, line, n_tp), name='middle...  313 us
    pallas_call x1, Pallas kernels, front(): pl.pallas_call(front_kernel, name='front', out_shape=outs, grid_spec=pltp...  14.6 us
  transfers between devices with their start and end apart: 3, of which 2 were waited for; matrix products, arithmetic and copies ran while one was open for 1% of the time, Pallas kernels for 0%

profile of v1, /device:TPU:0, one launch (start us, length us, event | category | flops | bytes accessed | tf_op | source)
XLA Modules:
  0.0 384.9 jit_solution(5204361470476554481)
XLA Ops:
  0.8 0.7 reshape.304
  1.7 1.2 sort.15
  4.6 1.4 multiply_sine_fusion
  8.7 1.0 reshape_squeeze.4.col_pos
  10.0 2.1 reduce_sum.99
  12.8 14.6 %front.1 = (bf16[2,384,1024]{2,1,0:T(8,128)(2,1)S(1)}, bf16[2,384,1024]{2,1,0:T(8,128)(2,1)}, bf16[2,384,1024]{2,1,0:T(8,128)(2,1)}, bf16[2,2,192,512]{3,2,1,0:T(8,128)(2,1)S(1)}, bf16[2,2,192,512]{3,2,1,0:T(8,128)(2,1)S(1)}) custom-call(s32[2]{0:T(128)S(1)} %add_convert_fusion.order, s32[1]{0:T(128)} %bitcast.2.side_ref, f32[2,192,2048]{2,1,0:T(8,128)} %bitcast.52, ...), custom_call_target="tpu_custom_call" | custom-call | flops 3221225472 | bytes 22544384 | tf_op jit(solution)/shard_map/front/pallas_call | solution.py:155
  27.4 1.1 copy-done.2
  28.5 0.9 copy-done.3
  29.4 0.9 copy-done.4
  30.3 313.2 %middle.1 = (bf16[2048,256]{1,0:T(8,128)(2,1)}, bf16[256,2048]{1,0:T(8,128)(2,1)}, bf16[512,256]{1,0:T(8,128)(2,1)}, bf16[256,1536]{1,0:T(8,128)(2,1)}, bf16[2,1...) custom-call(bf16[2,2,192,512]{3,2,1,0:T(8,128)(2,1)} %copy-done.3, ...), custom_call_target="tpu_custom_call" | custom-call | flops 48318382080 | bytes 33554432 | tf_op jit(solution)/shard_map/middle/pallas_call | solution.py:1030
  343.5 1.6 slice_bitcast_fusion.3
  346.8 0.9 copy-done.8
  347.6 1.5 convert_reduce_fusion
  350.0 0.8 copy-done.7
  351.3 5.0 %fusion.14 = (f32[2048]{0:T(1024)S(1)}, f32[384]{0:T(512)S(1)}, f32[384]{0:T(512)S(1)}, f32[2048]{0:T(1024)S(1)}, bf16[384,2048]{1,0:T(8,128)(2,1)}, /*index=5*/bf16[384,2048]{1,0:T(8,128)(2,1)}) fusion(f32[384,2048]{1,0:T(8,128)S(1)} %copy-done.5, f32[384]{0:T(512)S(1)} %add_rsqrt_fusion, f32[384]{0:T(512)S(1)} %broadcast_multiply_fusion.4, ...), kind=kLoop, calls=%fused_computation.24 | loop fusion | flops 18869504 | bytes 12621825 | tf_op jit(solution)/shard_map/reduce_sum | solution.py:1152
  356.2 1.3 slice_bitcast_fusion.5
  357.6 7.0 %fusion.20 = (f32[2048]{0:T(1024)S(1)}, f32[384,2048]{1,0:T(8,128)}, f32[384,2048]{1,0:T(8,128)}) fusion(f32[384,2048]{1,0:T(8,128)} %param.13, f32[384]{0:T(512)S(1)} %get-tuple-element.79, f32[384]{0:T(512)S(1)} %div.39, f32[2048]{0:T(1024)S(1)} %bitcast.61, bf16[384,2048]{1,0:T(8,128)(2,1)} %get-tuple-element.53, f32[384]{0:T(512)S(1)} %get-tuple-element.80, ...), kind=kLoop, calls=%fused_computation.77 | loop fusion | flops 19658752 | bytes 18916352 | tf_op jit(solution)/shard_map/reduce_sum | solution.py:1150
  365.3 4.0 %collective-permute-done = f32[13824]{0:T(1024)S(1)} collective-permute-done((f32[13824]{0:T(1024)S(1)}, f32[13824]{0:T(1024)S(1)}, u32[]{:S(2)}, u32[]{:S(2)}) %collective-permute-start) | collective-permute-done | bytes 55328 | tf_op jit(solution)/shard_map/ppermute | solution.py:1159
  369.3 5.7 %collective-permute-start.1 = (f32[13824]{0:T(1024)S(1)}, f32[13824]{0:T(1024)S(1)}, u32[]{:S(2)}, u32[]{:S(2)}) collective-permute-start(f32[13824]{0:T(1024)S(1)} %add.147), channel_id=1, source_target_pairs={{0,8},{4,12},{8,0},{12,4},{16,24},{20,28},{24,16},{28,20},{1,9},{5... | collective-permute-start | bytes 165896 | tf_op jit(solution)/shard_map/ppermute | solution.py:1159
  375.0 2.2 collective-permute-done.1
  377.3 1.6 convert_element_type.52
  378.8 1.5 convert_element_type.53
  380.3 1.3 convert_element_type.50
  381.6 0.8 convert_element_type.51
  (111 shorter events, 10.3 us)
Async XLA Ops:
  0.6 6.0 %copy-start.25 = (s32[16]{0:T(128)S(1)}, s32[16]{0:T(128)}, u32[]{:S(2)}) copy-start(s32[16]{0:T(128)} %param.23) | copy-start | bytes 196
  0.7 8.1 %copy-start.22 = (f32[1536]{0:T(1024)S(1)}, f32[1536]{0:T(1024)}, u32[]{:S(2)}) copy-start(f32[1536]{0:T(1024)} %param.17) | copy-start | bytes 18436
  0.7 9.4 %copy-start = (f32[2,2048]{1,0:T(2,128)S(1)}, f32[2,2048]{1,0:T(2,128)}, u32[]{:S(2)}) copy-start(f32[2,2048]{1,0:T(2,128)} %gain_ref.1) | copy-start | bytes 49156
  6.1 6.7 %copy-start.1 = (f32[2,2048]{1,0:T(2,128)S(1)}, f32[2,2048]{1,0:T(2,128)}, u32[]{:S(2)}) copy-start(f32[2,2048]{1,0:T(2,128)} %bias_ref.1) | copy-start | bytes 49156
  6.3 21.0 %copy-start.17 = (f32[2,384,128]{2,1,0:T(8,128)}, f32[2,384,128]{2,1,0:T(8,128)S(1)}, u32[]{:S(2)}) copy-start(f32[2,384,128]{2,1,0:T(8,128)S(1)} %maximum_maximum_fusion.cosine) | copy-start | bytes 1179652
  6.6 20.7 %copy-start.18 = (f32[2,384,128]{2,1,0:T(8,128)}, f32[2,384,128]{2,1,0:T(8,128)S(1)}, u32[]{:S(2)}) copy-start(f32[2,384,128]{2,1,0:T(8,128)S(1)} %maximum_maximum_fusion.1.sine) | copy-start | bytes 1179652
  27.4 1.1 copy-start.2
  343.5 1.9 copy-start.6
  345.5 1.3 copy-start.13
  345.5 2.1 copy-start.8
  347.6 1.9 copy-start.5
  349.3 1.5 copy-start.7
  349.3 1.9 copy-start.9
  351.3 5.0 %copy-start.14 = (bf16[2,192,2048]{2,1,0:T(8,128)(2,1)S(1)}, bf16[2,192,2048]{2,1,0:T(8,128)(2,1)}, u32[]{:S(2)}) copy-start(bf16[2,192,2048]{2,1,0:T(8,128)(2,1)} %get-tuple-element.33) | copy-start | bytes 4718596
  356.2 1.3 copy-start.24
  356.2 1.4 copy-start.23
  356.2 1.4 copy-start.21
  357.6 19.6 %copy-start.16 = (bf16[256,2048]{1,0:T(8,128)(2,1)S(1)}, bf16[256,2048]{1,0:T(8,128)(2,1)}, u32[]{:S(2)}) copy-start(bf16[256,2048]{1,0:T(8,128)(2,1)} %get-tuple-element.40) | copy-start | bytes 3145732
  364.7 14.2 %copy-start.15 = (bf16[2048,256]{1,0:T(8,128)(2,1)S(1)}, bf16[2048,256]{1,0:T(8,128)(2,1)}, u32[]{:S(2)}) copy-start(bf16[2048,256]{1,0:T(8,128)(2,1)} %get-tuple-element.41) | copy-start | bytes 3145732
  364.7 4.5 %collective-permute-start = (f32[13824]{0:T(1024)S(1)}, f32[13824]{0:T(1024)S(1)}, u32[]{:S(2)}, u32[]{:S(2)}) collective-permute-start(f32[13824]{0:T(1024)S(1)} %constant_dynamic-update-slice_fusion), channel_id=1, source_target_pairs={{0,4},{4,0},{8,12},{12,8},{16,20},{20,16},{24,28},{28,24},{1,5},{5... | collective-permute-start | bytes 165896 | tf_op jit(solution)/shard_map/ppermute | solution.py:1159
  369.3 7.9 %collective-permute-start.1 = (f32[13824]{0:T(1024)S(1)}, f32[13824]{0:T(1024)S(1)}, u32[]{:S(2)}, u32[]{:S(2)}) collective-permute-start(f32[13824]{0:T(1024)S(1)} %add.147), channel_id=1, source_target_pairs={{0,8},{4,12},{8,0},{12,4},{16,24},{20,28},{24,16},{28,20},{1,9},{5... | collective-permute-start | bytes 165896 | tf_op jit(solution)/shard_map/ppermute | solution.py:1159
  377.2 5.3 %collective-permute-start.2 = (f32[13824]{0:T(1024)S(1)}, f32[13824]{0:T(1024)S(1)}, u32[]{:S(2)}, u32[]{:S(2)}) collective-permute-start(f32[13824]{0:T(1024)S(1)} %add.148), channel_id=1, source_target_pairs={{0,16},{4,20},{8,24},{12,28},{16,0},{20,4},{24,8},{28,12},{1,17},{... | collective-permute-start | bytes 165896 | tf_op jit(solution)/shard_map/ppermute | solution.py:1159
  377.3 3.1 copy-start.19
  378.8 2.8 copy-start.20
  (5 other events, 4.9 us)

commit v2 on v1

v2 whole, which is shorter than its diff:
```python
import functools
import math

import jax
import jax.numpy as jnp
import numpy as np
from jax import lax
from jax.experimental import pallas as pl
from jax.experimental.pallas import tpu as pltpu
from jax.sharding import PartitionSpec as P

HD = 256
ROT = 64
LANES = 128
TILE = 256

masked_value = -1e30
norm_epsilon = 1e-05
root_half = 0.7071067811865476
inverse_root_two_pi = 0.3989422804014327

F32 = jnp.float32
BF16 = jnp.bfloat16
MESH = pl.DeviceIdType.MESH
ANY = pl.BlockSpec(memory_space=pl.ANY)
VMEM = pl.BlockSpec(memory_space=pltpu.VMEM)
SMEM = pl.BlockSpec(memory_space=pltpu.SMEM)


def nt(a, b):
    return lax.dot_general(a, b, (((1,), (1,)), ((), ())), preferred_element_type=F32)


def nn(a, b):
    return lax.dot_general(a, b, (((1,), (0,)), ((), ())), preferred_element_type=F32)


def tn(a, b):
    return lax.dot_general(a, b, (((0,), (0,)), ((), ())), preferred_element_type=F32)


def rope_tables(positions):
    half_rot = ROT // 2
    frequency = np.exp(np.arange(half_rot) * (-2.0 * math.log(10000.0) / ROT))
    angles = np.asarray(positions, np.float64)[:, None] * frequency
    table = np.zeros((2, angles.shape[0], LANES), np.float32)
    table[0] = 1.0
    for lo in (0, half_rot):
        table[0, :, lo : lo + half_rot] = np.cos(angles)
        table[1, :, lo : lo + half_rot] = np.sin(angles)
    return table


def turn(first, cosine, sine, sign):
    half_rot = ROT // 2
    scaled = first * sine if sign < 0 else first
    lane = lax.broadcasted_iota(jnp.int32, first.shape, 1)
    down = jnp.where(lane < half_rot, pltpu.roll(scaled, LANES - half_rot, 1), 0.0)
    up = jnp.where(
        jnp.logical_and(lane >= half_rot, lane < ROT), pltpu.roll(scaled, half_rot, 1), 0.0
    )
    if sign < 0:
        return first * cosine + (down - up)
    return first * cosine + (up - down) * sine


DOWN, UP, OUT, QKV = range(4)
(Y_KV, Y_QG, Y_COT, Y_MLP, Y_ATTN, Y_ACT, Y_HID, Y_ATT, Y_GQKV, Y_FIN) = range(10)
BRANCH, MLPB, ATTNB = range(3)
S_GAIN, S_SHIFT, S_OUT, S_UP, S_QKV = 0, 2, 4, 5, 6


def layer_kernel(
    line,
    n_tp,
    order,
    stream_in,
    cotangent,
    w_up,
    w_down,
    w_out,
    w_qkv,
    gain,
    shift,
    b_qkv,
    b_up,
    out_bias,
    block_table,
    row_table,
    down_o,
    up_o,
    out_o,
    qkv_o,
    stream_o,
    grad_o,
    small_o,
    kv_all,
    qg_all,
    rs_down,
    rs_up,
    rs_out,
    rs_qkv,
    attn_far,
    tp_far,
    xbuf,
    cbuf,
    cot,
    cot_far,
    norm,
    norm_far,
    attn,
    act,
    hid,
    act_far,
    hid_far,
    wcol,
    wrow,
    c_down,
    c_up,
    c_out,
    c_qkv,
    stage_down,
    stage_up,
    stage_out,
    stage_qkv,
    tp_part,
    tp_recv,
    kv_own,
    qg_own,
    kv_away,
    qg_away,
    chunk,
    att,
    att_far,
    stats,
    stats_all,
    gqkv,
    gqkv_far,
    acc_a,
    acc_b,
    run_m,
    run_l,
    cosine,
    sine,
    small,
    small_recv,
    ag_s,
    ag_r,
    y_s,
    y_r,
    core_s,
    core_r,
    rs_s,
    rs_r,
    tp_s,
    tp_r,
    st_s,
    st_r,
    sm_s,
    sm_r,
    local,
    wsem,
    csem,
    tsem,
):
    me, tp = lax.axis_index("ctx"), lax.axis_index("tp")
    z, y = me // 2, lax.rem(me, 2)
    core = lax.rem(tp, 2)
    partner = (me + 1 - 2 * y, tp)
    sibling = (me, tp + 1 - 2 * core)
    right, left = (me + 2, tp), (me - 2, tp)
    far_steps = []
    step = 2
    while step < n_tp:
        far_steps.append((me, tp + step - 2 * step * lax.rem(tp // step, 2)))
        step *= 2

    rows = norm.shape[1]
    blk = rows // 2
    half = norm.shape[2]
    hidden_half = act.shape[2]
    own_heads = kv_own.shape[-1] // (2 * HD)
    width = own_heads * HD
    block_cols = 2 * half // line
    scale = HD ** (-0.5)

    def place_of(j):
        return lax.rem(z + j, line) * 2 + y

    barrier = pltpu.get_barrier_semaphore()
    greet = [partner, sibling] + far_steps + [(place_of(j), tp) for j in range(1, line)]
    for device in greet:
        pl.semaphore_signal(barrier, inc=1, device_id=device, device_id_type=MESH)

    def rcopy(src, dst, s, r, device):
        return pltpu.make_async_remote_copy(
            src_ref=src, dst_ref=dst, send_sem=s, recv_sem=r, device_id=device, device_id_type=MESH
        )

    def lcopy(src, dst, sem):
        return pltpu.make_async_copy(src, dst, sem)

    def fin_parts(t):
        c = (c_down, c_up, c_out, c_qkv)[t]
        if t == DOWN:
            dst = down_o.at[pl.ds(pl.multiple_of(y * hidden_half, hidden_half), hidden_half), :]
        elif t == UP:
            dst = up_o.at[:, pl.ds(pl.multiple_of(y * hidden_half, hidden_half), hidden_half)]
        elif t == OUT:
            dst = out_o.at[pl.ds(pl.multiple_of(y * width, width), width), :]
        else:
            dst = qkv_o.at[:, pl.ds(pl.multiple_of(y * 3 * width, 3 * width), 3 * width)]
        return c, dst

    def y_copy(item, t=0):
        if item == Y_KV:
            src, dst = kv_away, kv_own.at[:, 1]
        elif item == Y_QG:
            src, dst = qg_away, qg_own.at[:, 1]
        elif item == Y_COT:
            src, dst = cot.at[core], cot_far.at[core]
        elif item == Y_MLP:
            src, dst = norm.at[core], norm_far.at[core]
        elif item == Y_ATTN:
            src, dst = attn.at[core], attn_far.at[core]
        elif item == Y_ACT:
            src, dst = act.at[1 - y], act_far
        elif item == Y_HID:
            src, dst = hid.at[1 - y], hid_far
        elif item == Y_ATT:
            src, dst = att.at[:, 1], att_far
        elif item == Y_GQKV:
            src, dst = gqkv.at[:, 1], gqkv_far
        else:
            c, dst = fin_parts(t)
            src = c.at[0, 1 - y]
            item = Y_FIN + t
        return rcopy(src, dst, y_s.at[item], y_r.at[item], partner)

    def core_copy(k):
        ref = (cot_far, norm_far, attn_far)[k]
        return rcopy(ref.at[core], ref.at[core], core_s.at[k], core_r.at[k], sibling)

    def pass_on(item, k):
        y_copy(item).wait_recv()
        core_copy(k).start()

    def ag_copy(t, h, to, hop, j_src, j_dst):
        ref = (kv_all, qg_all)[t]
        src = ref.at[:, 2 * j_src + h]
        if isinstance(hop, int) and hop == 1:
            src = (kv_own, qg_own)[t].at[:, h]
        return rcopy(
            src,
            ref.at[:, 2 * j_dst + h],
            ag_s.at[t, h, to, hop],
            ag_r.at[t, h, j_dst],
            (right, left)[to],
        )

    def ag_wait(t, h, hop):
        @pl.when(z >= hop)
        def _():
            ag_copy(t, h, 0, hop, line - hop, line - hop).wait_recv()

        @pl.when(z + hop <= line - 1)
        def _():
            ag_copy(t, h, 1, hop, hop, hop).wait_recv()

    def ag_send_when(hop):
        return (
            jnp.logical_and(z >= hop - 1, z <= line - 2),
            jnp.logical_and(z + hop - 1 <= line - 1, z >= 1),
        )

    def ag_hop(t, h, hop):
        if not (isinstance(hop, int) and hop == 1):
            ag_wait(t, h, hop - 1)
        to_right, to_left = ag_send_when(hop)

        @pl.when(to_right)
        def _():
            ag_copy(t, h, 0, hop, lax.rem(line - hop + 1, line), line - hop).start()

        @pl.when(to_left)
        def _():
            ag_copy(t, h, 1, hop, hop - 1, hop).start()

    def ag_rest(t, h, hop):
        def one(i, _):
            ag_hop(t, h, i)
            return 0

        if hop < line:
            lax.fori_loop(hop, line, one, 0)
        ag_wait(t, h, line - 1)

    def ag_drain(t, h):
        def one(hop, _):
            to_right, to_left = ag_send_when(hop)

            @pl.when(to_right)
            def _():
                ag_copy(t, h, 0, hop, lax.rem(line - hop + 1, line), line - hop).wait_send()

            @pl.when(to_left)
            def _():
                ag_copy(t, h, 1, hop, hop - 1, hop).wait_send()

            return 0

        lax.fori_loop(1, line, one, 0)

    rs = (
        (c_down, rs_down, stage_down),
        (c_up, rs_up, stage_up),
        (c_out, rs_out, stage_out),
        (c_qkv, rs_qkv, stage_qkv),
    )

    def rs_copy(t, j, slot, device):
        c, recv, _ = rs[t]
        return rcopy(c.at[j], recv.at[slot], rs_s.at[t, j], rs_r.at[t, slot], device)

    def rs_take(t, j, slot):
        c, recv, held = rs[t]
        rs_copy(t, j, slot, partner).wait_recv()
        copy = lcopy(recv.at[slot], held, tsem.at[t])
        copy.start()
        copy.wait()
        n = c.shape[2]
        part = min(64, n)

        def add(i, _):
            at = pl.ds(pl.multiple_of(i * part, part), part)
            for s in range(2):
                c[j, s, at, :] = (c[j, s, at, :].astype(F32) + held[s, at, :].astype(F32)).astype(
                    BF16
                )
            return 0

        lax.fori_loop(0, n // part, add, 0)

    def rs_ends(t, hops):
        def one(hop, _):
            @pl.when(z == 0)
            def _():
                rs_copy(t, line - hop, line - hop - 1, right).start()

            @pl.when(z == line - 1)
            def _():
                rs_copy(t, hop, hop + 1, left).start()

            return 0

        lax.fori_loop(*hops, one, 0)

    def rs_step(t, hop):
        jr, jl = line - hop, hop

        @pl.when(jnp.logical_and(hop >= z + 1, z >= 1))
        def _():
            rs_take(t, jr, jr)
            rs_copy(t, jr, jr - 1, right).start()

        @pl.when(jnp.logical_and(hop >= line - z, z <= line - 2))
        def _():
            rs_take(t, jl, jl)
            rs_copy(t, jl, jl + 1, left).start()

    def rs_rest(t, hop):
        def one(i, _):
            rs_step(t, i)
            return 0

        if hop < line:
            lax.fori_loop(hop, line, one, 0)

    def rs_finish(t):
        @pl.when(z >= 1)
        def _():
            rs_take(t, 0, 0)

        @pl.when(z <= line - 2)
        def _():
            rs_take(t, 0, line)

        c, dst = fin_parts(t)
        y_copy(Y_FIN, t).start()
        lcopy(c.at[0, y], dst, local.at[4 + t]).start()

    def rs_drain(t):
        def one(j, _):
            @pl.when(j <= line - 1 - z)
            def _():
                rs_copy(t, j, j - 1, right).wait_send()

            @pl.when(j > line - 1 - z)
            def _():
                rs_copy(t, j, j + 1, left).wait_send()

            return 0

        lax.fori_loop(1, line, one, 0)
        c, dst = fin_parts(t)
        y_copy(Y_FIN, t).wait()
        lcopy(c.at[0, y], dst, local.at[4 + t]).wait()

    last = len(far_steps) + 1

    def tp_copy(i, k):
        part = tp_part.at[i]
        if k == 0:
            src, dst, device = part.at[1 - core], tp_recv.at[i, 0], sibling
        elif k < last:
            src, dst, device = part.at[core], tp_recv.at[i, k], far_steps[k - 1]
        else:
            src, dst, device = part.at[core], tp_far.at[i], sibling
        return rcopy(src, dst, tp_s.at[i, k], tp_r.at[i, k], device)

    def tp_add(i, k):
        part = 64

        def add(n, _):
            at = pl.ds(pl.multiple_of(n * part, part), part)
            tp_part[i, core, at, :] = (
                tp_part[i, core, at, :].astype(F32) + tp_recv[i, k, at, :].astype(F32)
            ).astype(BF16)
            return 0

        lax.fori_loop(0, blk // part, add, 0)

    def tp_next(i, k):
        if k > 1:
            tp_copy(i, k - 1).wait_send()
        tp_copy(i, k - 1).wait_recv()
        tp_add(i, k - 1)
        tp_copy(i, k).start()

    def tp_done(i):
        tp_copy(i, last).wait_recv()
        tp_copy(i, 0).wait_send()

        other = lcopy(tp_far.at[i], tp_part.at[i, 1 - core], local.at[8])
        other.start()
        other.wait()

    def tp_drain(i):
        tp_copy(i, last).wait_send()

    def stream(lo, hi, fetches, body):
        for f in fetches:
            f(lo, lax.rem(lo, 2)).start()

        def one(i, _):
            slot = lax.rem(i, 2)

            @pl.when(i + 1 < hi)
            def _():
                for f in fetches:
                    f(i + 1, 1 - slot).start()

            for f in fetches:
                f(i, slot).wait()
            body(i, slot)
            return 0

        lax.fori_loop(lo, hi, one, 0)

    def col_tile(w):
        def fetch(i, slot):
            at = pl.ds(pl.multiple_of(i * TILE, TILE), TILE)
            return lcopy(w.at[:, at], wcol.at[slot, pl.ds(0, w.shape[0]), :], wsem.at[0, slot])

        return fetch

    def row_tile(w):
        def fetch(i, slot):
            at = pl.ds(pl.multiple_of(i * TILE, TILE), TILE)
            return lcopy(w.at[at, :], wrow.at[slot, pl.ds(0, TILE), pl.ds(0, w.shape[1])], wsem.at[1, slot])

        return fetch

    x_load = lcopy(stream_in, xbuf, local.at[0])
    c_load = lcopy(cotangent, cbuf, local.at[1])
    c_load.start()
    x_load.start()

    def number(place, side, k):
        return order[4 * place + 2 * side + k]

    late = [number(z, s, 0) > number(z, s, 1) for s in (y, 1 - y)]

    def block_number(lh, place, side):
        first, second = number(place, side, 0), number(place, side, 1)
        return jnp.minimum(first, second) if lh == 0 else jnp.maximum(first, second)

    for lh in range(2):
        for h in range(2):
            at_block = block_table[:, pl.ds(block_number(lh, z, (y, 1 - y)[h]), 1), :]
            cb, sb = at_block[0], at_block[1]
            ci, si = row_table[0], row_table[1]
            cosine[lh, h] = cb * ci - sb * si
            sine[lh, h] = sb * ci + cb * si

    def by_order(h, first, second):
        return jnp.where(late[h], second, first), jnp.where(late[h], first, second)

    small[...] = jnp.zeros(small.shape, F32)
    model = 2 * half
    chunk_rows = 64
    c_load.wait()

    def cast(i, _):
        at = pl.ds(pl.multiple_of(i * chunk_rows, chunk_rows), chunk_rows)
        c = cbuf[at, :]
        small[S_OUT : S_OUT + 1, :model] += jnp.sum(c, axis=0, keepdims=True)
        c = c.astype(BF16)
        cot[0, at, :] = c[:, :half]
        cot[1, at, :] = c[:, half:]
        return 0

    lax.fori_loop(0, rows // chunk_rows, cast, 0)
    pl.semaphore_wait(barrier, len(greet))
    y_copy(Y_COT).start()

    x_load.wait()

    def unit_of(at):
        x = xbuf[at, :]
        centred = x - jnp.mean(x, axis=-1, keepdims=True)
        variance = jnp.mean(centred * centred, axis=-1, keepdims=True)
        inv_scale = lax.rsqrt(variance + norm_epsilon)
        return centred * inv_scale, inv_scale

    def norms(i, _):
        at = pl.ds(pl.multiple_of(i * chunk_rows, chunk_rows), chunk_rows)
        unit, _ = unit_of(at)
        for n, ref in ((0, attn), (1, norm)):
            value = (unit * gain[n : n + 1, :] + shift[n : n + 1, :]).astype(BF16)
            ref[0, at, :] = value[:, :half]
            ref[1, at, :] = value[:, half:]
        return 0

    lax.fori_loop(0, rows // chunk_rows, norms, 0)


    def tile_at(i):
        return pl.ds(pl.multiple_of(i * TILE, TILE), TILE)

    def feed_forward(i, slot):
        h = nn(norm[0], wcol[slot, :half, :]) + nn(norm[1], wcol[slot, half : 2 * half, :])
        h = h + b_up[:, tile_at(i)]
        gate = 0.5 * (1.0 + lax.erf(h * root_half))
        slope = gate + h * jnp.exp(-0.5 * h * h) * inverse_root_two_pi
        g = nt(cot[0], wrow[slot, :TILE, :half]) + nt(cot[1], wrow[slot, :TILE, half : 2 * half])
        g = g * slope
        small[S_UP : S_UP + 1, tile_at(i)] = jnp.sum(g, axis=0, keepdims=True)
        at = pl.ds(pl.multiple_of(lax.rem(i * TILE, hidden_half), TILE), TILE)
        which = i * TILE // hidden_half
        act[which, :, at] = (h * gate).astype(BF16)
        hid[which, :, at] = g.astype(BF16)

    stream(0, 2 * hidden_half // TILE, (col_tile(w_up), row_tile(w_down)), feed_forward)
    y_copy(Y_ACT).start()


    def project(at, slot, place):
        value = nn(attn[0], wcol[slot, :half, :]) + nn(attn[1], wcol[slot, half : 2 * half, :])
        value = value + b_qkv[:, at]
        pieces = by_order(0, value[:blk], value[blk:])
        for lh in range(2):
            first, rest = pieces[lh][:, :LANES], pieces[lh][:, LANES:]
            place(lh, first, rest)

    def put(refs, which, lh, at, value):
        mine, away = refs

        @pl.when(which == 0)
        def _():
            mine[lh, 0, :, at] = value

        @pl.when(which == 1)
        def _():
            away[lh, :, at] = value

    def kv_index(i):
        which = 1 - i // (2 * own_heads)
        k, kind = lax.rem(i, 2 * own_heads) // 2, 1 + lax.rem(i, 2)
        head = jnp.where(which == 0, y, 1 - y) * own_heads + k
        return which, k, kind, 3 * head + kind

    def q_index(i):
        which = 1 - i // own_heads
        k = lax.rem(i, own_heads)
        head = jnp.where(which == 0, y, 1 - y) * own_heads + k
        return which, k, 3 * head, head

    def fetch_by(w, index):
        def fetch(i, slot):
            return lcopy(w.at[:, tile_at(index(i))], wcol.at[slot, pl.ds(0, w.shape[0]), :], wsem.at[0, slot])

        return fetch

    def lanes_at(start, n):
        return pl.ds(pl.multiple_of(start, LANES), n)

    def keys_values(i, slot):
        which, k, kind, tile = kv_index(i)
        base = jnp.where(kind == 1, 0, width) + k * HD

        def place(lh, first, rest):
            turned = turn(first, cosine[lh, 0], sine[lh, 0], 1)
            first = jnp.where(kind == 1, turned, first).astype(BF16)
            put((kv_own, kv_away), which, lh, lanes_at(base, LANES), first)
            put((kv_own, kv_away), which, lh, lanes_at(base + LANES, HD - LANES), rest.astype(BF16))

        project(tile_at(tile), slot, place)

    stream(0, 4 * own_heads, (fetch_by(w_qkv, lambda i: kv_index(i)[3]),), keys_values)
    y_copy(Y_KV).start()
    ag_hop(0, 0, 1)
    pass_on(Y_COT, 0)

    w_out_fetch = lcopy(w_out, wrow.at[0, pl.ds(0, w_out.shape[0]), pl.ds(0, model)], wsem.at[1, 0])
    w_out_fetch.start()
    w_out_fetch.wait()

    def queries(i, slot):
        which, k, tile, head = q_index(i)

        def place(lh, first, rest):
            turned = turn(first, cosine[lh, 0], sine[lh, 0], 1).astype(BF16)
            put((qg_own, qg_away), which, lh, lanes_at(k * HD, LANES), turned)
            put((qg_own, qg_away), which, lh, lanes_at(k * HD + LANES, HD - LANES), rest.astype(BF16))

        project(tile_at(tile), slot, place)
        at = pl.ds(pl.multiple_of(head * HD, HD), HD)
        g = nt(cot[0], wrow[0, at, :half]) + nt(cot[1], wrow[0, at, half : 2 * half])
        pieces = by_order(0, g[:blk], g[blk:])
        for lh in range(2):
            put((qg_own, qg_away), which, lh, lanes_at(width + k * HD, HD), pieces[lh].astype(BF16))

    stream(0, 2 * own_heads, (fetch_by(w_qkv, lambda i: q_index(i)[2]),), queries)
    y_copy(Y_QG).start()
    ag_hop(1, 0, 1)
    y_copy(Y_MLP).start()
    y_copy(Y_HID).start()
    y_copy(Y_ATTN).start()
    own_places = [
        lcopy(own.at[:, h], everyone.at[:, h], local.at[2 + 2 * t + h])
        for t, (own, everyone) in enumerate(((kv_own, kv_all), (qg_own, qg_all)))
        for h in range(2)
    ]
    own_places[0].start()
    own_places[2].start()

    def cols_at(ref, j):
        start = lax.rem(z + j, line) * block_cols
        at = pl.ds(pl.multiple_of(lax.rem(start, half), LANES), block_cols)
        return ref[start // half, :, at]

    def split_cols(ref, j, at, value):
        n = value.shape[1] // 2
        ref[j, 0, at, :] = value[:, :n].astype(BF16)
        ref[j, 1, at, :] = value[:, n:].astype(BF16)

    def split_rows(ref, j, at, value):
        n = value.shape[0] // 2
        ref[j, 0, :, at] = value[:n].astype(BF16)
        ref[j, 1, :, at] = value[n:].astype(BF16)

    def in_order(share, first=0, end=line):
        def one(k, _):
            j = jnp.where(lax.rem(k, 2) == 0, line - 1 - k // 2, k // 2 + 1)
            share(jnp.where(k == line - 1, 0, j))
            return 0

        lax.fori_loop(first, end, one, 0)


    def mlp_back(i, slot):
        value = nt(hid[0], wrow[slot, :TILE, :hidden_half]) + nt(
            hid[1], wrow[slot, :TILE, hidden_half : 2 * hidden_half]
        )
        tp_part[MLPB, :, :, tile_at(i)] = value.astype(BF16).reshape(2, blk, TILE)

    model_tiles = model // TILE
    stream(0, model_tiles // 2, (row_tile(w_up),), mlp_back)

    ag_hop(0, 0, 2)
    core_copy(0).wait_recv()
    y_copy(Y_ACT).wait_recv()


    def share_down(j):
        g0, g1 = cols_at(cot, j), cols_at(cot_far, j)

        def one(i, _):
            split_cols(
                c_down, j, tile_at(i), tn(act[y, :, tile_at(i)], g0) + tn(act_far[:, tile_at(i)], g1)
            )
            return 0

        lax.fori_loop(0, hidden_half // TILE, one, 0)

    in_order(share_down, 0, 2)
    rs_ends(DOWN, (1, 2))
    in_order(share_down, 2, line)
    stream(model_tiles // 2, model_tiles, (row_tile(w_up),), mlp_back)
    tp_copy(MLPB, 0).start()

    y_copy(Y_KV).wait_recv()
    ag_hop(0, 1, 1)
    own_places[1].start()
    tp_next(MLPB, 1)
    ag_hop(0, 0, 3)
    y_copy(Y_QG).wait_recv()
    own_places[3].start()
    ag_hop(1, 0, 2)
    pass_on(Y_MLP, 1)
    ag_hop(0, 1, 2)
    ag_hop(1, 1, 1)
    rs_ends(DOWN, (2, line))
    ag_hop(0, 1, 3)
    rs_step(DOWN, 1)
    rs_step(DOWN, 2)
    ag_hop(1, 0, 3)
    ag_hop(1, 1, 2)

    y_copy(Y_HID).wait_recv()
    core_copy(1).wait_recv()

    def share_up(j):
        m0, m1 = cols_at(norm, j), cols_at(norm_far, j)

        def one(i, _):
            split_rows(c_up, j, tile_at(i), tn(m0, hid[y, :, tile_at(i)]) + tn(m1, hid_far[:, tile_at(i)]))
            return 0

        lax.fori_loop(0, hidden_half // TILE, one, 0)

    in_order(share_up)
    tp_next(MLPB, 2)
    ag_rest(0, 0, 4)
    ag_rest(0, 1, 4)
    for copy in own_places:
        copy.wait()

    pair = 2 * blk
    same = lax.broadcasted_iota(jnp.int32, (pair, pair), 0) == lax.broadcasted_iota(
        jnp.int32, (pair, pair), 1
    )

    def positions(lh, place, along):
        shape = (1, pair) if along else (pair, 1)
        at = lax.broadcasted_iota(jnp.int32, shape, along)
        here, there = block_number(lh, place, y), block_number(lh, place, 1 - y)
        return at + jnp.where(at < blk, here * blk, there * blk - blk)

    def piece_positions(lh_start, i, along):
        place = lax.rem(z + i, line)
        early, late_ = positions(0, place, along), positions(1, place, along)
        return jnp.where(i < line, early, late_)

    def piece(t):
        def fetch(i, slot):
            ref = (kv_all, qg_all)[t]
            return lcopy(
                ref.at[i // line, pl.ds(2 * lax.rem(i, line), 2)], chunk.at[slot], csem.at[slot]
            )

        return fetch

    for lh in range(2):
        for head in range(own_heads):
            at_k, at_v = head * HD, width + head * HD
            run_m[...] = jnp.full(run_m.shape, masked_value, F32)
            run_l[...] = jnp.zeros(run_l.shape, F32)
            acc_a[...] = jnp.zeros(acc_a.shape, F32)

            def attend(i, slot):
                k = chunk[slot, :, :, at_k : at_k + HD].reshape(pair, HD)
                v = chunk[slot, :, :, at_v : at_v + HD].reshape(pair, HD)
                q = qg_own[lh, :, :, at_k : at_k + HD].reshape(pair, HD)
                s = nt(q, k) * scale
                seen = piece_positions(lh, i, 1) <= positions(lh, z, 0)
                s = jnp.where(seen, s, masked_value)
                old = run_m[...]
                top = jnp.maximum(old, jnp.max(s, axis=1, keepdims=True))
                p = jnp.exp(s - top)
                fade = jnp.exp(old - top)
                run_m[...] = top
                run_l[...] = run_l[...] * fade + jnp.sum(p, axis=1, keepdims=True)
                acc_a[...] = acc_a[...] * fade + nn(p.astype(BF16), v)

            stream(0, line * (lh + 1), (piece(0),), attend)
            out = (acc_a[...] / run_l[...]).astype(BF16)
            att[lh, :, :, at_k : at_k + HD] = out.reshape(2, blk, HD)
            log_total = run_m[...] + jnp.log(run_l[...])
            g = qg_own[lh, :, :, at_v : at_v + HD].reshape(pair, HD)
            dots = jnp.sum(g.astype(F32) * out.astype(F32), axis=1, keepdims=True)
            stats[lh, head, 0:1, :] = jnp.sum(jnp.where(same, log_total, 0.0), 0, keepdims=True)
            stats[lh, head, 1:2, :] = jnp.sum(jnp.where(same, dots, 0.0), 0, keepdims=True)

    def store_order(ref):
        for h in range(2):
            first, second = by_order(h, ref[0, h], ref[1, h])
            ref[0, h] = first
            ref[1, h] = second

    store_order(att)

    def stat_copy(j):
        return rcopy(
            stats, stats_all.at[line - j], st_s.at[j], st_r.at[line - j], (place_of(j), tp)
        )

    for j in range(1, line):
        stat_copy(j).start()
    y_copy(Y_ATT).start()
    rs_ends(UP, (1, line))
    ag_hop(1, 1, 3)
    rs_step(DOWN, 3) if line > 3 else None


    def undo(value, lh, head, kind):
        at = (3 * head + kind) * HD
        first = value[:, :LANES]
        if kind < 2:
            first = turn(
                first, cosine[lh].reshape(pair, LANES), sine[lh].reshape(pair, LANES), -1
            )
        for lo, hi, part in ((0, LANES, first), (LANES, HD, value[:, LANES:])):
            spot = lanes_at(y * 3 * width + at + lo, hi - lo)
            small[S_QKV : S_QKV + 1, spot] += jnp.sum(part, axis=0, keepdims=True)
            gqkv[lh, :, :, at + lo : at + hi] = part.astype(BF16).reshape(2, blk, hi - lo)

    for lh in range(2):
        for head in range(own_heads):
            at_k, at_v = head * HD, width + head * HD
            run_m[...] = jnp.sum(
                jnp.where(same, stats[lh, head, 0:1, :], 0.0), axis=1, keepdims=True
            )
            run_l[...] = jnp.sum(
                jnp.where(same, stats[lh, head, 1:2, :], 0.0), axis=1, keepdims=True
            )
            acc_a[...] = jnp.zeros(acc_a.shape, F32)

            def back_q(i, slot):
                k = chunk[slot, :, :, at_k : at_k + HD].reshape(pair, HD)
                v = chunk[slot, :, :, at_v : at_v + HD].reshape(pair, HD)
                q = qg_own[lh, :, :, at_k : at_k + HD].reshape(pair, HD)
                g = qg_own[lh, :, :, at_v : at_v + HD].reshape(pair, HD)
                s = nt(q, k) * scale
                seen = piece_positions(lh, i, 1) <= positions(lh, z, 0)
                s = jnp.where(seen, s, masked_value)
                p = jnp.exp(s - run_m[...])
                ds = (p * (nt(g, v) - run_l[...]) * scale).astype(BF16)
                acc_a[...] += nn(ds, k)

            stream(0, line * (lh + 1), (piece(0),), back_q)
            undo(acc_a[...], lh, head, 0)

    ag_rest(1, 0, 4)
    ag_rest(1, 1, 4)
    for j in range(1, line):
        stat_copy(line - j).wait_recv()
    own_stats = lcopy(stats, stats_all.at[0], local.at[0])
    own_stats.start()
    own_stats.wait()

    for lh in range(2):
        for head in range(own_heads):
            at_k, at_v = head * HD, width + head * HD
            acc_a[...] = jnp.zeros(acc_a.shape, F32)
            acc_b[...] = jnp.zeros(acc_b.shape, F32)

            def back_k(i, slot):
                q = chunk[slot, :, :, at_k : at_k + HD].reshape(pair, HD)
                g = chunk[slot, :, :, at_v : at_v + HD].reshape(pair, HD)
                k = kv_own[lh, :, :, at_k : at_k + HD].reshape(pair, HD)
                v = kv_own[lh, :, :, at_v : at_v + HD].reshape(pair, HD)
                stat = stats_all[lax.rem(i, line), i // line, head]
                s = nt(k, q) * scale
                seen = positions(lh, z, 0) <= piece_positions(lh, i, 1)
                s = jnp.where(seen, s, masked_value)
                p = jnp.exp(s - stat[0:1, :])
                ds = (p * (nt(v, g) - stat[1:2, :]) * scale).astype(BF16)
                acc_a[...] += nn(ds, q)
                acc_b[...] += nn(p.astype(BF16), g)

            stream(lh * line, 2 * line, (piece(1),), back_k)
            undo(acc_a[...], lh, head, 1)
            undo(acc_b[...], lh, head, 2)
    store_order(gqkv)
    y_copy(Y_GQKV).start()

    pass_on(Y_ATTN, 2)
    core_copy(2).wait_recv()
    core_copy(1).wait_send()
    far_again = lcopy(attn_far, norm_far, local.at[1])
    far_again.start()
    far_again.wait()


    def share_qkv(j):
        m0, m1 = cols_at(attn, j), cols_at(norm_far, j)

        def one(i, _):
            g0 = gqkv[:, 0, :, tile_at(i)].reshape(rows, TILE)
            g1 = gqkv[:, 1, :, tile_at(i)].reshape(rows, TILE)
            split_rows(c_qkv, j, tile_at(i), tn(m0, g0) + tn(m1, g1))
            return 0

        lax.fori_loop(0, 3 * width // TILE, one, 0)

    in_order(share_qkv)
    rs_step(UP, 1)
    rs_step(UP, 2)

    y_copy(Y_GQKV).wait_recv()

    def attn_back(i, slot):
        own = gqkv[:, 0].reshape(rows, 3 * width)
        far = gqkv_far[...].reshape(rows, 3 * width)
        mine = wrow[slot, :TILE, pl.ds(pl.multiple_of(y * 3 * width, LANES), 3 * width)]
        theirs = wrow[slot, :TILE, pl.ds(pl.multiple_of((1 - y) * 3 * width, LANES), 3 * width)]
        value = nt(own, mine) + nt(far, theirs)
        tp_part[ATTNB, :, :, tile_at(i)] = value.astype(BF16).reshape(2, blk, TILE)

    stream(0, model_tiles, (row_tile(w_qkv),), attn_back)
    tp_copy(ATTNB, 0).start()

    def share_out(j):
        g0, g1 = cols_at(cot, j), cols_at(cot_far, j)

        def one(i, _):
            a0 = att[:, 0, :, tile_at(i)].reshape(rows, TILE)
            a1 = att[:, 1, :, tile_at(i)].reshape(rows, TILE)
            split_cols(c_out, j, tile_at(i), tn(a0, g0) + tn(a1, g1))
            return 0

        lax.fori_loop(0, width // TILE, one, 0)

    in_order(share_out)

    tp_next(ATTNB, 1)
    rs_rest(DOWN, 4 if line > 3 else 3)
    rs_finish(DOWN)

    y_copy(Y_ATT).wait_recv()
    w_out_fetch.start()
    w_out_fetch.wait()

    def branch(i, slot):
        value = nn(act[0], wcol[slot, :hidden_half, :]) + nn(
            act[1], wcol[slot, hidden_half : 2 * hidden_half, :]
        )
        own = att[:, 0].reshape(rows, width)
        far = att_far[...].reshape(rows, width)
        mine = wrow[0, pl.ds(pl.multiple_of(y * width, width), width), tile_at(i)]
        theirs = wrow[0, pl.ds(pl.multiple_of((1 - y) * width, width), width), tile_at(i)]
        value += nn(own, mine) + nn(far, theirs)
        tp_part[BRANCH, :, :, tile_at(i)] = value.astype(BF16).reshape(2, blk, TILE)

    stream(0, model_tiles // 2, (col_tile(w_down),), branch)

    rs_step(UP, 3) if line > 3 else None
    stream(model_tiles // 2, model_tiles, (col_tile(w_down),), branch)

    tp_next(ATTNB, 2)
    tp_done(MLPB)
    tp_done(ATTNB)


    def back_norms(i, _):
        at = pl.ds(pl.multiple_of(i * chunk_rows, chunk_rows), chunk_rows)
        at_part = pl.ds(pl.multiple_of(lax.rem(i * chunk_rows, blk), chunk_rows), chunk_rows)
        which = i * chunk_rows // blk
        unit, inv_scale = unit_of(at)
        total = jnp.zeros((chunk_rows, model), F32)
        for n, part in ((0, ATTNB), (1, MLPB)):
            value = tp_part[part, which, at_part, :].astype(F32)
            small[S_GAIN + n : S_GAIN + n + 1, :model] += jnp.sum(value * unit, 0, keepdims=True)
            small[S_SHIFT + n : S_SHIFT + n + 1, :model] += jnp.sum(value, 0, keepdims=True)
            total = total + value * gain[n : n + 1, :]
        cbuf[at, :] = cbuf[at, :] + inv_scale * (
            total
            - jnp.mean(total, axis=-1, keepdims=True)
            - unit * jnp.mean(total * unit, axis=-1, keepdims=True)
        )
        return 0

    lax.fori_loop(0, rows // chunk_rows, back_norms, 0)
    grad_store = lcopy(cbuf, grad_o, local.at[1])
    grad_store.start()

    small_pair = rcopy(small, small_recv.at[0], sm_s.at[0], sm_r.at[0], partner)
    small_pair.start()
    small_pair.wait()
    small[...] += small_recv[0]

    def small_copy(j):
        return rcopy(
            small, small_recv.at[line - j], sm_s.at[j], sm_r.at[line - j], (place_of(j), tp)
        )

    for j in range(1, line):
        small_copy(j).start()
    rs_ends(QKV, (1, line))
    rs_ends(OUT, (1, line))
    tp_copy(BRANCH, 0).start()
    rs_rest(UP, 4 if line > 3 else 3)
    tp_next(BRANCH, 1)
    rs_finish(UP)
    for j in range(1, line):
        small_copy(line - j).wait_recv()
    for j in range(1, line):
        small_copy(j).wait_send()
    small_recv[0] = small[...]
    small[...] = small_recv[lax.rem(line - z, line)]
    for p in range(1, line):
        small[...] += small_recv[lax.rem(p + line - z, line)]
    small_store = lcopy(small, small_o, local.at[2])
    small_store.start()
    rs_step(QKV, 1)
    rs_step(QKV, 2)
    tp_next(BRANCH, 2)
    tp_done(BRANCH)

    def stream_rows(i, _):
        at = pl.ds(pl.multiple_of(i * chunk_rows, chunk_rows), chunk_rows)
        at_part = pl.ds(pl.multiple_of(lax.rem(i * chunk_rows, blk), chunk_rows), chunk_rows)
        which = i * chunk_rows // blk
        xbuf[at, :] = xbuf[at, :] + out_bias[...] + tp_part[BRANCH, which, at_part, :].astype(F32)
        return 0

    lax.fori_loop(0, rows // chunk_rows, stream_rows, 0)
    stream_store = lcopy(xbuf, stream_o, local.at[0])
    stream_store.start()
    rs_rest(QKV, 3)
    rs_step(OUT, 1)
    rs_step(OUT, 2)
    rs_finish(QKV)
    rs_rest(OUT, 3)
    rs_finish(OUT)

    for t in range(2):
        for h in range(2):
            ag_drain(t, h)
    for item in (Y_KV, Y_QG, Y_COT, Y_MLP, Y_ATTN, Y_ACT, Y_HID, Y_ATT, Y_GQKV):
        y_copy(item).wait_send()
    core_copy(0).wait_send()
    core_copy(2).wait_send()
    for j in range(1, line):
        stat_copy(j).wait_send()
    for i in range(3):
        tp_drain(i)
    grad_store.wait()
    small_store.wait()
    stream_store.wait()
    for t in range(4):
        rs_drain(t)


def layer(line, n_tp, order, stream_in, cotangent, ln_gain, ln_bias, w_qkv, b_qkv, w_out, out_bias, w_up, b_up, w_down):
    rows, model = stream_in.shape
    half, blk = model // 2, rows // 2
    hidden = w_up.shape[1]
    hidden_half = hidden // 2
    width = w_out.shape[0] // 2
    own_heads = width // HD
    part_cols = model // line // 2
    pair = 2 * blk
    tp_steps = 0
    while (2 << tp_steps) < n_tp:
        tp_steps += 1
    small_shape = (8, max(model, hidden, 6 * width))
    shares = (
        (2, hidden_half, part_cols),
        (2, part_cols, hidden_half),
        (2, width, part_cols),
        (2, part_cols, 3 * width),
    )
    b = lambda *s: jax.ShapeDtypeStruct(s, BF16)
    f = lambda *s: jax.ShapeDtypeStruct(s, F32)
    vb = lambda *s: pltpu.VMEM(s, BF16)
    vf = lambda *s: pltpu.VMEM(s, F32)
    dma = pltpu.SemaphoreType.DMA
    outs = (
        b(hidden, part_cols),
        b(part_cols, hidden),
        b(2 * width, part_cols),
        b(part_cols, 6 * width),
        f(rows, model),
        f(rows, model),
        f(*small_shape),
        b(2, 2 * line, blk, 2 * width),
        b(2, 2 * line, blk, 2 * width),
        b(line + 1, *shares[0]),
        b(line + 1, *shares[1]),
        b(line + 1, *shares[2]),
        b(line + 1, *shares[3]),
        b(2, rows, half),
        b(3, blk, model),
    )
    wide = max(model, hidden)
    scratch = (
        [vf(rows, model)] * 2
        + [vb(2, rows, half)] * 5
        + [vb(2, rows, hidden_half)] * 2
        + [vb(rows, hidden_half)] * 2
        + [vb(2, wide, TILE), vb(2, max(TILE, 2 * width), wide)]
        + [vb(line, *s) for s in shares]
        + [vb(*s) for s in shares]
        + [vb(3, 2, blk, model), vb(3, tp_steps + 1, blk, model)]
        + [vb(2, 2, blk, 2 * width)] * 2
        + [vb(2, blk, 2 * width)] * 2
        + [
            vb(2, 2, blk, 2 * width),
            vb(2, 2, blk, width),
            vb(2, blk, width),
            vf(2, own_heads, 2, pair),
            vf(line, 2, own_heads, 2, pair),
            vb(2, 2, blk, 3 * width),
            vb(2, blk, 3 * width),
            vf(pair, HD),
            vf(pair, HD),
            vf(pair, 1),
            vf(pair, 1),
            vf(2, 2, blk, LANES),
            vf(2, 2, blk, LANES),
            vf(*small_shape),
            vf(line, *small_shape),
            dma((2, 2, 2, line)),
            dma((2, 2, line)),
            dma((Y_FIN + 4,)),
            dma((Y_FIN + 4,)),
            dma((3,)),
            dma((3,)),
            dma((4, line)),
            dma((4, line + 1)),
            dma((3, tp_steps + 2)),
            dma((3, tp_steps + 2)),
            dma((line,)),
            dma((line,)),
            dma((line,)),
            dma((line,)),
            dma((9,)),
            dma((2, 2)),
            dma((2,)),
            dma((4,)),
        ]
    )
    blocks = order.shape[0]
    operands = (
        order,
        stream_in,
        cotangent,
        w_up,
        w_down,
        w_out,
        w_qkv,
        ln_gain,
        ln_bias,
        b_qkv.reshape(1, -1),
        b_up.reshape(1, -1),
        out_bias.reshape(1, -1),
        jnp.asarray(rope_tables(np.arange(blocks) * blk)),
        jnp.asarray(rope_tables(np.arange(blk))),
    )
    return pl.pallas_call(
        functools.partial(layer_kernel, line, n_tp),
        name="layer",
        out_shape=outs,
        in_specs=[SMEM] + [ANY] * 6 + [VMEM] * 7,
        out_specs=[ANY] * len(outs),
        scratch_shapes=scratch,
        cost_estimate=pl.CostEstimate(
            flops=40 * rows * model * hidden,
            transcendentals=rows * hidden,
            bytes_accessed=8 * w_up.size,
        ),
        compiler_params=pltpu.CompilerParams(
            collective_id=0, has_side_effects=True, vmem_limit_bytes=67043328
        ),
    )(*operands)


def shards(
    n_ctx,
    n_tp,
    stream_in,
    cotangent,
    ln_gain,
    ln_bias,
    w_qkv,
    b_qkv,
    w_out,
    out_bias,
    w_up,
    b_up,
    w_down,
    block_order,
):
    model, hidden = w_up.shape
    (down, up, out, qkv, stream_out, grad_in, small, *_) = layer(
        n_ctx // 2,
        n_tp,
        block_order,
        stream_in,
        cotangent,
        ln_gain,
        ln_bias,
        w_qkv,
        b_qkv,
        w_out,
        out_bias,
        w_up,
        b_up,
        w_down,
    )
    return (
        stream_out,
        grad_in,
        qkv.astype(F32),
        small[S_QKV, : w_qkv.shape[1]],
        out.astype(F32),
        small[S_OUT, :model],
        up.astype(F32),
        small[S_UP, :hidden],
        down.astype(F32),
        small[S_GAIN : S_GAIN + 2, :model],
        small[S_SHIFT : S_SHIFT + 2, :model],
    )


def solution(mesh):
    placed = (
        P("ctx", None),
        P("ctx", None),
        P(),
        P(),
        P(None, "tp"),
        P("tp"),
        P("tp", None),
        P(),
        P(None, "tp"),
        P("tp"),
        P("tp", None),
        P(),
    )
    return jax.shard_map(
        functools.partial(shards, mesh.shape["ctx"], mesh.shape["tp"]),
        mesh=mesh,
        in_specs=placed,
        out_specs=(
            P("ctx", None),
            P("ctx", None),
            P("ctx", "tp"),
            P("tp"),
            P("tp", "ctx"),
            P(),
            P("ctx", "tp"),
            P("tp"),
            P("tp", "ctx"),
            P(),
            P(),
        ),
        check_vma=False,
    )
```

time: 387 us -> 305 us (0.79)
  Pallas kernels: 328 us -> 284 us
  other arithmetic: 26.6 us -> 7.36 us
  starting transfers between devices: 6.37 us -> 0 us
  waiting for transfers between devices: 6.11 us -> 0 us
  local copies, waits for them, and re-layouts: 15.7 us -> 10.6 us
    pallas_call x2 -> x1, Pallas kernels: 328 us -> 284 us  [layer(): pl.pallas_call(functools.partial(layer_kernel, line, n_tp), name='layer',...]
    reduce_sum x5 -> x0, other arithmetic: 16 us -> none  [the longest x1 7.03 us: shards(): jnp.sum(cotangent, axis=0)]
    ppermute x3 -> x0, starting transfers between devices: 6.37 us -> none  [shards(): lax.ppermute(small, 'ctx', [(i, i ^ step) for i in range(n_ctx)])]
    ppermute x3 -> x0, waiting for transfers between devices: 6.11 us -> none  [shards(): lax.ppermute(small, 'ctx', [(i, i ^ step) for i in range(n_ctx)])]
  transfers between devices with their start and end apart: 3 -> 0, of which waited for: 2 -> 0; matrix products, arithmetic and copies ran while one was open for 1% -> 0% of each run, Pallas kernels for 0% -> 0%
where the time goes in v2:
time: 305 us; the launch traced here: 302 us
  Pallas kernels  284 us (93%)
  local copies, waits for them, and re-layouts  10.6 us (3%)
  other arithmetic  7.36 us (2%)
    pallas_call x1, Pallas kernels, layer(): pl.pallas_call(functools.partial(layer_kernel, line, n_tp), name='layer',...  284 us

profile of v2, /device:TPU:0, one launch (start us, length us, event | category | flops | bytes accessed | tf_op | source)
XLA Modules:
  0.0 302.2 jit_solution(16277070970090745228)
XLA Ops:
  0.6 1.3 reshape.31.b_qkv
  1.9 283.6 %layer.1 = (bf16[2048,256]{1,0:T(8,128)(2,1)}, bf16[256,2048]{1,0:T(8,128)(2,1)}, bf16[512,256]{1,0:T(8,128)(2,1)}, bf16[256,1536]{1,0:T(8,128)(2,1)}, f32[384,2...) custom-call(s32[16]{0:T(128)} %order.1, ...), custom_call_target="tpu_custom_call" | custom-call | flops 64424509440 | bytes 33554432 | tf_op jit(solution)/shard_map/layer/pallas_call | solution.py:1173
  285.6 0.0 copy-start.3
  285.6 1.5 slice_reduce_fusion
  287.1 1.5 fusion.1
  288.6 1.5 fusion
  290.1 0.0 copy-start.2
  290.1 1.9 convert_element_type.13
  292.0 2.5 convert_element_type.12
  294.5 0.0 copy-done.3
  294.5 0.0 copy-start.1
  294.5 1.6 convert_element_type.14
  296.0 0.0 copy-done.2
  296.0 1.5 convert_element_type.15
  297.5 0.0 copy-done.1
  297.5 0.0 copy-start
  297.5 1.7 copy.27
  299.2 1.4 copy-done
  300.5 1.7 copy.28
Async XLA Ops:
  285.6 8.9 %copy-start.3 = (bf16[256,2048]{1,0:T(8,128)(2,1)S(1)}, bf16[256,2048]{1,0:T(8,128)(2,1)}, u32[]{:S(2)}) copy-start(bf16[256,2048]{1,0:T(8,128)(2,1)} %get-tuple-element.23) | copy-start | bytes 3145732
  290.1 5.9 %copy-start.2 = (bf16[2048,256]{1,0:T(8,128)(2,1)S(1)}, bf16[2048,256]{1,0:T(8,128)(2,1)}, u32[]{:S(2)}) copy-start(bf16[2048,256]{1,0:T(8,128)(2,1)} %get-tuple-element.24) | copy-start | bytes 3145732
  294.5 3.0 %copy-start.1 = (f32[384,2048]{1,0:T(8,128)S(1)}, f32[384,2048]{1,0:T(8,128)}, u32[]{:S(2)}) copy-start(f32[384,2048]{1,0:T(8,128)} %get-tuple-element.40) | copy-start | bytes 9437188
  297.5 3.0 %copy-start = (f32[384,2048]{1,0:T(8,128)S(1)}, f32[384,2048]{1,0:T(8,128)}, u32[]{:S(2)}) copy-start(f32[384,2048]{1,0:T(8,128)} %get-tuple-element.41) | copy-start | bytes 9437188

commit v3 on v2

--- a/solution.py
+++ b/solution.py
@@ -102,6 +102,8 @@
     rs_qkv,
     attn_far,
     tp_far,
+    cot_end,
+    act_end,
     xbuf,
     cbuf,
     cot,
@@ -150,6 +152,8 @@
     y_r,
     core_s,
     core_r,
+    x_s,
+    x_r,
     rs_s,
     rs_r,
     tp_s,
@@ -158,6 +162,10 @@
     st_r,
     sm_s,
     sm_r,
+    end_s,
+    end_r,
+    ex_s,
+    ex_r,
     local,
     wsem,
     csem,
@@ -177,6 +185,9 @@
 
     rows = norm.shape[1]
     blk = rows // 2
+    across = n_tp // 2
+    xpos = tp // 2
+    x_others = [(me, lax.rem(tp + 2 * k, n_tp)) for k in range(1, across)]
     half = norm.shape[2]
     hidden_half = act.shape[2]
     own_heads = kv_own.shape[-1] // (2 * HD)
@@ -188,7 +199,7 @@
         return lax.rem(z + j, line) * 2 + y
 
     barrier = pltpu.get_barrier_semaphore()
-    greet = [partner, sibling] + far_steps + [(place_of(j), tp) for j in range(1, line)]
+    greet = [partner, sibling] + x_others + [(place_of(j), tp) for j in range(1, line)]
     for device in greet:
         pl.semaphore_signal(barrier, inc=1, device_id=device, device_id_type=MESH)
 
@@ -212,17 +223,21 @@
             dst = qkv_o.at[:, pl.ds(pl.multiple_of(y * 3 * width, 3 * width), 3 * width)]
         return c, dst
 
+    def part_rows(x):
+        n = rows // across
+        return pl.ds(pl.multiple_of(x * n, n), n)
+
     def y_copy(item, t=0):
         if item == Y_KV:
             src, dst = kv_away, kv_own.at[:, 1]
         elif item == Y_QG:
             src, dst = qg_away, qg_own.at[:, 1]
         elif item == Y_COT:
-            src, dst = cot.at[core], cot_far.at[core]
+            src, dst = cot.at[core, part_rows(xpos)], cot_far.at[core, part_rows(xpos)]
         elif item == Y_MLP:
-            src, dst = norm.at[core], norm_far.at[core]
+            src, dst = norm.at[core, part_rows(xpos)], norm_far.at[core, part_rows(xpos)]
         elif item == Y_ATTN:
-            src, dst = attn.at[core], attn_far.at[core]
+            src, dst = attn.at[core, part_rows(xpos)], attn_far.at[core, part_rows(xpos)]
         elif item == Y_ACT:
             src, dst = act.at[1 - y], act_far
         elif item == Y_HID:
@@ -241,9 +256,92 @@
         ref = (cot_far, norm_far, attn_far)[k]
         return rcopy(ref.at[core], ref.at[core], core_s.at[k], core_r.at[k], sibling)
 
+    def x_copy(k, n):
+        ref = (cot_far, norm_far, attn_far)[k].at[core, part_rows(xpos)]
+        return rcopy(ref, ref, x_s.at[k, n], x_r.at[k, n], x_others[n])
+
+    def x_arrival(k, n):
+        ref = (cot_far, norm_far, attn_far)[k].at[core, part_rows(lax.rem(xpos + across - n - 1, across))]
+        return rcopy(ref, ref, x_s.at[k, n], x_r.at[k, n], x_others[n])
+
+    def pass_x(item, k):
+        y_copy(item).wait_recv()
+        for n in range(across - 1):
+            x_copy(k, n).start()
+
     def pass_on(item, k):
-        y_copy(item).wait_recv()
+        for n in range(across - 1):
+            x_arrival(k, n).wait_recv()
         core_copy(k).start()
+
+    def x_drain(k):
+        for n in range(across - 1):
+            x_copy(k, n).wait_send()
+
+    E_COT, E_COT_FAR, E_ACT, E_ACT_FAR = range(4)
+    next_to_end = jnp.logical_or(z == 1, z == line - 2)
+
+    def end_part(k, x):
+        n = rows // across
+        return cot_end.at[
+            pl.ds(pl.multiple_of(k * rows + x * n, n), n), pl.ds(pl.multiple_of(core * half, half), half)
+        ]
+
+    def end_copy(item, device):
+        if item == E_COT:
+            src, dst = cot.at[core, part_rows(xpos)], end_part(0, xpos)
+        elif item == E_COT_FAR:
+            src, dst = cot_far.at[core, part_rows(xpos)], end_part(1, xpos)
+        elif item == E_ACT:
+            src, dst = act.at[y], act_end.at[pl.ds(0, rows), :]
+        else:
+            src, dst = act_far, act_end.at[pl.ds(rows, rows), :]
+        return rcopy(src, dst, end_s.at[item], end_r.at[item], device)
+
+    def end_x(k, n, arriving):
+        x = lax.rem(xpos + across - n - 1, across) if arriving else xpos
+        ref = end_part(k, x)
+        return rcopy(ref, ref, ex_s.at[k, n], ex_r.at[k, n], x_others[n])
+
+    def end_share(k):
+        ref = cot_end.at[pl.ds(k * rows, rows), pl.ds(pl.multiple_of(core * half, half), half)]
+        return rcopy(ref, ref, end_s.at[4 + k], end_r.at[4 + k], sibling)
+
+    def end_send(item):
+        @pl.when(z == 0)
+        def _():
+            end_copy(item, right).start()
+
+        @pl.when(z == line - 1)
+        def _():
+            end_copy(item, left).start()
+
+    def end_pass_x(k):
+        @pl.when(next_to_end)
+        def _():
+            end_copy(E_COT + k, partner).wait_recv()
+            for n in range(across - 1):
+                end_x(k, n, False).start()
+
+    def end_pass(k):
+        @pl.when(next_to_end)
+        def _():
+            for n in range(across - 1):
+                end_x(k, n, True).wait_recv()
+            end_share(k).start()
+
+    def end_drain():
+        @pl.when(jnp.logical_or(z == 0, z == line - 1))
+        def _():
+            for item in range(4):
+                end_copy(item, partner).wait_send()
+
+        @pl.when(next_to_end)
+        def _():
+            for k in range(2):
+                end_share(k).wait_send()
+                for n in range(across - 1):
+                    end_x(k, n, False).wait_send()
 
     def ag_copy(t, h, to, hop, j_src, j_dst):
         ref = (kv_all, qg_all)[t]
@@ -258,15 +356,6 @@
             (right, left)[to],
         )
 
-    def ag_wait(t, h, hop):
-        @pl.when(z >= hop)
-        def _():
-            ag_copy(t, h, 0, hop, line - hop, line - hop).wait_recv()
-
-        @pl.when(z + hop <= line - 1)
-        def _():
-            ag_copy(t, h, 1, hop, hop, hop).wait_recv()
-
     def ag_send_when(hop):
         return (
             jnp.logical_and(z >= hop - 1, z <= line - 2),
@@ -274,16 +363,19 @@
         )
 
     def ag_hop(t, h, hop):
-        if not (isinstance(hop, int) and hop == 1):
-            ag_wait(t, h, hop - 1)
+        first = isinstance(hop, int) and hop == 1
         to_right, to_left = ag_send_when(hop)
 
         @pl.when(to_right)
         def _():
+            if not first:
+                ag_copy(t, h, 0, hop - 1, line - hop + 1, line - hop + 1).wait_recv()
             ag_copy(t, h, 0, hop, lax.rem(line - hop + 1, line), line - hop).start()
 
         @pl.when(to_left)
         def _():
+            if not first:
+                ag_copy(t, h, 1, hop - 1, hop - 1, hop - 1).wait_recv()
             ag_copy(t, h, 1, hop, hop - 1, hop).start()
 
     def ag_rest(t, h, hop):
@@ -291,9 +383,16 @@
             ag_hop(t, h, i)
             return 0
 
+        def come(i, _):
+            ag_copy(t, h, 0, i, i, i).wait_recv()
+            return 0
+
         if hop < line:
             lax.fori_loop(hop, line, one, 0)
-        ag_wait(t, h, line - 1)
+
+        @pl.when(jnp.logical_or(z == 0, z == line - 1))
+        def _():
+            lax.fori_loop(1, line, come, 0)
 
     def ag_drain(t, h):
         def one(hop, _):
@@ -341,13 +440,18 @@
 
         lax.fori_loop(0, n // part, add, 0)
 
+    def first_from(t):
+        return 2 if t == DOWN else 1
+
     def rs_ends(t, hops):
+        first = first_from(t)
+
         def one(hop, _):
-            @pl.when(z == 0)
+            @pl.when(jnp.logical_and(z == first - 1, hop >= first))
             def _():
                 rs_copy(t, line - hop, line - hop - 1, right).start()
 
-            @pl.when(z == line - 1)
+            @pl.when(jnp.logical_and(z == line - first, hop >= first))
             def _():
                 rs_copy(t, hop, hop + 1, left).start()
 
@@ -357,13 +461,14 @@
 
     def rs_step(t, hop):
         jr, jl = line - hop, hop
-
-        @pl.when(jnp.logical_and(hop >= z + 1, z >= 1))
+        first = first_from(t)
+
+        @pl.when(jnp.logical_and(hop >= z + 1, z >= first))
         def _():
             rs_take(t, jr, jr)
             rs_copy(t, jr, jr - 1, right).start()
 
-        @pl.when(jnp.logical_and(hop >= line - z, z <= line - 2))
+        @pl.when(jnp.logical_and(hop >= line - z, z <= line - 1 - first))
         def _():
             rs_take(t, jl, jl)
             rs_copy(t, jl, jl + 1, left).start()
@@ -377,11 +482,13 @@
             lax.fori_loop(hop, line, one, 0)
 
     def rs_finish(t):
-        @pl.when(z >= 1)
+        first = first_from(t)
+
+        @pl.when(z >= first)
         def _():
             rs_take(t, 0, 0)
 
-        @pl.when(z <= line - 2)
+        @pl.when(z <= line - 1 - first)
         def _():
             rs_take(t, 0, line)
 
@@ -390,12 +497,14 @@
         lcopy(c.at[0, y], dst, local.at[4 + t]).start()
 
     def rs_drain(t):
+        sends = jnp.logical_and(z >= first_from(t) - 1, z <= line - first_from(t))
+
         def one(j, _):
-            @pl.when(j <= line - 1 - z)
+            @pl.when(jnp.logical_and(sends, j <= line - 1 - z))
             def _():
                 rs_copy(t, j, j - 1, right).wait_send()
 
-            @pl.when(j > line - 1 - z)
+            @pl.when(jnp.logical_and(sends, j > line - 1 - z))
             def _():
                 rs_copy(t, j, j + 1, left).wait_send()
 
@@ -523,6 +632,7 @@
     lax.fori_loop(0, rows // chunk_rows, cast, 0)
     pl.semaphore_wait(barrier, len(greet))
     y_copy(Y_COT).start()
+    end_send(E_COT)
 
     x_load.wait()
 
@@ -548,21 +658,31 @@
     def tile_at(i):
         return pl.ds(pl.multiple_of(i * TILE, TILE), TILE)
 
-    def feed_forward(i, slot):
+    def hidden_at(i):
+        at = pl.ds(pl.multiple_of(lax.rem(i * TILE, hidden_half), TILE), TILE)
+        return i * TILE // hidden_half, at
+
+    def activate(i, slot):
         h = nn(norm[0], wcol[slot, :half, :]) + nn(norm[1], wcol[slot, half : 2 * half, :])
         h = h + b_up[:, tile_at(i)]
         gate = 0.5 * (1.0 + lax.erf(h * root_half))
+        which, at = hidden_at(i)
+        act[which, :, at] = (h * gate).astype(BF16)
         slope = gate + h * jnp.exp(-0.5 * h * h) * inverse_root_two_pi
+        hid[which, :, at] = slope.astype(BF16)
+
+    def hidden_back(i, slot):
         g = nt(cot[0], wrow[slot, :TILE, :half]) + nt(cot[1], wrow[slot, :TILE, half : 2 * half])
-        g = g * slope
+        which, at = hidden_at(i)
+        g = g * hid[which, :, at].astype(F32)
         small[S_UP : S_UP + 1, tile_at(i)] = jnp.sum(g, axis=0, keepdims=True)
-        at = pl.ds(pl.multiple_of(lax.rem(i * TILE, hidden_half), TILE), TILE)
-        which = i * TILE // hidden_half
-        act[which, :, at] = (h * gate).astype(BF16)
         hid[which, :, at] = g.astype(BF16)
 
-    stream(0, 2 * hidden_half // TILE, (col_tile(w_up), row_tile(w_down)), feed_forward)
+    hidden_tiles = 2 * hidden_half // TILE
+    stream(0, hidden_tiles, (col_tile(w_up),), activate)
     y_copy(Y_ACT).start()
+    pass_x(Y_COT, 0)
+    end_send(E_COT_FAR)
 
 
     def project(at, slot, place):
@@ -620,7 +740,7 @@
     stream(0, 4 * own_heads, (fetch_by(w_qkv, lambda i: kv_index(i)[3]),), keys_values)
     y_copy(Y_KV).start()
     ag_hop(0, 0, 1)
-    pass_on(Y_COT, 0)
+    end_send(E_ACT)
 
     w_out_fetch = lcopy(w_out, wrow.at[0, pl.ds(0, w_out.shape[0]), pl.ds(0, model)], wsem.at[1, 0])
     w_out_fetch.start()
@@ -645,8 +765,8 @@
     y_copy(Y_QG).start()
     ag_hop(1, 0, 1)
     y_copy(Y_MLP).start()
-    y_copy(Y_HID).start()
-    y_copy(Y_ATTN).start()
+    pass_on(Y_COT, 0)
+    end_pass_x(0)
     own_places = [
         lcopy(own.at[:, h], everyone.at[:, h], local.at[2 + 2 * t + h])
         for t, (own, everyone) in enumerate(((kv_own, kv_all), (qg_own, qg_all)))
@@ -678,6 +798,7 @@
 
         lax.fori_loop(first, end, one, 0)
 
+    stream(0, hidden_tiles // 2, (row_tile(w_down),), hidden_back)
 
     def mlp_back(i, slot):
         value = nt(hid[0], wrow[slot, :TILE, :hidden_half]) + nt(
@@ -686,8 +807,7 @@
         tp_part[MLPB, :, :, tile_at(i)] = value.astype(BF16).reshape(2, blk, TILE)
 
     model_tiles = model // TILE
-    stream(0, model_tiles // 2, (row_tile(w_up),), mlp_back)
-
+    end_pass_x(1)
     ag_hop(0, 0, 2)
     core_copy(0).wait_recv()
     y_copy(Y_ACT).wait_recv()
@@ -704,30 +824,29 @@
 
         lax.fori_loop(0, hidden_half // TILE, one, 0)
 
-    in_order(share_down, 0, 2)
-    rs_ends(DOWN, (1, 2))
-    in_order(share_down, 2, line)
-    stream(model_tiles // 2, model_tiles, (row_tile(w_up),), mlp_back)
-    tp_copy(MLPB, 0).start()
+    in_order(share_down)
+    end_pass(0)
+    stream(hidden_tiles // 2, hidden_tiles, (row_tile(w_down),), hidden_back)
+    y_copy(Y_HID).start()
+    y_copy(Y_ATTN).start()
 
     y_copy(Y_KV).wait_recv()
     ag_hop(0, 1, 1)
+    end_send(E_ACT_FAR)
     own_places[1].start()
-    tp_next(MLPB, 1)
+    end_pass(1)
     ag_hop(0, 0, 3)
     y_copy(Y_QG).wait_recv()
     own_places[3].start()
+    ag_hop(1, 1, 1)
     ag_hop(1, 0, 2)
+    stream(0, model_tiles, (row_tile(w_up),), mlp_back)
+    pass_x(Y_MLP, 1)
+    tp_copy(MLPB, 0).start()
+    ag_hop(0, 1, 2)
+    ag_hop(0, 1, 3)
     pass_on(Y_MLP, 1)
-    ag_hop(0, 1, 2)
-    ag_hop(1, 1, 1)
-    rs_ends(DOWN, (2, line))
-    ag_hop(0, 1, 3)
-    rs_step(DOWN, 1)
-    rs_step(DOWN, 2)
-    ag_hop(1, 0, 3)
-    ag_hop(1, 1, 2)
-
+    tp_next(MLPB, 1)
     y_copy(Y_HID).wait_recv()
     core_copy(1).wait_recv()
 
@@ -741,7 +860,51 @@
         lax.fori_loop(0, hidden_half // TILE, one, 0)
 
     in_order(share_up)
-    tp_next(MLPB, 2)
+    rs_ends(UP, (1, 2))
+    ag_hop(1, 0, 3)
+    ag_hop(1, 1, 2)
+
+
+    @pl.when(next_to_end)
+    def _():
+        for k in range(2):
+            end_share(k).wait_recv()
+        blocks = [
+            lcopy(
+                cot_end.at[pl.ds(k * rows, rows), :],
+                wrow.at[k, pl.ds(0, rows), pl.ds(0, model)],
+                wsem.at[1, k],
+            )
+            for k in range(2)
+        ]
+        for copy in blocks:
+            copy.start()
+        for item in (E_ACT, E_ACT_FAR):
+            end_copy(item, partner).wait_recv()
+        for copy in blocks:
+            copy.wait()
+
+        def add_tile(i, slot):
+            at = tile_at(i)
+
+            def add_block(k, _):
+                j = jnp.where(z == 1, k, lax.rem(k + 2, line))
+                start = pl.multiple_of(lax.rem(z + j, line) * block_cols, LANES)
+                value = tn(wcol[slot, :rows, :], wrow[0, :rows, pl.ds(start, block_cols)]) + tn(
+                    wcol[slot, rows : 2 * rows, :], wrow[1, :rows, pl.ds(start, block_cols)]
+                )
+                n = block_cols // 2
+                for side in range(2):
+                    c_down[j, side, at, :] = (
+                        c_down[j, side, at, :].astype(F32) + value[:, side * n : (side + 1) * n]
+                    ).astype(BF16)
+                return 0
+
+            lax.fori_loop(0, line - 1, add_block, 0)
+
+        stream(0, hidden_half // TILE, (col_tile(act_end),), add_tile)
+
+    rs_ends(DOWN, (1, 3))
     ag_rest(0, 0, 4)
     ag_rest(0, 1, 4)
     for copy in own_places:
@@ -819,9 +982,24 @@
     for j in range(1, line):
         stat_copy(j).start()
     y_copy(Y_ATT).start()
-    rs_ends(UP, (1, line))
+    rs_ends(UP, (2, line))
+    rs_ends(DOWN, (3, line))
+    tp_next(MLPB, 2)
+    pass_x(Y_ATTN, 2)
     ag_hop(1, 1, 3)
-    rs_step(DOWN, 3) if line > 3 else None
+
+    def share_out(j):
+        g0, g1 = cols_at(cot, j), cols_at(cot_far, j)
+
+        def one(i, _):
+            a0 = att[:, 0, :, tile_at(i)].reshape(rows, TILE)
+            a1 = att[:, 1, :, tile_at(i)].reshape(rows, TILE)
+            split_cols(c_out, j, tile_at(i), tn(a0, g0) + tn(a1, g1))
+            return 0
+
+        lax.fori_loop(0, width // TILE, one, 0)
+
+    in_order(share_out)
 
 
     def undo(value, lh, head, kind):
@@ -862,6 +1040,29 @@
             stream(0, line * (lh + 1), (piece(0),), back_q)
             undo(acc_a[...], lh, head, 0)
 
+    rs_step(DOWN, 1)
+    rs_step(DOWN, 2)
+    rs_step(DOWN, 3) if line > 3 else None
+    rs_step(UP, 1)
+    rs_step(UP, 2)
+    y_copy(Y_ATT).wait_recv()
+    w_out_fetch.start()
+    w_out_fetch.wait()
+
+    def branch(i, slot):
+        value = nn(act[0], wcol[slot, :hidden_half, :]) + nn(
+            act[1], wcol[slot, hidden_half : 2 * hidden_half, :]
+        )
+        own = att[:, 0].reshape(rows, width)
+        far = att_far[...].reshape(rows, width)
+        mine = wrow[0, pl.ds(pl.multiple_of(y * width, width), width), tile_at(i)]
+        theirs = wrow[0, pl.ds(pl.multiple_of((1 - y) * width, width), width), tile_at(i)]
+        value += nn(own, mine) + nn(far, theirs)
+        tp_part[BRANCH, :, :, tile_at(i)] = value.astype(BF16).reshape(2, blk, TILE)
+
+    stream(0, model_tiles, (col_tile(w_down),), branch)
+
+    tp_copy(BRANCH, 0).start()
     ag_rest(1, 0, 4)
     ag_rest(1, 1, 4)
     for j in range(1, line):
@@ -893,12 +1094,14 @@
             stream(lh * line, 2 * line, (piece(1),), back_k)
             undo(acc_a[...], lh, head, 1)
             undo(acc_b[...], lh, head, 2)
+    tp_next(BRANCH, 1)
     store_order(gqkv)
     y_copy(Y_GQKV).start()
 
     pass_on(Y_ATTN, 2)
     core_copy(2).wait_recv()
     core_copy(1).wait_send()
+    x_drain(1)
     far_again = lcopy(attn_far, norm_far, local.at[1])
     far_again.start()
     far_again.wait()
@@ -916,8 +1119,9 @@
         lax.fori_loop(0, 3 * width // TILE, one, 0)
 
     in_order(share_qkv)
-    rs_step(UP, 1)
-    rs_step(UP, 2)
+    rs_ends(QKV, (1, line))
+    rs_ends(OUT, (1, line))
+    rs_step(UP, 3) if line > 3 else None
 
     y_copy(Y_GQKV).wait_recv()
 
@@ -931,44 +1135,15 @@
 
     stream(0, model_tiles, (row_tile(w_qkv),), attn_back)
     tp_copy(ATTNB, 0).start()
-
-    def share_out(j):
-        g0, g1 = cols_at(cot, j), cols_at(cot_far, j)
-
-        def one(i, _):
-            a0 = att[:, 0, :, tile_at(i)].reshape(rows, TILE)
-            a1 = att[:, 1, :, tile_at(i)].reshape(rows, TILE)
-            split_cols(c_out, j, tile_at(i), tn(a0, g0) + tn(a1, g1))
-            return 0
-
-        lax.fori_loop(0, width // TILE, one, 0)
-
-    in_order(share_out)
-
+    tp_next(BRANCH, 2)
     tp_next(ATTNB, 1)
     rs_rest(DOWN, 4 if line > 3 else 3)
     rs_finish(DOWN)
 
-    y_copy(Y_ATT).wait_recv()
-    w_out_fetch.start()
-    w_out_fetch.wait()
-
-    def branch(i, slot):
-        value = nn(act[0], wcol[slot, :hidden_half, :]) + nn(
-            act[1], wcol[slot, hidden_half : 2 * hidden_half, :]
-        )
-        own = att[:, 0].reshape(rows, width)
-        far = att_far[...].reshape(rows, width)
-        mine = wrow[0, pl.ds(pl.multiple_of(y * width, width), width), tile_at(i)]
-        theirs = wrow[0, pl.ds(pl.multiple_of((1 - y) * width, width), width), tile_at(i)]
-        value += nn(own, mine) + nn(far, theirs)
-        tp_part[BRANCH, :, :, tile_at(i)] = value.astype(BF16).reshape(2, blk, TILE)
-
-    stream(0, model_tiles // 2, (col_tile(w_down),), branch)
-
-    rs_step(UP, 3) if line > 3 else None
-    stream(model_tiles // 2, model_tiles, (col_tile(w_down),), branch)
-
+    rs_rest(UP, 4 if line > 3 else 3)
+    rs_finish(UP)
+    rs_step(QKV, 1)
+    rs_step(QKV, 2)
     tp_next(ATTNB, 2)
     tp_done(MLPB)
     tp_done(ATTNB)
@@ -1008,12 +1183,24 @@
 
     for j in range(1, line):
         small_copy(j).start()
-    rs_ends(QKV, (1, line))
-    rs_ends(OUT, (1, line))
-    tp_copy(BRANCH, 0).start()
-    rs_rest(UP, 4 if line > 3 else 3)
-    tp_next(BRANCH, 1)
-    rs_finish(UP)
+    rs_rest(QKV, 3)
+    tp_done(BRANCH)
+
+    def stream_rows(i, _):
+        at = pl.ds(pl.multiple_of(i * chunk_rows, chunk_rows), chunk_rows)
+        at_part = pl.ds(pl.multiple_of(lax.rem(i * chunk_rows, blk), chunk_rows), chunk_rows)
+        which = i * chunk_rows // blk
+        xbuf[at, :] = xbuf[at, :] + out_bias[...] + tp_part[BRANCH, which, at_part, :].astype(F32)
+        return 0
+
+    lax.fori_loop(0, rows // chunk_rows, stream_rows, 0)
+    stream_store = lcopy(xbuf, stream_o, local.at[0])
+    stream_store.start()
+    rs_step(OUT, 1)
+    rs_step(OUT, 2)
+    rs_finish(QKV)
+    rs_rest(OUT, 3)
+    rs_finish(OUT)
     for j in range(1, line):
         small_copy(line - j).wait_recv()
     for j in range(1, line):
@@ -1024,27 +1211,6 @@
         small[...] += small_recv[lax.rem(p + line - z, line)]
     small_store = lcopy(small, small_o, local.at[2])
     small_store.start()
-    rs_step(QKV, 1)
-    rs_step(QKV, 2)
-    tp_next(BRANCH, 2)
-    tp_done(BRANCH)
-
-    def stream_rows(i, _):
-        at = pl.ds(pl.multiple_of(i * chunk_rows, chunk_rows), chunk_rows)
-        at_part = pl.ds(pl.multiple_of(lax.rem(i * chunk_rows, blk), chunk_rows), chunk_rows)
-        which = i * chunk_rows // blk
-        xbuf[at, :] = xbuf[at, :] + out_bias[...] + tp_part[BRANCH, which, at_part, :].astype(F32)
-        return 0
-
-    lax.fori_loop(0, rows // chunk_rows, stream_rows, 0)
-    stream_store = lcopy(xbuf, stream_o, local.at[0])
-    stream_store.start()
-    rs_rest(QKV, 3)
-    rs_step(OUT, 1)
-    rs_step(OUT, 2)
-    rs_finish(QKV)
-    rs_rest(OUT, 3)
-    rs_finish(OUT)
 
     for t in range(2):
         for h in range(2):
@@ -1053,6 +1219,8 @@
         y_copy(item).wait_send()
     core_copy(0).wait_send()
     core_copy(2).wait_send()
+    x_drain(0)
+    x_drain(2)
     for j in range(1, line):
         stat_copy(j).wait_send()
     for i in range(3):
@@ -1062,6 +1230,7 @@
     stream_store.wait()
     for t in range(4):
         rs_drain(t)
+    end_drain()
 
 
 def layer(line, n_tp, order, stream_in, cotangent, ln_gain, ln_bias, w_qkv, b_qkv, w_out, out_bias, w_up, b_up, w_down):
@@ -1104,6 +1273,8 @@
         b(line + 1, *shares[3]),
         b(2, rows, half),
         b(3, blk, model),
+        b(2 * rows, model),
+        b(2 * rows, hidden_half),
     )
     wide = max(model, hidden)
     scratch = (
@@ -1139,6 +1310,8 @@
             dma((Y_FIN + 4,)),
             dma((3,)),
             dma((3,)),
+            dma((3, n_tp // 2)),
+            dma((3, n_tp // 2)),
             dma((4, line)),
             dma((4, line + 1)),
             dma((3, tp_steps + 2)),
@@ -1147,6 +1320,10 @@
             dma((line,)),
             dma((line,)),
             dma((line,)),
+            dma((6,)),
+            dma((6,)),
+            dma((2, n_tp // 2)),
+            dma((2, n_tp // 2)),
             dma((9,)),
             dma((2, 2)),
             dma((2,)),

time: 305 us -> 280 us (0.918)
  Pallas kernels: 284 us -> 259 us
    pallas_call x1, Pallas kernels: 284 us -> 259 us  [layer(): pl.pallas_call(functools.partial(layer_kernel, line, n_tp), name='layer',...]
where the time goes in v3:
time: 280 us; the launch traced here: 278 us
  Pallas kernels  259 us (92%)
  local copies, waits for them, and re-layouts  10.6 us (4%)
  other arithmetic  7.36 us (3%)
    pallas_call x1, Pallas kernels, layer(): pl.pallas_call(functools.partial(layer_kernel, line, n_tp), name='layer',...  259 us

profile of v3, /device:TPU:0, one launch (start us, length us, event | category | flops | bytes accessed | tf_op | source)
XLA Modules:
  0.0 277.8 jit_solution(1200913372691315673)
XLA Ops:
  0.6 1.3 reshape.31.b_qkv
  1.9 259.2 %layer.1 = (bf16[2048,256]{1,0:T(8,128)(2,1)}, bf16[256,2048]{1,0:T(8,128)(2,1)}, bf16[512,256]{1,0:T(8,128)(2,1)}, bf16[256,1536]{1,0:T(8,128)(2,1)}, f32[384,2...) custom-call(s32[16]{0:T(128)} %order.1, ...), custom_call_target="tpu_custom_call" | custom-call | flops 64424509440 | bytes 33554432 | tf_op jit(solution)/shard_map/layer/pallas_call | solution.py:1350
  261.2 0.0 copy-start.3
  261.2 1.5 slice_reduce_fusion
  262.7 1.5 fusion.1
  264.2 1.5 fusion
  265.8 0.0 copy-start.2
  265.8 1.9 convert_element_type.13
  267.6 2.5 convert_element_type.12
  270.1 0.0 copy-done.3
  270.1 0.0 copy-start.1
  270.1 1.6 convert_element_type.14
  271.7 0.0 copy-done.2
  271.7 1.5 convert_element_type.15
  273.1 0.0 copy-done.1
  273.1 0.0 copy-start
  273.1 1.7 copy.27
  274.8 1.4 copy-done
  276.2 1.7 copy.28
Async XLA Ops:
  261.2 8.9 %copy-start.3 = (bf16[256,2048]{1,0:T(8,128)(2,1)S(1)}, bf16[256,2048]{1,0:T(8,128)(2,1)}, u32[]{:S(2)}) copy-start(bf16[256,2048]{1,0:T(8,128)(2,1)} %get-tuple-element.23) | copy-start | bytes 3145732
  265.8 5.9 %copy-start.2 = (bf16[2048,256]{1,0:T(8,128)(2,1)S(1)}, bf16[2048,256]{1,0:T(8,128)(2,1)}, u32[]{:S(2)}) copy-start(bf16[2048,256]{1,0:T(8,128)(2,1)} %get-tuple-element.24) | copy-start | bytes 3145732
  270.1 3.0 %copy-start.1 = (f32[384,2048]{1,0:T(8,128)S(1)}, f32[384,2048]{1,0:T(8,128)}, u32[]{:S(2)}) copy-start(f32[384,2048]{1,0:T(8,128)} %get-tuple-element.40) | copy-start | bytes 9437188
  273.1 3.0 %copy-start = (f32[384,2048]{1,0:T(8,128)S(1)}, f32[384,2048]{1,0:T(8,128)}, u32[]{:S(2)}) copy-start(f32[384,2048]{1,0:T(8,128)} %get-tuple-element.41) | copy-start | bytes 9437188

commit v4 on v3

--- a/solution.py
+++ b/solution.py
@@ -145,6 +145,8 @@
     cosine,
     sine,
     small,
+    small_pair,
+    small_sent,
     small_recv,
     ag_s,
     ag_r,
@@ -291,7 +293,7 @@
         if item == E_COT:
             src, dst = cot.at[core, part_rows(xpos)], end_part(0, xpos)
         elif item == E_COT_FAR:
-            src, dst = cot_far.at[core, part_rows(xpos)], end_part(1, xpos)
+            src, dst = end_part(0, xpos), end_part(1, xpos)
         elif item == E_ACT:
             src, dst = act.at[y], act_end.at[pl.ds(0, rows), :]
         else:
@@ -322,6 +324,8 @@
             end_copy(E_COT + k, partner).wait_recv()
             for n in range(across - 1):
                 end_x(k, n, False).start()
+            if k == 0:
+                end_copy(E_COT_FAR, partner).start()
 
     def end_pass(k):
         @pl.when(next_to_end)
@@ -333,11 +337,12 @@
     def end_drain():
         @pl.when(jnp.logical_or(z == 0, z == line - 1))
         def _():
-            for item in range(4):
+            for item in (E_COT, E_ACT, E_ACT_FAR):
                 end_copy(item, partner).wait_send()
 
         @pl.when(next_to_end)
         def _():
+            end_copy(E_COT_FAR, partner).wait_send()
             for k in range(2):
                 end_share(k).wait_send()
                 for n in range(across - 1):
@@ -362,9 +367,11 @@
             jnp.logical_and(z + hop - 1 <= line - 1, z >= 1),
         )
 
-    def ag_hop(t, h, hop):
+    def ag_hop(t, h, hop, only=None):
         first = isinstance(hop, int) and hop == 1
         to_right, to_left = ag_send_when(hop)
+        if only is not None:
+            to_right, to_left = jnp.logical_and(to_right, only), jnp.logical_and(to_left, only)
 
         @pl.when(to_right)
         def _():
@@ -417,14 +424,16 @@
         (c_qkv, rs_qkv, stage_qkv),
     )
 
-    def rs_copy(t, j, slot, device):
+    def rs_copy(t, p, j, slot, device):
         c, recv, _ = rs[t]
-        return rcopy(c.at[j], recv.at[slot], rs_s.at[t, j], rs_r.at[t, slot], device)
-
-    def rs_take(t, j, slot):
+        return rcopy(
+            c.at[j, p], recv.at[slot, p], rs_s.at[t, p, j], rs_r.at[t, p, slot], device
+        )
+
+    def rs_take(t, p, j, slot):
         c, recv, held = rs[t]
-        rs_copy(t, j, slot, partner).wait_recv()
-        copy = lcopy(recv.at[slot], held, tsem.at[t])
+        rs_copy(t, p, j, slot, partner).wait_recv()
+        copy = lcopy(recv.at[slot, p], held.at[p], tsem.at[t])
         copy.start()
         copy.wait()
         n = c.shape[2]
@@ -432,10 +441,7 @@
 
         def add(i, _):
             at = pl.ds(pl.multiple_of(i * part, part), part)
-            for s in range(2):
-                c[j, s, at, :] = (c[j, s, at, :].astype(F32) + held[s, at, :].astype(F32)).astype(
-                    BF16
-                )
+            c[j, p, at, :] = (c[j, p, at, :].astype(F32) + held[p, at, :].astype(F32)).astype(BF16)
             return 0
 
         lax.fori_loop(0, n // part, add, 0)
@@ -443,39 +449,67 @@
     def first_from(t):
         return 2 if t == DOWN else 1
 
-    def rs_ends(t, hops):
+    def rs_ends(t, hops, parts=(0, 1)):
         first = first_from(t)
 
         def one(hop, _):
-            @pl.when(jnp.logical_and(z == first - 1, hop >= first))
-            def _():
-                rs_copy(t, line - hop, line - hop - 1, right).start()
-
-            @pl.when(jnp.logical_and(z == line - first, hop >= first))
-            def _():
-                rs_copy(t, hop, hop + 1, left).start()
+            for p in parts:
+
+                @pl.when(jnp.logical_and(z == first - 1, hop >= first))
+                def _():
+                    rs_copy(t, p, line - hop, line - hop - 1, right).start()
+
+                @pl.when(jnp.logical_and(z == line - first, hop >= first))
+                def _():
+                    rs_copy(t, p, hop, hop + 1, left).start()
 
             return 0
 
         lax.fori_loop(*hops, one, 0)
 
-    def rs_step(t, hop):
-        jr, jl = line - hop, hop
-        first = first_from(t)
-
-        @pl.when(jnp.logical_and(hop >= z + 1, z >= first))
+    near = 2 * z < line
+
+    def halves(step):
+        def one(p, _):
+            step(p)
+            return 0
+
+        lax.fori_loop(0, 2, one, 0)
+
+    def rs_right(t, hop, only):
+        jr, first = line - hop, first_from(t)
+
+        @pl.when(jnp.logical_and(only, jnp.logical_and(hop >= z + 1, z >= first)))
         def _():
-            rs_take(t, jr, jr)
-            rs_copy(t, jr, jr - 1, right).start()
-
-        @pl.when(jnp.logical_and(hop >= line - z, z <= line - 1 - first))
+            def step(p):
+                rs_take(t, p, jr, jr)
+                rs_copy(t, p, jr, jr - 1, right).start()
+
+            halves(step)
+
+    def rs_left(t, hop, only):
+        jl, first = hop, first_from(t)
+
+        @pl.when(jnp.logical_and(only, jnp.logical_and(hop >= line - z, z <= line - 1 - first)))
         def _():
-            rs_take(t, jl, jl)
-            rs_copy(t, jl, jl + 1, left).start()
+            def step(p):
+                rs_take(t, p, jl, jl)
+                rs_copy(t, p, jl, jl + 1, left).start()
+
+            halves(step)
+
+    def rs_cross(t, hop):
+        rs_right(t, hop, near)
+        rs_left(t, hop, jnp.logical_not(near))
+
+    def rs_home(t, hop):
+        rs_right(t, hop, jnp.logical_not(near))
+        rs_left(t, hop, near)
 
     def rs_rest(t, hop):
         def one(i, _):
-            rs_step(t, i)
+            rs_cross(t, i)
+            rs_home(t, i)
             return 0
 
         if hop < line:
@@ -483,30 +517,41 @@
 
     def rs_finish(t):
         first = first_from(t)
-
-        @pl.when(z >= first)
-        def _():
-            rs_take(t, 0, 0)
-
-        @pl.when(z <= line - 1 - first)
-        def _():
-            rs_take(t, 0, line)
-
         c, dst = fin_parts(t)
-        y_copy(Y_FIN, t).start()
+
+        def take(k, _):
+            p = jnp.where(k == 0, 1 - y, y)
+
+            @pl.when(z >= first)
+            def _():
+                rs_take(t, p, 0, 0)
+
+            @pl.when(z <= line - 1 - first)
+            def _():
+                rs_take(t, p, 0, line)
+
+            @pl.when(k == 0)
+            def _():
+                y_copy(Y_FIN, t).start()
+
+            return 0
+
+        lax.fori_loop(0, 2, take, 0)
         lcopy(c.at[0, y], dst, local.at[4 + t]).start()
 
     def rs_drain(t):
         sends = jnp.logical_and(z >= first_from(t) - 1, z <= line - first_from(t))
 
         def one(j, _):
-            @pl.when(jnp.logical_and(sends, j <= line - 1 - z))
-            def _():
-                rs_copy(t, j, j - 1, right).wait_send()
-
-            @pl.when(jnp.logical_and(sends, j > line - 1 - z))
-            def _():
-                rs_copy(t, j, j + 1, left).wait_send()
+            for p in range(2):
+
+                @pl.when(jnp.logical_and(sends, j <= line - 1 - z))
+                def _():
+                    rs_copy(t, p, j, j - 1, right).wait_send()
+
+                @pl.when(jnp.logical_and(sends, j > line - 1 - z))
+                def _():
+                    rs_copy(t, p, j, j + 1, left).wait_send()
 
             return 0
 
@@ -654,7 +699,6 @@
 
     lax.fori_loop(0, rows // chunk_rows, norms, 0)
 
-
     def tile_at(i):
         return pl.ds(pl.multiple_of(i * TILE, TILE), TILE)
 
@@ -679,15 +723,9 @@
         hid[which, :, at] = g.astype(BF16)
 
     hidden_tiles = 2 * hidden_half // TILE
-    stream(0, hidden_tiles, (col_tile(w_up),), activate)
-    y_copy(Y_ACT).start()
-    pass_x(Y_COT, 0)
-    end_send(E_COT_FAR)
-
-
     def project(at, slot, place):
         value = nn(attn[0], wcol[slot, :half, :]) + nn(attn[1], wcol[slot, half : 2 * half, :])
-        value = value + b_qkv[:, at]
+        value = value + b_qkv[at][None, :]
         pieces = by_order(0, value[:blk], value[blk:])
         for lh in range(2):
             first, rest = pieces[lh][:, :LANES], pieces[lh][:, LANES:]
@@ -737,14 +775,7 @@
 
         project(tile_at(tile), slot, place)
 
-    stream(0, 4 * own_heads, (fetch_by(w_qkv, lambda i: kv_index(i)[3]),), keys_values)
-    y_copy(Y_KV).start()
-    ag_hop(0, 0, 1)
-    end_send(E_ACT)
-
     w_out_fetch = lcopy(w_out, wrow.at[0, pl.ds(0, w_out.shape[0]), pl.ds(0, model)], wsem.at[1, 0])
-    w_out_fetch.start()
-    w_out_fetch.wait()
 
     def queries(i, slot):
         which, k, tile, head = q_index(i)
@@ -761,19 +792,11 @@
         for lh in range(2):
             put((qg_own, qg_away), which, lh, lanes_at(width + k * HD, HD), pieces[lh].astype(BF16))
 
-    stream(0, 2 * own_heads, (fetch_by(w_qkv, lambda i: q_index(i)[2]),), queries)
-    y_copy(Y_QG).start()
-    ag_hop(1, 0, 1)
-    y_copy(Y_MLP).start()
-    pass_on(Y_COT, 0)
-    end_pass_x(0)
     own_places = [
         lcopy(own.at[:, h], everyone.at[:, h], local.at[2 + 2 * t + h])
         for t, (own, everyone) in enumerate(((kv_own, kv_all), (qg_own, qg_all)))
         for h in range(2)
     ]
-    own_places[0].start()
-    own_places[2].start()
 
     def cols_at(ref, j):
         start = lax.rem(z + j, line) * block_cols
@@ -798,8 +821,6 @@
 
         lax.fori_loop(first, end, one, 0)
 
-    stream(0, hidden_tiles // 2, (row_tile(w_down),), hidden_back)
-
     def mlp_back(i, slot):
         value = nt(hid[0], wrow[slot, :TILE, :hidden_half]) + nt(
             hid[1], wrow[slot, :TILE, hidden_half : 2 * hidden_half]
@@ -807,11 +828,6 @@
         tp_part[MLPB, :, :, tile_at(i)] = value.astype(BF16).reshape(2, blk, TILE)
 
     model_tiles = model // TILE
-    end_pass_x(1)
-    ag_hop(0, 0, 2)
-    core_copy(0).wait_recv()
-    y_copy(Y_ACT).wait_recv()
-
 
     def share_down(j):
         g0, g1 = cols_at(cot, j), cols_at(cot_far, j)
@@ -824,32 +840,6 @@
 
         lax.fori_loop(0, hidden_half // TILE, one, 0)
 
-    in_order(share_down)
-    end_pass(0)
-    stream(hidden_tiles // 2, hidden_tiles, (row_tile(w_down),), hidden_back)
-    y_copy(Y_HID).start()
-    y_copy(Y_ATTN).start()
-
-    y_copy(Y_KV).wait_recv()
-    ag_hop(0, 1, 1)
-    end_send(E_ACT_FAR)
-    own_places[1].start()
-    end_pass(1)
-    ag_hop(0, 0, 3)
-    y_copy(Y_QG).wait_recv()
-    own_places[3].start()
-    ag_hop(1, 1, 1)
-    ag_hop(1, 0, 2)
-    stream(0, model_tiles, (row_tile(w_up),), mlp_back)
-    pass_x(Y_MLP, 1)
-    tp_copy(MLPB, 0).start()
-    ag_hop(0, 1, 2)
-    ag_hop(0, 1, 3)
-    pass_on(Y_MLP, 1)
-    tp_next(MLPB, 1)
-    y_copy(Y_HID).wait_recv()
-    core_copy(1).wait_recv()
-
     def share_up(j):
         m0, m1 = cols_at(norm, j), cols_at(norm_far, j)
 
@@ -859,56 +849,44 @@
 
         lax.fori_loop(0, hidden_half // TILE, one, 0)
 
-    in_order(share_up)
-    rs_ends(UP, (1, 2))
-    ag_hop(1, 0, 3)
-    ag_hop(1, 1, 2)
-
-
-    @pl.when(next_to_end)
-    def _():
-        for k in range(2):
+    def end_tile(k):
+        def fetch(i, slot):
+            return lcopy(
+                act_end.at[pl.ds(k * rows, rows), tile_at(i)], wcol.at[slot, pl.ds(0, rows), :], wsem.at[0, slot]
+            )
+
+        return fetch
+
+    def add_end_tokens(k):
+        @pl.when(next_to_end)
+        def _():
             end_share(k).wait_recv()
-        blocks = [
-            lcopy(
+            held = lcopy(
                 cot_end.at[pl.ds(k * rows, rows), :],
                 wrow.at[k, pl.ds(0, rows), pl.ds(0, model)],
                 wsem.at[1, k],
             )
-            for k in range(2)
-        ]
-        for copy in blocks:
-            copy.start()
-        for item in (E_ACT, E_ACT_FAR):
-            end_copy(item, partner).wait_recv()
-        for copy in blocks:
-            copy.wait()
-
-        def add_tile(i, slot):
-            at = tile_at(i)
-
-            def add_block(k, _):
-                j = jnp.where(z == 1, k, lax.rem(k + 2, line))
-                start = pl.multiple_of(lax.rem(z + j, line) * block_cols, LANES)
-                value = tn(wcol[slot, :rows, :], wrow[0, :rows, pl.ds(start, block_cols)]) + tn(
-                    wcol[slot, rows : 2 * rows, :], wrow[1, :rows, pl.ds(start, block_cols)]
-                )
-                n = block_cols // 2
-                for side in range(2):
-                    c_down[j, side, at, :] = (
-                        c_down[j, side, at, :].astype(F32) + value[:, side * n : (side + 1) * n]
-                    ).astype(BF16)
-                return 0
-
-            lax.fori_loop(0, line - 1, add_block, 0)
-
-        stream(0, hidden_half // TILE, (col_tile(act_end),), add_tile)
-
-    rs_ends(DOWN, (1, 3))
-    ag_rest(0, 0, 4)
-    ag_rest(0, 1, 4)
-    for copy in own_places:
-        copy.wait()
+            held.start()
+            end_copy(E_ACT + k, partner).wait_recv()
+            held.wait()
+
+            def add_tile(i, slot):
+                at = tile_at(i)
+
+                def add_block(n, _):
+                    j = jnp.where(z == 1, n, lax.rem(n + 2, line))
+                    start = pl.multiple_of(lax.rem(z + j, line) * block_cols, LANES)
+                    value = tn(wcol[slot, :rows, :], wrow[k, :rows, pl.ds(start, block_cols)])
+                    n = block_cols // 2
+                    for p in range(2):
+                        c_down[j, p, at, :] = (
+                            c_down[j, p, at, :].astype(F32) + value[:, p * n : (p + 1) * n]
+                        ).astype(BF16)
+                    return 0
+
+                lax.fori_loop(0, line - 1, add_block, 0)
+
+            stream(0, hidden_half // TILE, (end_tile(k),), add_tile)
 
     pair = 2 * blk
     same = lax.broadcasted_iota(jnp.int32, (pair, pair), 0) == lax.broadcasted_iota(
@@ -935,58 +913,48 @@
 
         return fetch
 
-    for lh in range(2):
-        for head in range(own_heads):
-            at_k, at_v = head * HD, width + head * HD
-            run_m[...] = jnp.full(run_m.shape, masked_value, F32)
-            run_l[...] = jnp.zeros(run_l.shape, F32)
-            acc_a[...] = jnp.zeros(acc_a.shape, F32)
-
-            def attend(i, slot):
-                k = chunk[slot, :, :, at_k : at_k + HD].reshape(pair, HD)
-                v = chunk[slot, :, :, at_v : at_v + HD].reshape(pair, HD)
-                q = qg_own[lh, :, :, at_k : at_k + HD].reshape(pair, HD)
-                s = nt(q, k) * scale
-                seen = piece_positions(lh, i, 1) <= positions(lh, z, 0)
-                s = jnp.where(seen, s, masked_value)
-                old = run_m[...]
-                top = jnp.maximum(old, jnp.max(s, axis=1, keepdims=True))
-                p = jnp.exp(s - top)
-                fade = jnp.exp(old - top)
-                run_m[...] = top
-                run_l[...] = run_l[...] * fade + jnp.sum(p, axis=1, keepdims=True)
-                acc_a[...] = acc_a[...] * fade + nn(p.astype(BF16), v)
-
-            stream(0, line * (lh + 1), (piece(0),), attend)
-            out = (acc_a[...] / run_l[...]).astype(BF16)
-            att[lh, :, :, at_k : at_k + HD] = out.reshape(2, blk, HD)
-            log_total = run_m[...] + jnp.log(run_l[...])
-            g = qg_own[lh, :, :, at_v : at_v + HD].reshape(pair, HD)
-            dots = jnp.sum(g.astype(F32) * out.astype(F32), axis=1, keepdims=True)
-            stats[lh, head, 0:1, :] = jnp.sum(jnp.where(same, log_total, 0.0), 0, keepdims=True)
-            stats[lh, head, 1:2, :] = jnp.sum(jnp.where(same, dots, 0.0), 0, keepdims=True)
-
     def store_order(ref):
         for h in range(2):
             first, second = by_order(h, ref[0, h], ref[1, h])
             ref[0, h] = first
             ref[1, h] = second
 
-    store_order(att)
+    def attend_forward():
+        for lh in range(2):
+            for head in range(own_heads):
+                at_k, at_v = head * HD, width + head * HD
+                run_m[...] = jnp.full(run_m.shape, masked_value, F32)
+                run_l[...] = jnp.zeros(run_l.shape, F32)
+                acc_a[...] = jnp.zeros(acc_a.shape, F32)
+
+                def attend(i, slot):
+                    k = chunk[slot, :, :, at_k : at_k + HD].reshape(pair, HD)
+                    v = chunk[slot, :, :, at_v : at_v + HD].reshape(pair, HD)
+                    q = qg_own[lh, :, :, at_k : at_k + HD].reshape(pair, HD)
+                    s = nt(q, k) * scale
+                    seen = piece_positions(lh, i, 1) <= positions(lh, z, 0)
+                    s = jnp.where(seen, s, masked_value)
+                    old = run_m[...]
+                    top = jnp.maximum(old, jnp.max(s, axis=1, keepdims=True))
+                    p = jnp.exp(s - top)
+                    fade = jnp.exp(old - top)
+                    run_m[...] = top
+                    run_l[...] = run_l[...] * fade + jnp.sum(p, axis=1, keepdims=True)
+                    acc_a[...] = acc_a[...] * fade + nn(p.astype(BF16), v)
+
+                stream(0, line * (lh + 1), (piece(0),), attend)
+                out = (acc_a[...] / run_l[...]).astype(BF16)
+                att[lh, :, :, at_k : at_k + HD] = out.reshape(2, blk, HD)
+                log_total = run_m[...] + jnp.log(run_l[...])
+                g = qg_own[lh, :, :, at_v : at_v + HD].reshape(pair, HD)
+                dots = jnp.sum(g.astype(F32) * out.astype(F32), axis=1, keepdims=True)
+                stats[lh, head, 0:1, :] = jnp.sum(jnp.where(same, log_total, 0.0), 0, keepdims=True)
+                stats[lh, head, 1:2, :] = jnp.sum(jnp.where(same, dots, 0.0), 0, keepdims=True)
 
     def stat_copy(j):
         return rcopy(
             stats, stats_all.at[line - j], st_s.at[j], st_r.at[line - j], (place_of(j), tp)
         )
-
-    for j in range(1, line):
-        stat_copy(j).start()
-    y_copy(Y_ATT).start()
-    rs_ends(UP, (2, line))
-    rs_ends(DOWN, (3, line))
-    tp_next(MLPB, 2)
-    pass_x(Y_ATTN, 2)
-    ag_hop(1, 1, 3)
 
     def share_out(j):
         g0, g1 = cols_at(cot, j), cols_at(cot_far, j)
@@ -998,9 +966,6 @@
             return 0
 
         lax.fori_loop(0, width // TILE, one, 0)
-
-    in_order(share_out)
-
 
     def undo(value, lh, head, kind):
         at = (3 * head + kind) * HD
@@ -1014,40 +979,32 @@
             small[S_QKV : S_QKV + 1, spot] += jnp.sum(part, axis=0, keepdims=True)
             gqkv[lh, :, :, at + lo : at + hi] = part.astype(BF16).reshape(2, blk, hi - lo)
 
-    for lh in range(2):
-        for head in range(own_heads):
-            at_k, at_v = head * HD, width + head * HD
-            run_m[...] = jnp.sum(
-                jnp.where(same, stats[lh, head, 0:1, :], 0.0), axis=1, keepdims=True
-            )
-            run_l[...] = jnp.sum(
-                jnp.where(same, stats[lh, head, 1:2, :], 0.0), axis=1, keepdims=True
-            )
-            acc_a[...] = jnp.zeros(acc_a.shape, F32)
-
-            def back_q(i, slot):
-                k = chunk[slot, :, :, at_k : at_k + HD].reshape(pair, HD)
-                v = chunk[slot, :, :, at_v : at_v + HD].reshape(pair, HD)
-                q = qg_own[lh, :, :, at_k : at_k + HD].reshape(pair, HD)
-                g = qg_own[lh, :, :, at_v : at_v + HD].reshape(pair, HD)
-                s = nt(q, k) * scale
-                seen = piece_positions(lh, i, 1) <= positions(lh, z, 0)
-                s = jnp.where(seen, s, masked_value)
-                p = jnp.exp(s - run_m[...])
-                ds = (p * (nt(g, v) - run_l[...]) * scale).astype(BF16)
-                acc_a[...] += nn(ds, k)
-
-            stream(0, line * (lh + 1), (piece(0),), back_q)
-            undo(acc_a[...], lh, head, 0)
-
-    rs_step(DOWN, 1)
-    rs_step(DOWN, 2)
-    rs_step(DOWN, 3) if line > 3 else None
-    rs_step(UP, 1)
-    rs_step(UP, 2)
-    y_copy(Y_ATT).wait_recv()
-    w_out_fetch.start()
-    w_out_fetch.wait()
+    def attend_back_queries():
+        for lh in range(2):
+            for head in range(own_heads):
+                at_k, at_v = head * HD, width + head * HD
+                run_m[...] = jnp.sum(
+                    jnp.where(same, stats[lh, head, 0:1, :], 0.0), axis=1, keepdims=True
+                )
+                run_l[...] = jnp.sum(
+                    jnp.where(same, stats[lh, head, 1:2, :], 0.0), axis=1, keepdims=True
+                )
+                acc_a[...] = jnp.zeros(acc_a.shape, F32)
+
+                def back_q(i, slot):
+                    k = chunk[slot, :, :, at_k : at_k + HD].reshape(pair, HD)
+                    v = chunk[slot, :, :, at_v : at_v + HD].reshape(pair, HD)
+                    q = qg_own[lh, :, :, at_k : at_k + HD].reshape(pair, HD)
+                    g = qg_own[lh, :, :, at_v : at_v + HD].reshape(pair, HD)
+                    s = nt(q, k) * scale
+                    seen = piece_positions(lh, i, 1) <= positions(lh, z, 0)
+                    s = jnp.where(seen, s, masked_value)
+                    p = jnp.exp(s - run_m[...])
+                    ds = (p * (nt(g, v) - run_l[...]) * scale).astype(BF16)
+                    acc_a[...] += nn(ds, k)
+
+                stream(0, line * (lh + 1), (piece(0),), back_q)
+                undo(acc_a[...], lh, head, 0)
 
     def branch(i, slot):
         value = nn(act[0], wcol[slot, :hidden_half, :]) + nn(
@@ -1060,52 +1017,30 @@
         value += nn(own, mine) + nn(far, theirs)
         tp_part[BRANCH, :, :, tile_at(i)] = value.astype(BF16).reshape(2, blk, TILE)
 
-    stream(0, model_tiles, (col_tile(w_down),), branch)
-
-    tp_copy(BRANCH, 0).start()
-    ag_rest(1, 0, 4)
-    ag_rest(1, 1, 4)
-    for j in range(1, line):
-        stat_copy(line - j).wait_recv()
-    own_stats = lcopy(stats, stats_all.at[0], local.at[0])
-    own_stats.start()
-    own_stats.wait()
-
-    for lh in range(2):
-        for head in range(own_heads):
-            at_k, at_v = head * HD, width + head * HD
-            acc_a[...] = jnp.zeros(acc_a.shape, F32)
-            acc_b[...] = jnp.zeros(acc_b.shape, F32)
-
-            def back_k(i, slot):
-                q = chunk[slot, :, :, at_k : at_k + HD].reshape(pair, HD)
-                g = chunk[slot, :, :, at_v : at_v + HD].reshape(pair, HD)
-                k = kv_own[lh, :, :, at_k : at_k + HD].reshape(pair, HD)
-                v = kv_own[lh, :, :, at_v : at_v + HD].reshape(pair, HD)
-                stat = stats_all[lax.rem(i, line), i // line, head]
-                s = nt(k, q) * scale
-                seen = positions(lh, z, 0) <= piece_positions(lh, i, 1)
-                s = jnp.where(seen, s, masked_value)
-                p = jnp.exp(s - stat[0:1, :])
-                ds = (p * (nt(v, g) - stat[1:2, :]) * scale).astype(BF16)
-                acc_a[...] += nn(ds, q)
-                acc_b[...] += nn(p.astype(BF16), g)
-
-            stream(lh * line, 2 * line, (piece(1),), back_k)
-            undo(acc_a[...], lh, head, 1)
-            undo(acc_b[...], lh, head, 2)
-    tp_next(BRANCH, 1)
-    store_order(gqkv)
-    y_copy(Y_GQKV).start()
-
-    pass_on(Y_ATTN, 2)
-    core_copy(2).wait_recv()
-    core_copy(1).wait_send()
-    x_drain(1)
-    far_again = lcopy(attn_far, norm_far, local.at[1])
-    far_again.start()
-    far_again.wait()
-
+    def attend_back_keys():
+        for lh in range(2):
+            for head in range(own_heads):
+                at_k, at_v = head * HD, width + head * HD
+                acc_a[...] = jnp.zeros(acc_a.shape, F32)
+                acc_b[...] = jnp.zeros(acc_b.shape, F32)
+
+                def back_k(i, slot):
+                    q = chunk[slot, :, :, at_k : at_k + HD].reshape(pair, HD)
+                    g = chunk[slot, :, :, at_v : at_v + HD].reshape(pair, HD)
+                    k = kv_own[lh, :, :, at_k : at_k + HD].reshape(pair, HD)
+                    v = kv_own[lh, :, :, at_v : at_v + HD].reshape(pair, HD)
+                    stat = stats_all[lax.rem(i, line), i // line, head]
+                    s = nt(k, q) * scale
+                    seen = positions(lh, z, 0) <= piece_positions(lh, i, 1)
+                    s = jnp.where(seen, s, masked_value)
+                    p = jnp.exp(s - stat[0:1, :])
+                    ds = (p * (nt(v, g) - stat[1:2, :]) * scale).astype(BF16)
+                    acc_a[...] += nn(ds, q)
+                    acc_b[...] += nn(p.astype(BF16), g)
+
+                stream(lh * line, 2 * line, (piece(1),), back_k)
+                undo(acc_a[...], lh, head, 1)
+                undo(acc_b[...], lh, head, 2)
 
     def share_qkv(j):
         m0, m1 = cols_at(attn, j), cols_at(norm_far, j)
@@ -1117,13 +1052,6 @@
             return 0
 
         lax.fori_loop(0, 3 * width // TILE, one, 0)
-
-    in_order(share_qkv)
-    rs_ends(QKV, (1, line))
-    rs_ends(OUT, (1, line))
-    rs_step(UP, 3) if line > 3 else None
-
-    y_copy(Y_GQKV).wait_recv()
 
     def attn_back(i, slot):
         own = gqkv[:, 0].reshape(rows, 3 * width)
@@ -1132,22 +1060,6 @@
         theirs = wrow[slot, :TILE, pl.ds(pl.multiple_of((1 - y) * 3 * width, LANES), 3 * width)]
         value = nt(own, mine) + nt(far, theirs)
         tp_part[ATTNB, :, :, tile_at(i)] = value.astype(BF16).reshape(2, blk, TILE)
-
-    stream(0, model_tiles, (row_tile(w_qkv),), attn_back)
-    tp_copy(ATTNB, 0).start()
-    tp_next(BRANCH, 2)
-    tp_next(ATTNB, 1)
-    rs_rest(DOWN, 4 if line > 3 else 3)
-    rs_finish(DOWN)
-
-    rs_rest(UP, 4 if line > 3 else 3)
-    rs_finish(UP)
-    rs_step(QKV, 1)
-    rs_step(QKV, 2)
-    tp_next(ATTNB, 2)
-    tp_done(MLPB)
-    tp_done(ATTNB)
-
 
     def back_norms(i, _):
         at = pl.ds(pl.multiple_of(i * chunk_rows, chunk_rows), chunk_rows)
@@ -1167,24 +1079,10 @@
         )
         return 0
 
-    lax.fori_loop(0, rows // chunk_rows, back_norms, 0)
-    grad_store = lcopy(cbuf, grad_o, local.at[1])
-    grad_store.start()
-
-    small_pair = rcopy(small, small_recv.at[0], sm_s.at[0], sm_r.at[0], partner)
-    small_pair.start()
-    small_pair.wait()
-    small[...] += small_recv[0]
-
     def small_copy(j):
         return rcopy(
-            small, small_recv.at[line - j], sm_s.at[j], sm_r.at[line - j], (place_of(j), tp)
+            small_sent, small_recv.at[line - j], sm_s.at[j], sm_r.at[line - j], (place_of(j), tp)
         )
-
-    for j in range(1, line):
-        small_copy(j).start()
-    rs_rest(QKV, 3)
-    tp_done(BRANCH)
 
     def stream_rows(i, _):
         at = pl.ds(pl.multiple_of(i * chunk_rows, chunk_rows), chunk_rows)
@@ -1193,22 +1091,165 @@
         xbuf[at, :] = xbuf[at, :] + out_bias[...] + tp_part[BRANCH, which, at_part, :].astype(F32)
         return 0
 
+    at_end = jnp.logical_or(z == 0, z == line - 1)
+    stream(0, 4 * own_heads, (fetch_by(w_qkv, lambda i: kv_index(i)[3]),), keys_values)
+    y_copy(Y_KV).start()
+    ag_hop(0, 0, 1)
+    own_places[0].start()
+    w_out_fetch.start()
+    w_out_fetch.wait()
+    stream(0, 2 * own_heads, (fetch_by(w_qkv, lambda i: q_index(i)[2]),), queries)
+    y_copy(Y_QG).start()
+    ag_hop(1, 0, 1)
+    own_places[2].start()
+    pass_x(Y_COT, 0)
+
+    stream(0, hidden_tiles // 2, (col_tile(w_up),), activate)
+    y_copy(Y_KV).wait_recv()
+    ag_hop(0, 1, 1)
+    own_places[1].start()
+    stream(hidden_tiles // 2, hidden_tiles, (col_tile(w_up),), activate)
+    y_copy(Y_ACT).start()
+    y_copy(Y_MLP).start()
+    end_send(E_ACT)
+    pass_on(Y_COT, 0)
+    ag_hop(0, 0, 2)
+    end_pass_x(0)
+    stream(0, hidden_tiles // 2, (row_tile(w_down),), hidden_back)
+    y_copy(Y_QG).wait_recv()
+    own_places[3].start()
+    ag_hop(1, 1, 1, jnp.logical_not(at_end))
+    ag_hop(1, 0, 2)
+    stream(hidden_tiles // 2, hidden_tiles, (row_tile(w_down),), hidden_back)
+    y_copy(Y_HID).start()
+    y_copy(Y_ATTN).start()
+    end_pass(0)
+    stream(0, model_tiles, (row_tile(w_up),), mlp_back)
+    tp_copy(MLPB, 0).start()
+    ag_hop(0, 0, 3)
+    ag_hop(0, 1, 2)
+    core_copy(0).wait_recv()
+    y_copy(Y_ACT).wait_recv()
+    end_send(E_ACT_FAR)
+    ag_hop(1, 1, 1, at_end)
+    in_order(share_down)
+    pass_x(Y_MLP, 1)
+    end_pass_x(1)
+    ag_hop(0, 1, 3)
+    add_end_tokens(0)
+    pass_on(Y_MLP, 1)
+    end_pass(1)
+    ag_hop(1, 0, 3)
+    add_end_tokens(1)
+    rs_ends(DOWN, (1, 3), (0,))
+    ag_hop(1, 1, 2)
+    rs_ends(DOWN, (1, 3), (1,))
+    tp_next(MLPB, 1)
+    y_copy(Y_HID).wait_recv()
+    core_copy(1).wait_recv()
+    in_order(share_up)
+    rs_ends(UP, (1, 2))
+    ag_rest(0, 0, 4)
+    ag_rest(0, 1, 4)
+    for copy in own_places:
+        copy.wait()
+
+    attend_forward()
+    store_order(att)
+    for j in range(1, line):
+        stat_copy(j).start()
+    y_copy(Y_ATT).start()
+    rs_ends(UP, (2, line))
+    rs_ends(DOWN, (3, line))
+    in_order(share_out)
+    small[S_QKV : S_QKV + 1, :] = jnp.zeros((1, small.shape[1]), F32)
+    attend_back_queries()
+    tp_next(MLPB, 2)
+    ag_hop(1, 1, 3)
+    pass_x(Y_ATTN, 2)
+    for hop in range(1, min(line, 4)):
+        rs_cross(DOWN, hop)
+    y_copy(Y_ATT).wait_recv()
+    w_out_fetch.start()
+    w_out_fetch.wait()
+    stream(0, model_tiles, (col_tile(w_down),), branch)
+    tp_copy(BRANCH, 0).start()
+    rs_cross(UP, 1)
+    rs_cross(UP, 2)
+    ag_rest(1, 0, 4)
+    ag_rest(1, 1, 4)
+    for j in range(1, line):
+        stat_copy(line - j).wait_recv()
+    own_stats = lcopy(stats, stats_all.at[0], local.at[0])
+    own_stats.start()
+    own_stats.wait()
+    attend_back_keys()
+    store_order(gqkv)
+    y_copy(Y_GQKV).start()
+    tp_next(BRANCH, 1)
+    pass_on(Y_ATTN, 2)
+    core_copy(2).wait_recv()
+    core_copy(1).wait_send()
+    x_drain(1)
+    far_again = lcopy(attn_far, norm_far, local.at[1])
+    far_again.start()
+    far_again.wait()
+    in_order(share_qkv)
+    rs_ends(QKV, (1, line))
+    rs_ends(OUT, (1, line))
+    for hop in range(1, min(line, 4)):
+        rs_home(DOWN, hop)
+    rs_home(UP, 1)
+    rs_home(UP, 2)
+    y_copy(Y_GQKV).wait_recv()
+    stream(0, model_tiles, (row_tile(w_qkv),), attn_back)
+    tp_copy(ATTNB, 0).start()
+    tp_next(BRANCH, 2)
+    rs_cross(UP, 3) if line > 3 else None
+    tp_next(ATTNB, 1)
+
+    rs_rest(DOWN, 4 if line > 3 else 3)
+    rs_finish(DOWN)
+    tp_done(BRANCH)
+    tp_done(MLPB)
+    rs_home(UP, 3) if line > 3 else None
+    rs_cross(QKV, 1)
+    rs_cross(QKV, 2)
+    tp_next(ATTNB, 2)
+    tp_done(ATTNB)
+    lax.fori_loop(0, rows // chunk_rows, back_norms, 0)
+    grad_store = lcopy(cbuf, grad_o, local.at[1])
+    grad_store.start()
+    rs_cross(QKV, 3) if line > 3 else None
+    pair_copy = rcopy(small, small_pair, sm_s.at[0], sm_r.at[0], partner)
+    pair_copy.start()
+    pair_copy.wait()
+    small_sent[...] = (small[...] + small_pair[...]).astype(BF16)
+    for j in range(1, line):
+        small_copy(j).start()
     lax.fori_loop(0, rows // chunk_rows, stream_rows, 0)
     stream_store = lcopy(xbuf, stream_o, local.at[0])
     stream_store.start()
-    rs_step(OUT, 1)
-    rs_step(OUT, 2)
+    rs_rest(UP, 4 if line > 3 else 3)
+    rs_finish(UP)
+    rs_home(QKV, 1)
+    rs_home(QKV, 2)
+    rs_home(QKV, 3) if line > 3 else None
+    rs_rest(QKV, 4 if line > 3 else 3)
+    rs_cross(OUT, 1)
+    rs_cross(OUT, 2)
+    rs_cross(OUT, 3) if line > 3 else None
     rs_finish(QKV)
-    rs_rest(OUT, 3)
+    for hop in range(1, min(line, 4)):
+        rs_home(OUT, hop)
+    rs_rest(OUT, 4 if line > 3 else 3)
     rs_finish(OUT)
     for j in range(1, line):
         small_copy(line - j).wait_recv()
-    for j in range(1, line):
-        small_copy(j).wait_send()
-    small_recv[0] = small[...]
-    small[...] = small_recv[lax.rem(line - z, line)]
+    small_recv[0] = small_sent[...]
+    small[...] = small_recv[lax.rem(line - z, line)].astype(F32)
     for p in range(1, line):
-        small[...] += small_recv[lax.rem(p + line - z, line)]
+        small[...] += small_recv[lax.rem(p + line - z, line)].astype(F32)
     small_store = lcopy(small, small_o, local.at[2])
     small_store.start()
 
@@ -1223,6 +1264,7 @@
     x_drain(2)
     for j in range(1, line):
         stat_copy(j).wait_send()
+        small_copy(j).wait_send()
     for i in range(3):
         tp_drain(i)
     grad_store.wait()
@@ -1245,7 +1287,7 @@
     tp_steps = 0
     while (2 << tp_steps) < n_tp:
         tp_steps += 1
-    small_shape = (8, max(model, hidden, 6 * width))
+    small_shape = (16, max(model, hidden, 6 * width))
     shares = (
         (2, hidden_half, part_cols),
         (2, part_cols, hidden_half),
@@ -1303,7 +1345,9 @@
             vf(2, 2, blk, LANES),
             vf(2, 2, blk, LANES),
             vf(*small_shape),
-            vf(line, *small_shape),
+            vf(*small_shape),
+            vb(*small_shape),
+            vb(line, *small_shape),
             dma((2, 2, 2, line)),
             dma((2, 2, line)),
             dma((Y_FIN + 4,)),
@@ -1312,8 +1356,8 @@
             dma((3,)),
             dma((3, n_tp // 2)),
             dma((3, n_tp // 2)),
-            dma((4, line)),
-            dma((4, line + 1)),
+            dma((4, 2, line)),
+            dma((4, 2, line + 1)),
             dma((3, tp_steps + 2)),
             dma((3, tp_steps + 2)),
             dma((line,)),
@@ -1341,7 +1385,7 @@
         w_qkv,
         ln_gain,
         ln_bias,
-        b_qkv.reshape(1, -1),
+        b_qkv,
         b_up.reshape(1, -1),
         out_bias.reshape(1, -1),
         jnp.asarray(rope_tables(np.arange(blocks) * blk)),
@@ -1365,6 +1409,75 @@
     )(*operands)
 
 
+def results_kernel(
+    down,
+    up,
+    out,
+    qkv,
+    stream,
+    grad,
+    small,
+    stream_o,
+    grad_o,
+    qkv_o,
+    bqkv_o,
+    out_o,
+    obias_o,
+    up_o,
+    bup_o,
+    down_o,
+    gain_o,
+    shift_o,
+):
+    stream_o[...] = stream[...]
+    grad_o[...] = grad[...]
+    for src, dst in ((qkv, qkv_o), (out, out_o), (up, up_o), (down, down_o)):
+        dst[...] = src[...].astype(F32)
+
+    @pl.when(pl.program_id(0) == 0)
+    def _():
+        bqkv_o[...] = small[S_QKV, : bqkv_o.shape[0]]
+        obias_o[...] = small[S_OUT, : obias_o.shape[0]]
+        bup_o[...] = small[S_UP, : bup_o.shape[0]]
+        gain_o[...] = small[S_GAIN : S_GAIN + 2, : gain_o.shape[1]]
+        shift_o[...] = small[S_SHIFT : S_SHIFT + 2, : shift_o.shape[1]]
+
+
+def results(down, up, out, qkv, stream_out, grad_in, small, model, fused, hidden):
+    steps = 8
+    f = lambda *s: jax.ShapeDtypeStruct(s, F32)
+    rows_of = lambda a: pl.BlockSpec((a.shape[0] // steps,) + a.shape[1:], lambda i: (i, 0))
+    whole = lambda a: pl.BlockSpec(a.shape, lambda i: (0,) * len(a.shape))
+    large = (down, up, out, qkv, stream_out, grad_in)
+    while any(a.shape[0] % (16 * steps) for a in large[:4]):
+        steps //= 2
+    outs = (
+        (f(*stream_out.shape), True),
+        (f(*grad_in.shape), True),
+        (f(*qkv.shape), True),
+        (f(fused), False),
+        (f(*out.shape), True),
+        (f(model), False),
+        (f(*up.shape), True),
+        (f(hidden), False),
+        (f(*down.shape), True),
+        (f(2, model), False),
+        (f(2, model), False),
+    )
+    return pl.pallas_call(
+        results_kernel,
+        name="results",
+        grid=(steps,),
+        out_shape=[o for o, _ in outs],
+        in_specs=[rows_of(a) for a in large] + [whole(small)],
+        out_specs=[rows_of(o) if tall else whole(o) for o, tall in outs],
+        cost_estimate=pl.CostEstimate(
+            flops=down.size, transcendentals=0, bytes_accessed=8 * down.size + 16 * stream_out.size
+        ),
+        compiler_params=pltpu.CompilerParams(vmem_limit_bytes=67043328),
+    )(*large, small)
+
+
 def shards(
     n_ctx,
     n_tp,
@@ -1381,7 +1494,6 @@
     w_down,
     block_order,
 ):
-    model, hidden = w_up.shape
     (down, up, out, qkv, stream_out, grad_in, small, *_) = layer(
         n_ctx // 2,
         n_tp,
@@ -1398,19 +1510,7 @@
         b_up,
         w_down,
     )
-    return (
-        stream_out,
-        grad_in,
-        qkv.astype(F32),
-        small[S_QKV, : w_qkv.shape[1]],
-        out.astype(F32),
-        small[S_OUT, :model],
-        up.astype(F32),
-        small[S_UP, :hidden],
-        down.astype(F32),
-        small[S_GAIN : S_GAIN + 2, :model],
-        small[S_SHIFT : S_SHIFT + 2, :model],
-    )
+    return results(down, up, out, qkv, stream_out, grad_in, small, *w_qkv.shape, w_up.shape[1])
 
 
 def solution(mesh):

time: 280 us -> 265 us (0.946)
  local copies, waits for them, and re-layouts: 10.6 us -> 0 us
  other arithmetic: 7.36 us -> 0 us
    pallas_call x0 -> x1, Pallas kernels: none -> 10.4 us  [results(): pl.pallas_call(results_kernel, name='results', grid=(steps,), out_shape=[...]
    pallas_call x1, Pallas kernels: 259 us -> 251 us  [layer(): pl.pallas_call(functools.partial(layer_kernel, line, n_tp), name='layer',...]
    convert_element_type x4 -> x0, other arithmetic: 7.36 us -> none  [the longest x1 2.46 us: shards(): qkv.astype(F32)]
    unnamed x10 -> x0, local copies, waits for them, and re-layouts: 4.7 us -> none
    slice x3 -> x0, local copies, waits for them, and re-layouts: 4.57 us -> none  [the longest x1 1.53 us: shards(): small[S_SHIFT:S_SHIFT + 2, :model]]
where the time goes in v4:
time: 265 us; the launch traced here: 262 us
  Pallas kernels  261 us (98%)
    pallas_call x1, Pallas kernels, layer(): pl.pallas_call(functools.partial(layer_kernel, line, n_tp), name='layer',...  251 us
    pallas_call x1, Pallas kernels, results(): pl.pallas_call(results_kernel, name='results', grid=(steps,), out_shape=[...  10.4 us

profile of v4, /device:TPU:0, one launch (start us, length us, event | category | flops | bytes accessed | tf_op | source)
XLA Modules:
  0.0 262.3 jit_solution(18374753027883950156)
XLA Ops:
  0.6 251.1 %layer.1 = (bf16[2048,256]{1,0:T(8,128)(2,1)}, bf16[256,2048]{1,0:T(8,128)(2,1)}, bf16[512,256]{1,0:T(8,128)(2,1)}, bf16[256,1536]{1,0:T(8,128)(2,1)}, f32[384,2...) custom-call(s32[16]{0:T(128)} %order.1, ...), custom_call_target="tpu_custom_call" | custom-call | flops 64424509440 | bytes 33554432 | tf_op jit(solution)/shard_map/layer/pallas_call | solution.py:1394
  251.7 10.4 %results.1 = (f32[384,2048]{1,0:T(8,128)}, f32[384,2048]{1,0:T(8,128)}, f32[256,1536]{1,0:T(8,128)}, f32[1536]{0:T(1024)}, f32[512,256]{1,0:T(8,128)}, /*index=5...) custom-call(bf16[2048,256]{1,0:T(8,128)(2,1)} %get-tuple-element.18., ...), custom_call_target="tpu_custom_call" | custom-call | flops 524288 | bytes 16777216 | tf_op jit(solution)/shard_map/results/pallas_call | solution.py:1467

commit v5 on v4

--- a/solution.py
+++ b/solution.py
@@ -280,7 +280,7 @@
         for n in range(across - 1):
             x_copy(k, n).wait_send()
 
-    E_COT, E_COT_FAR, E_ACT, E_ACT_FAR = range(4)
+    E_COT, E_COT_FAR, E_ACT, E_ACT_FAR, E_ACT_LAST = range(5)
     next_to_end = jnp.logical_or(z == 1, z == line - 2)
 
     def end_part(k, x):
@@ -297,7 +297,9 @@
         elif item == E_ACT:
             src, dst = act.at[y], act_end.at[pl.ds(0, rows), :]
         else:
-            src, dst = act_far, act_end.at[pl.ds(rows, rows), :]
+            n = hidden_half // 2
+            part = pl.ds(0 if item == E_ACT_FAR else n, n)
+            src, dst = act_far.at[:, part], act_end.at[pl.ds(rows, rows), part]
         return rcopy(src, dst, end_s.at[item], end_r.at[item], device)
 
     def end_x(k, n, arriving):
@@ -307,7 +309,7 @@
 
     def end_share(k):
         ref = cot_end.at[pl.ds(k * rows, rows), pl.ds(pl.multiple_of(core * half, half), half)]
-        return rcopy(ref, ref, end_s.at[4 + k], end_r.at[4 + k], sibling)
+        return rcopy(ref, ref, end_s.at[5 + k], end_r.at[5 + k], sibling)
 
     def end_send(item):
         @pl.when(z == 0)
@@ -337,7 +339,7 @@
     def end_drain():
         @pl.when(jnp.logical_or(z == 0, z == line - 1))
         def _():
-            for item in (E_COT, E_ACT, E_ACT_FAR):
+            for item in (E_COT, E_ACT, E_ACT_FAR, E_ACT_LAST):
                 end_copy(item, partner).wait_send()
 
         @pl.when(next_to_end)
@@ -424,27 +426,42 @@
         (c_qkv, rs_qkv, stage_qkv),
     )
 
+    def piece_of(ref, t, p):
+        if t != DOWN:
+            return ref.at[p]
+        n = hidden_half // 2
+        return ref.at[:, pl.ds(pl.multiple_of(p * n, n), n), :]
+
     def rs_copy(t, p, j, slot, device):
         c, recv, _ = rs[t]
         return rcopy(
-            c.at[j, p], recv.at[slot, p], rs_s.at[t, p, j], rs_r.at[t, p, slot], device
+            piece_of(c.at[j], t, p), piece_of(recv.at[slot], t, p), rs_s.at[t, p, j], rs_r.at[t, p, slot], device
         )
 
     def rs_take(t, p, j, slot):
         c, recv, held = rs[t]
         rs_copy(t, p, j, slot, partner).wait_recv()
-        copy = lcopy(recv.at[slot, p], held.at[p], tsem.at[t])
+        copy = lcopy(piece_of(recv.at[slot], t, p), piece_of(held, t, p), tsem.at[t])
         copy.start()
         copy.wait()
         n = c.shape[2]
         part = min(64, n)
 
-        def add(i, _):
+        def add(side, i):
             at = pl.ds(pl.multiple_of(i * part, part), part)
-            c[j, p, at, :] = (c[j, p, at, :].astype(F32) + held[p, at, :].astype(F32)).astype(BF16)
+            c[j, side, at, :] = (
+                c[j, side, at, :].astype(F32) + held[side, at, :].astype(F32)
+            ).astype(BF16)
+
+        def one(i, _):
+            if t != DOWN:
+                add(p, i)
+            else:
+                for side in range(2):
+                    add(side, p * (n // part // 2) + i)
             return 0
 
-        lax.fori_loop(0, n // part, add, 0)
+        lax.fori_loop(0, n // part // (2 if t == DOWN else 1), one, 0)
 
     def first_from(t):
         return 2 if t == DOWN else 1
@@ -453,7 +470,8 @@
         first = first_from(t)
 
         def one(hop, _):
-            for p in parts:
+            for k in parts:
+                p = k if t == DOWN else (1 - y if k == 0 else y)
 
                 @pl.when(jnp.logical_and(z == first - 1, hop >= first))
                 def _():
@@ -469,9 +487,9 @@
 
     near = 2 * z < line
 
-    def halves(step):
-        def one(p, _):
-            step(p)
+    def halves(t, step):
+        def one(k, _):
+            step(k if t == DOWN else jnp.where(k == 0, 1 - y, y))
             return 0
 
         lax.fori_loop(0, 2, one, 0)
@@ -485,7 +503,7 @@
                 rs_take(t, p, jr, jr)
                 rs_copy(t, p, jr, jr - 1, right).start()
 
-            halves(step)
+            halves(t, step)
 
     def rs_left(t, hop, only):
         jl, first = hop, first_from(t)
@@ -496,7 +514,7 @@
                 rs_take(t, p, jl, jl)
                 rs_copy(t, p, jl, jl + 1, left).start()
 
-            halves(step)
+            halves(t, step)
 
     def rs_cross(t, hop):
         rs_right(t, hop, near)
@@ -530,7 +548,7 @@
             def _():
                 rs_take(t, p, 0, line)
 
-            @pl.when(k == 0)
+            @pl.when(k == (1 if t == DOWN else 0))
             def _():
                 y_copy(Y_FIN, t).start()
 
@@ -857,17 +875,18 @@
 
         return fetch
 
-    def add_end_tokens(k):
+    def add_end_tokens(k, item, tiles):
         @pl.when(next_to_end)
         def _():
-            end_share(k).wait_recv()
+            if item != E_ACT_LAST:
+                end_share(k).wait_recv()
             held = lcopy(
                 cot_end.at[pl.ds(k * rows, rows), :],
                 wrow.at[k, pl.ds(0, rows), pl.ds(0, model)],
                 wsem.at[1, k],
             )
             held.start()
-            end_copy(E_ACT + k, partner).wait_recv()
+            end_copy(item, partner).wait_recv()
             held.wait()
 
             def add_tile(i, slot):
@@ -886,7 +905,7 @@
 
                 lax.fori_loop(0, line - 1, add_block, 0)
 
-            stream(0, hidden_half // TILE, (end_tile(k),), add_tile)
+            stream(*tiles, (end_tile(k),), add_tile)
 
     pair = 2 * blk
     same = lax.broadcasted_iota(jnp.int32, (pair, pair), 0) == lax.broadcasted_iota(
@@ -1091,7 +1110,6 @@
         xbuf[at, :] = xbuf[at, :] + out_bias[...] + tp_part[BRANCH, which, at_part, :].astype(F32)
         return 0
 
-    at_end = jnp.logical_or(z == 0, z == line - 1)
     stream(0, 4 * own_heads, (fetch_by(w_qkv, lambda i: kv_index(i)[3]),), keys_values)
     y_copy(Y_KV).start()
     ag_hop(0, 0, 1)
@@ -1118,7 +1136,7 @@
     stream(0, hidden_tiles // 2, (row_tile(w_down),), hidden_back)
     y_copy(Y_QG).wait_recv()
     own_places[3].start()
-    ag_hop(1, 1, 1, jnp.logical_not(at_end))
+    ag_hop(1, 1, 1)
     ag_hop(1, 0, 2)
     stream(hidden_tiles // 2, hidden_tiles, (row_tile(w_down),), hidden_back)
     y_copy(Y_HID).start()
@@ -1131,18 +1149,20 @@
     core_copy(0).wait_recv()
     y_copy(Y_ACT).wait_recv()
     end_send(E_ACT_FAR)
-    ag_hop(1, 1, 1, at_end)
+    end_send(E_ACT_LAST)
     in_order(share_down)
     pass_x(Y_MLP, 1)
     end_pass_x(1)
     ag_hop(0, 1, 3)
-    add_end_tokens(0)
+    end_tiles = hidden_half // TILE
+    add_end_tokens(0, E_ACT, (0, end_tiles))
     pass_on(Y_MLP, 1)
     end_pass(1)
     ag_hop(1, 0, 3)
-    add_end_tokens(1)
+    ag_hop(1, 1, 2)
+    add_end_tokens(1, E_ACT_FAR, (0, end_tiles // 2))
     rs_ends(DOWN, (1, 3), (0,))
-    ag_hop(1, 1, 2)
+    add_end_tokens(1, E_ACT_LAST, (end_tiles // 2, end_tiles))
     rs_ends(DOWN, (1, 3), (1,))
     tp_next(MLPB, 1)
     y_copy(Y_HID).wait_recv()
@@ -1169,6 +1189,7 @@
     pass_x(Y_ATTN, 2)
     for hop in range(1, min(line, 4)):
         rs_cross(DOWN, hop)
+        rs_home(DOWN, hop)
     y_copy(Y_ATT).wait_recv()
     w_out_fetch.start()
     w_out_fetch.wait()
@@ -1197,30 +1218,32 @@
     in_order(share_qkv)
     rs_ends(QKV, (1, line))
     rs_ends(OUT, (1, line))
-    for hop in range(1, min(line, 4)):
-        rs_home(DOWN, hop)
+    rs_cross(UP, 3) if line > 3 else None
     rs_home(UP, 1)
     rs_home(UP, 2)
+    rs_home(UP, 3) if line > 3 else None
     y_copy(Y_GQKV).wait_recv()
     stream(0, model_tiles, (row_tile(w_qkv),), attn_back)
     tp_copy(ATTNB, 0).start()
     tp_next(BRANCH, 2)
-    rs_cross(UP, 3) if line > 3 else None
     tp_next(ATTNB, 1)
 
     rs_rest(DOWN, 4 if line > 3 else 3)
     rs_finish(DOWN)
     tp_done(BRANCH)
     tp_done(MLPB)
-    rs_home(UP, 3) if line > 3 else None
     rs_cross(QKV, 1)
     rs_cross(QKV, 2)
+    rs_cross(QKV, 3) if line > 3 else None
     tp_next(ATTNB, 2)
     tp_done(ATTNB)
     lax.fori_loop(0, rows // chunk_rows, back_norms, 0)
     grad_store = lcopy(cbuf, grad_o, local.at[1])
     grad_store.start()
-    rs_cross(QKV, 3) if line > 3 else None
+    rs_home(QKV, 1)
+    rs_home(QKV, 2)
+    rs_home(QKV, 3) if line > 3 else None
+    rs_rest(QKV, 4 if line > 3 else 3)
     pair_copy = rcopy(small, small_pair, sm_s.at[0], sm_r.at[0], partner)
     pair_copy.start()
     pair_copy.wait()
@@ -1232,10 +1255,6 @@
     stream_store.start()
     rs_rest(UP, 4 if line > 3 else 3)
     rs_finish(UP)
-    rs_home(QKV, 1)
-    rs_home(QKV, 2)
-    rs_home(QKV, 3) if line > 3 else None
-    rs_rest(QKV, 4 if line > 3 else 3)
     rs_cross(OUT, 1)
     rs_cross(OUT, 2)
     rs_cross(OUT, 3) if line > 3 else None
@@ -1287,7 +1306,7 @@
     tp_steps = 0
     while (2 << tp_steps) < n_tp:
         tp_steps += 1
-    small_shape = (16, max(model, hidden, 6 * width))
+    small_shape = (8, max(model, hidden, 6 * width))
     shares = (
         (2, hidden_half, part_cols),
         (2, part_cols, hidden_half),
@@ -1364,8 +1383,8 @@
             dma((line,)),
             dma((line,)),
             dma((line,)),
-            dma((6,)),
-            dma((6,)),
+            dma((7,)),
+            dma((7,)),
             dma((2, n_tp // 2)),
             dma((2, n_tp // 2)),
             dma((9,)),
@@ -1444,7 +1463,7 @@
 
 
 def results(down, up, out, qkv, stream_out, grad_in, small, model, fused, hidden):
-    steps = 8
+    steps = 4
     f = lambda *s: jax.ShapeDtypeStruct(s, F32)
     rows_of = lambda a: pl.BlockSpec((a.shape[0] // steps,) + a.shape[1:], lambda i: (i, 0))
     whole = lambda a: pl.BlockSpec(a.shape, lambda i: (0,) * len(a.shape))

time: 265 us -> 252 us (0.951)
  Pallas kernels: 261 us -> 248 us
    pallas_call x1, Pallas kernels: 251 us -> 239 us  [layer(): pl.pallas_call(functools.partial(layer_kernel, line, n_tp), name='layer',...]
where the time goes in v5:
time: 252 us; the launch traced here: 249 us
  Pallas kernels  248 us (98%)
    pallas_call x1, Pallas kernels, layer(): pl.pallas_call(functools.partial(layer_kernel, line, n_tp), name='layer',...  239 us
    pallas_call x1, Pallas kernels, results(): pl.pallas_call(results_kernel, name='results', grid=(steps,), out_shape=[...  8.52 us

profile of v5, /device:TPU:0, one launch (start us, length us, event | category | flops | bytes accessed | tf_op | source)
XLA Modules:
  0.0 248.8 jit_solution(698078945022865071)
XLA Ops:
  0.6 239.5 %layer.1 = (bf16[2048,256]{1,0:T(8,128)(2,1)}, bf16[256,2048]{1,0:T(8,128)(2,1)}, bf16[512,256]{1,0:T(8,128)(2,1)}, bf16[256,1536]{1,0:T(8,128)(2,1)}, f32[384,2...) custom-call(s32[16]{0:T(128)} %order.1, ...), custom_call_target="tpu_custom_call" | custom-call | flops 64424509440 | bytes 33554432 | tf_op jit(solution)/shard_map/layer/pallas_call | solution.py:1413
  240.1 8.5 %results.1 = (f32[384,2048]{1,0:T(8,128)}, f32[384,2048]{1,0:T(8,128)}, f32[256,1536]{1,0:T(8,128)}, f32[1536]{0:T(1024)}, f32[512,256]{1,0:T(8,128)}, /*index=5...) custom-call(bf16[2048,256]{1,0:T(8,128)(2,1)} %get-tuple-element.18., ...), custom_call_target="tpu_custom_call" | custom-call | flops 524288 | bytes 16777216 | tf_op jit(solution)/shard_map/results/pallas_call | solution.py:1486

commit v6 on v5

--- a/solution.py
+++ b/solution.py
@@ -533,29 +533,27 @@
         if hop < line:
             lax.fori_loop(hop, line, one, 0)
 
-    def rs_finish(t):
+    def rs_finish_half(t, k):
         first = first_from(t)
         c, dst = fin_parts(t)
-
-        def take(k, _):
-            p = jnp.where(k == 0, 1 - y, y)
-
-            @pl.when(z >= first)
-            def _():
-                rs_take(t, p, 0, 0)
-
-            @pl.when(z <= line - 1 - first)
-            def _():
-                rs_take(t, p, 0, line)
-
-            @pl.when(k == (1 if t == DOWN else 0))
-            def _():
-                y_copy(Y_FIN, t).start()
-
-            return 0
-
-        lax.fori_loop(0, 2, take, 0)
-        lcopy(c.at[0, y], dst, local.at[4 + t]).start()
+        p = k if t == DOWN else (1 - y if k == 0 else y)
+
+        @pl.when(z >= first)
+        def _():
+            rs_take(t, p, 0, 0)
+
+        @pl.when(z <= line - 1 - first)
+        def _():
+            rs_take(t, p, 0, line)
+
+        if k == (1 if t == DOWN else 0):
+            y_copy(Y_FIN, t).start()
+        if k == 1:
+            lcopy(c.at[0, y], dst, local.at[4 + t]).start()
+
+    def rs_finish(t):
+        rs_finish_half(t, 0)
+        rs_finish_half(t, 1)
 
     def rs_drain(t):
         sends = jnp.logical_and(z >= first_from(t) - 1, z <= line - first_from(t))
@@ -1169,6 +1167,7 @@
     core_copy(1).wait_recv()
     in_order(share_up)
     rs_ends(UP, (1, 2))
+    ag_hop(1, 1, 3)
     ag_rest(0, 0, 4)
     ag_rest(0, 1, 4)
     for copy in own_places:
@@ -1185,18 +1184,17 @@
     small[S_QKV : S_QKV + 1, :] = jnp.zeros((1, small.shape[1]), F32)
     attend_back_queries()
     tp_next(MLPB, 2)
-    ag_hop(1, 1, 3)
     pass_x(Y_ATTN, 2)
     for hop in range(1, min(line, 4)):
         rs_cross(DOWN, hop)
         rs_home(DOWN, hop)
+    rs_cross(UP, 1)
+    rs_cross(UP, 2)
     y_copy(Y_ATT).wait_recv()
     w_out_fetch.start()
     w_out_fetch.wait()
     stream(0, model_tiles, (col_tile(w_down),), branch)
     tp_copy(BRANCH, 0).start()
-    rs_cross(UP, 1)
-    rs_cross(UP, 2)
     ag_rest(1, 0, 4)
     ag_rest(1, 1, 4)
     for j in range(1, line):
@@ -1204,6 +1202,7 @@
     own_stats = lcopy(stats, stats_all.at[0], local.at[0])
     own_stats.start()
     own_stats.wait()
+    rs_cross(UP, 3) if line > 3 else None
     attend_back_keys()
     store_order(gqkv)
     y_copy(Y_GQKV).start()
@@ -1218,7 +1217,6 @@
     in_order(share_qkv)
     rs_ends(QKV, (1, line))
     rs_ends(OUT, (1, line))
-    rs_cross(UP, 3) if line > 3 else None
     rs_home(UP, 1)
     rs_home(UP, 2)
     rs_home(UP, 3) if line > 3 else None
@@ -1228,22 +1226,24 @@
     tp_next(BRANCH, 2)
     tp_next(ATTNB, 1)
 
+    rs_cross(QKV, 1)
+    rs_cross(QKV, 2)
     rs_rest(DOWN, 4 if line > 3 else 3)
     rs_finish(DOWN)
     tp_done(BRANCH)
     tp_done(MLPB)
-    rs_cross(QKV, 1)
-    rs_cross(QKV, 2)
     rs_cross(QKV, 3) if line > 3 else None
+    rs_rest(UP, 4 if line > 3 else 3)
+    rs_finish(UP)
+    rs_home(QKV, 1)
+    rs_home(QKV, 2)
+    rs_home(QKV, 3) if line > 3 else None
+    rs_rest(QKV, 4 if line > 3 else 3)
     tp_next(ATTNB, 2)
     tp_done(ATTNB)
     lax.fori_loop(0, rows // chunk_rows, back_norms, 0)
     grad_store = lcopy(cbuf, grad_o, local.at[1])
     grad_store.start()
-    rs_home(QKV, 1)
-    rs_home(QKV, 2)
-    rs_home(QKV, 3) if line > 3 else None
-    rs_rest(QKV, 4 if line > 3 else 3)
     pair_copy = rcopy(small, small_pair, sm_s.at[0], sm_r.at[0], partner)
     pair_copy.start()
     pair_copy.wait()
@@ -1253,15 +1253,14 @@
     lax.fori_loop(0, rows // chunk_rows, stream_rows, 0)
     stream_store = lcopy(xbuf, stream_o, local.at[0])
     stream_store.start()
-    rs_rest(UP, 4 if line > 3 else 3)
-    rs_finish(UP)
     rs_cross(OUT, 1)
     rs_cross(OUT, 2)
     rs_cross(OUT, 3) if line > 3 else None
-    rs_finish(QKV)
+    rs_finish_half(QKV, 0)
     for hop in range(1, min(line, 4)):
         rs_home(OUT, hop)
     rs_rest(OUT, 4 if line > 3 else 3)
+    rs_finish_half(QKV, 1)
     rs_finish(OUT)
     for j in range(1, line):
         small_copy(line - j).wait_recv()
@@ -1463,7 +1462,7 @@
 
 
 def results(down, up, out, qkv, stream_out, grad_in, small, model, fused, hidden):
-    steps = 4
+    steps = 2
     f = lambda *s: jax.ShapeDtypeStruct(s, F32)
     rows_of = lambda a: pl.BlockSpec((a.shape[0] // steps,) + a.shape[1:], lambda i: (i, 0))
     whole = lambda a: pl.BlockSpec(a.shape, lambda i: (0,) * len(a.shape))

time: 252 us -> 246 us (0.976)
  Pallas kernels: 248 us -> 241 us
    pallas_call x1, Pallas kernels: 239 us -> 234 us  [layer(): pl.pallas_call(functools.partial(layer_kernel, line, n_tp), name='layer',...]
where the time goes in v6:
time: 246 us; the launch traced here: 242 us
  Pallas kernels  241 us (98%)
    pallas_call x1, Pallas kernels, layer(): pl.pallas_call(functools.partial(layer_kernel, line, n_tp), name='layer',...  234 us
    pallas_call x1, Pallas kernels, results(): pl.pallas_call(results_kernel, name='results', grid=(steps,), out_shape=[...  7.7 us

profile of v6, /device:TPU:0, one launch (start us, length us, event | category | flops | bytes accessed | tf_op | source)
XLA Modules:
  0.0 242.2 jit_solution(12299305429196565206)
XLA Ops:
  0.6 233.7 %layer.1 = (bf16[2048,256]{1,0:T(8,128)(2,1)}, bf16[256,2048]{1,0:T(8,128)(2,1)}, bf16[512,256]{1,0:T(8,128)(2,1)}, bf16[256,1536]{1,0:T(8,128)(2,1)}, f32[384,2...) custom-call(s32[16]{0:T(128)} %order.1, ...), custom_call_target="tpu_custom_call" | custom-call | flops 64424509440 | bytes 33554432 | tf_op jit(solution)/shard_map/layer/pallas_call | solution.py:1412
  234.4 7.7 %results.1 = (f32[384,2048]{1,0:T(8,128)}, f32[384,2048]{1,0:T(8,128)}, f32[256,1536]{1,0:T(8,128)}, f32[1536]{0:T(1024)}, f32[512,256]{1,0:T(8,128)}, /*index=5...) custom-call(bf16[2048,256]{1,0:T(8,128)(2,1)} %get-tuple-element.18., ...), custom_call_target="tpu_custom_call" | custom-call | flops 524288 | bytes 16777216 | tf_op jit(solution)/shard_map/results/pallas_call | solution.py:1485

commit v7 on v6

--- a/solution.py
+++ b/solution.py
@@ -1152,12 +1152,12 @@
     pass_x(Y_MLP, 1)
     end_pass_x(1)
     ag_hop(0, 1, 3)
+    ag_hop(1, 1, 2)
     end_tiles = hidden_half // TILE
     add_end_tokens(0, E_ACT, (0, end_tiles))
     pass_on(Y_MLP, 1)
     end_pass(1)
     ag_hop(1, 0, 3)
-    ag_hop(1, 1, 2)
     add_end_tokens(1, E_ACT_FAR, (0, end_tiles // 2))
     rs_ends(DOWN, (1, 3), (0,))
     add_end_tokens(1, E_ACT_LAST, (end_tiles // 2, end_tiles))

time: 246 us -> 246 us (level)
  no operation moved by 1% of the time
where the time goes in v7:
time: 246 us; the launch traced here: 242 us
  Pallas kernels  241 us (98%)
    pallas_call x1, Pallas kernels, layer(): pl.pallas_call(functools.partial(layer_kernel, line, n_tp), name='layer',...  234 us
    pallas_call x1, Pallas kernels, results(): pl.pallas_call(results_kernel, name='results', grid=(steps,), out_shape=[...  7.7 us

profile of v7, /device:TPU:0, one launch (start us, length us, event | category | flops | bytes accessed | tf_op | source)
XLA Modules:
  0.0 242.2 jit_solution(11302458686406454402)
XLA Ops:
  0.6 233.6 %layer.1 = (bf16[2048,256]{1,0:T(8,128)(2,1)}, bf16[256,2048]{1,0:T(8,128)(2,1)}, bf16[512,256]{1,0:T(8,128)(2,1)}, bf16[256,1536]{1,0:T(8,128)(2,1)}, f32[384,2...) custom-call(s32[16]{0:T(128)} %order.1, ...), custom_call_target="tpu_custom_call" | custom-call | flops 64424509440 | bytes 33554432 | tf_op jit(solution)/shard_map/layer/pallas_call | solution.py:1412
  234.3 7.7 %results.1 = (f32[384,2048]{1,0:T(8,128)}, f32[384,2048]{1,0:T(8,128)}, f32[256,1536]{1,0:T(8,128)}, f32[1536]{0:T(1024)}, f32[512,256]{1,0:T(8,128)}, /*index=5...) custom-call(bf16[2048,256]{1,0:T(8,128)(2,1)} %get-tuple-element.18., ...), custom_call_target="tpu_custom_call" | custom-call | flops 524288 | bytes 16777216 | tf_op jit(solution)/shard_map/results/pallas_call | solution.py:1485
